TPU v7x, 256 devices: a whole 4x4x8 slice. The times are simulated.
256 devices in a mesh: vpair: 16 (over x, y), rank: 16 (over z, core).
Axes of the slice: x: 4, y: 4, z: 8, core: 2. Of those that a mesh axis runs over, the one named last changes fastest.
Arguments:
- amplitudes: bfloat16 [8, 1200, 1200], P(None, 'vpair', 'rank'), may hold values from -6 to 6
- factors: bfloat16 [1200, 8192], P('vpair', 'rank'), may hold values from -0.1875 to 0.1875
- kernel: bfloat16 [8192, 8192], P('vpair', 'rank'), may hold values from -0.875 to 0.875
- other_terms: float32 [8, 1200, 1200], P(None, 'vpair'), may hold values from -6 to 6
- virt_energy: float32 [1200], replicated, may hold values from 0.2 to 4
- pair_energy: float32 [8], replicated, may hold values from -3 to -0.5
Outputs:
- residual: float32 [8, 1200, 1200], P(None, 'vpair')
- update_rms: float32 [], replicated
All inputs are finite; a program needn't handle non-finite values.
Results may differ from a plain program's by a relative error of at most 0.0035.
Values may be sent and summed in bfloat16 or wider, within the bound.
No kernel may reach another device: no remote copies, remote signals or barrier semaphores. Data moves between devices by JAX's collectives and lax.ppermute only.
A program may use at most 192 MiB of HBM per device.

v0:
```python
import jax
import jax.numpy as jnp
from jax import lax
from jax.sharding import Mesh
from jax.sharding import PartitionSpec as P

VPAIR = ("vpair_0", "vpair_1")


epsilon = 1e-06


def sent_to_all(shard, axis):
    copies = jnp.broadcast_to(shard, (lax.axis_size(axis), *shard.shape))
    return lax.all_to_all(copies, axis, split_axis=0, concat_axis=0, tiled=True)


def in_order(tiles, dim):
    lengths = list(tiles.shape[1:])
    lengths[dim] *= tiles.shape[0]
    return jnp.moveaxis(tiles, 0, dim).reshape(lengths)


def collect(shard, axis, dim):
    tiles = sent_to_all(shard, axis)
    return in_order(tiles, dim)


def filled_up(lines, count):
    spare = -len(lines) % count
    return jnp.pad(lines, [(0, spare)] + [(0, 0)] * (lines.ndim - 1))


def total_of(shard, axis):
    lines = shard.reshape(-1, *shard.shape[1:][-1:])
    padded = filled_up(lines, lax.axis_size(axis))
    own = lax.psum_scatter(padded, axis, scatter_dimension=0, tiled=True)
    whole = lax.all_gather(own, axis, axis=0, tiled=True)
    return whole[: len(lines)].reshape(shard.shape)


def one_axis_at_a_time(shard, axes):
    for axis in axes:
        shard = lax.psum(shard, axis)
    return shard


def shards(amplitudes, factors, kernel, other_terms, virt_energy, pair_energy):
    vpair_count = lax.axis_size(VPAIR)
    pair_count = amplitudes.shape[0]
    row_block = amplitudes.shape[1]
    virt_count = row_block * vpair_count
    right_block = kernel.shape[1]
    factor_rows = collect(factors, "rank", 1)
    factor_full = lax.all_gather(factor_rows, VPAIR, axis=0, tiled=True)
    factor_cols = lax.dynamic_slice_in_dim(
        factor_full, lax.axis_index("rank") * right_block, right_block, 1
    )
    half_done = jnp.einsum(
        "ons,sh->onh",
        collect(amplitudes, "rank", 2),
        factor_cols,
        preferred_element_type=jnp.float32,
    ).astype(jnp.bfloat16)
    kernel_sub = lax.all_to_all(kernel, VPAIR, split_axis=1, concat_axis=0, tiled=True).astype(
        jnp.float32
    )
    coupled = jnp.einsum(
        "cp,icq->ipq",
        factor_full,
        lax.all_to_all(half_done, VPAIR, split_axis=2, concat_axis=1, tiled=True),
        preferred_element_type=jnp.float32,
    )
    weighted = (kernel_sub[None] * coupled).astype(jnp.bfloat16)
    ladder_half = jnp.einsum(
        "ap,ipq->iaq", factor_full, weighted, preferred_element_type=jnp.float32
    ).astype(jnp.bfloat16)
    back_half = lax.all_to_all(ladder_half, VPAIR, split_axis=1, concat_axis=2, tiled=True)
    partial_value = jnp.einsum(
        "iaq,bq->iab", back_half, factor_cols, preferred_element_type=jnp.float32
    )
    row_energy = lax.dynamic_slice_in_dim(
        virt_energy, lax.axis_index(VPAIR) * row_block, row_block, 0
    )
    ladder = total_of(partial_value, "rank")
    residual = other_terms + ladder
    denominator = (
        row_energy[None, :, None] + virt_energy[None, None, :] - pair_energy[:, None, None]
    )
    update = residual / denominator
    squares = one_axis_at_a_time(jnp.sum(update * update), VPAIR)
    update_rms = jnp.sqrt(squares / (pair_count * virt_count * virt_count) + epsilon)
    return (residual, update_rms)


def solution(mesh):
    torus = Mesh(mesh.devices.reshape(4, 4, mesh.shape["rank"]), ("vpair_0", "vpair_1", "rank"))
    return jax.shard_map(
        shards,
        mesh=torus,
        in_specs=(
            P(None, VPAIR, "rank"),
            P(VPAIR, "rank"),
            P(VPAIR, "rank"),
            P(None, VPAIR, None),
            P(),
            P(),
        ),
        out_specs=(P(None, VPAIR, None), P()),
        check_vma=False,
    )
```

profile of v0, /device:TPU:1, one launch (start us, length us, event | category | flops | bytes accessed | tf_op | source)
XLA Modules:
  0.0 426.1 jit_solution(5133619606905226404)
XLA Ops:
  8.2 43.8 %all_to_all.56 = bf16[16,75,512]{2,1,0:T(8,128)(2,1)S(1)} all-to-all(bf16[16,75,512]{2,1,0:T(8,128)(2,1)S(1)} %broadcast_in_dim.4), channel_id=1, replica_groups=mesh['vpair_0'=4,'vpair_1'=4,'rank'=16] {'rank'}, dimensions={0} | all-to-all | bytes 2457600 | tf_op jit(solution)/shard_map/all_to_all | solution.py:15
  52.7 1.7 reshape.63
  54.4 1.8 broadcast_in_dim.5
  56.2 3.6 all-to-all-start.2
  60.8 54.8 %all-to-all-done.2 = bf16[16,8,75,75]{3,1,2,0:T(8,128)(2,1)S(1)} async-done(((bf16[16,8,75,75]{3,1,2,0:T(8,128)(2,1)}), bf16[16,8,75,75]{3,1,2,0:T(8,128)(2,1)S(1)}, u32[]{:S(2)}, u32[]{:S(2)}) %all-to-all-start.2) | async-done | bytes 1440032 | tf_op jit(solution)/shard_map/all_to_all | solution.py:15
  115.6 6.7 %all-to-all-start = ((bf16[512,16,32]{0,2,1:T(8,128)(2,1)}), bf16[512,16,32]{0,2,1:T(8,128)(2,1)S(1)}, u32[]{:S(2)}, u32[]{:S(2)}) async-start(bf16[512,16,32]{0,2,1:T(8,128)(2,1)} %bitcast), calls=%async_computation | async-start | bytes 1048576 | tf_op jit(solution)/shard_map/all_to_all | solution.py:65
  122.3 1.8 copy.40
  124.0 4.2 reshape.70
  128.3 66.2 %all-gather.5.cloned.1.call-done = bf16[16,75,8192]{2,1,0:T(8,128)(2,1)} async-done(((bf16[1,75,8192]{2,1,0:T(8,128)(2,1)}), bf16[16,75,8192]{2,1,0:T(8,128)(2,1)}) %all-gather.5.cloned.1.call-update) | async-done | bytes 19660816 | tf_op jit(solution)/shard_map/all_gather | solution.py:55
  194.5 22.4 %reshape.64 = bf16[1200,8192]{1,0:T(8,128)(2,1)} reshape(bf16[16,75,8192]{2,1,0:T(8,128)(2,1)} %all-gather.5.cloned.1.call-done) | data formatting | bytes 39321600
  216.9 2.3 fusion.4
  219.2 1.5 copy.33
  220.7 5.0 %all-to-all-start.3 = ((bf16[8,75,512]{1,0,2:T(8,128)(2,1)}), bf16[8,75,512]{1,0,2:T(8,128)(2,1)S(1)}, u32[]{:S(2)}, u32[]{:S(2)}) async-start(bf16[8,75,512]{1,0,2:T(8,128)(2,1)} %copy.33), calls=%async_computation.3 | async-start | bytes 2097152 | tf_op jit(solution)/shard_map/all_to_all | solution.py:71
  226.2 22.3 %reshape.69 = bf16[1200,8192,1]{1,0,2:T(8,128)(2,1)} reshape(bf16[16,75,8192]{2,1,0:T(8,128)(2,1)} %all-gather.5.cloned.1.call-done) | data formatting | bytes 39321600
  250.5 17.8 %fusion.3 = bf16[8,1200,32]{1,2,0:T(8,128)(2,1)} fusion(bf16[1200,8192,1]{1,0,2:T(8,128)(2,1)} %reshape.69, bf16[8,1200,32]{1,2,0:T(8,128)(2,1)S(1)} %all_to_all.47, f32[8192,32]{0,1:T(8,128)S(1)} %bitcast.57), kind=kOutput, calls=%fused_computation.6 | convolution fusion | flops 10070831104 | bytes 21938176 | tf_op jit(solution)/shard_map/ap,ipq->iaq/dot_general | solution.py:75
  268.3 3.9 copy.36
  272.2 2.4 reshape.73
  274.7 17.1 %all_to_all.57 = bf16[16,2,9600]{2,1,0:T(2,128)(2,1)} all-to-all(bf16[16,2,9600]{2,1,0:T(2,128)(2,1)S(1)} %reshape.73), channel_id=1, replica_groups=mesh['vpair_0'=4,'vpair_1'=4,'rank'=16] {'vpair_0','vpair_1'}, dimensions={0} | all-to-all | bytes 1228800 | tf_op jit(solution)/shard_map/all_to_all | solution.py:78
  291.8 3.6 reshape.74
  295.4 2.8 copy.37
  299.0 2.4 fusion.6
  301.6 33.1 %fusion = f32[40,1200]{1,0:T(8,128)S(1)} fusion(f32[608,1200]{1,0:T(8,128)S(1)} %pad.4), kind=kCustom, calls=%all-reduce-scatter | all-reduce-scatter fusion | flops 768001 | bytes 3111424
  334.7 3.4 collective-permute-start
  339.4 1.4 collective-permute-done
  342.7 40.5 %all-gather.7.cloned.1.call-done = f32[16,38,1200]{2,1,0:T(8,128)} async-done(((f32[1,38,1200]{2,1,0:T(8,128)}), f32[16,38,1200]{2,1,0:T(8,128)}) %all-gather.7.cloned.1.call-update) | async-done | bytes 2918416 | tf_op jit(solution)/shard_map/all_gather | solution.py:38
  383.2 2.1 reshape.66
  385.4 1.8 slice.4
  387.2 3.9 reshape.61
  391.2 4.8 %multiply_reduce_fusion = (f32[]{:T(128)}, f32[8,75,1200]{2,1,0:T(8,128)S(1)}) fusion(f32[8]{0:T(128)S(1)} %copy-done.3, f32[75,1200]{1,0:T(8,128)} %broadcast_add_fusion, f32[8,75,1200]{2,1,0:T(8,128)} %reshape.61, f32[8,75,1200]{2,0,1:T(8,128)} %param.9), kind=kLoop, calls=%fused_computation.4 | loop fusion | flops 3599999 | bytes 9000036 | tf_op jit(solution)/shard_map/reduce_sum | solution.py:91
  395.9 9.0 %psum.14 = f32[]{:T(128)} all-reduce(f32[]{:T(128)} %get-tuple-element.8), channel_id=1, replica_groups=mesh['vpair_0'=4,'vpair_1'=4,'rank'=16] {'vpair_0'}, use_global_device_ids=true, to_apply=%region_2.3 | all-reduce | flops 1 | bytes 8 | tf_op jit(solution)/shard_map/psum | solution.py:44
  404.9 3.4 copy.39
  408.3 9.1 %psum.15 = f32[]{:T(128)} all-reduce(f32[]{:T(128)} %psum.14), channel_id=1, replica_groups=mesh['vpair_0'=4,'vpair_1'=4,'rank'=16] {'vpair_1'}, use_global_device_ids=true, to_apply=%region_3.4 | all-reduce | flops 1 | bytes 8 | tf_op jit(solution)/shard_map/psum | solution.py:44
  (31 shorter events, 8.7 us)
Async XLA Ops:
  7.2 187.3 %all-gather.5.cloned.1.call-start = ((), (), s32[]{:S(2)}) async-start(), calls=%async_computation.5 | async-start | bytes 22282240 | tf_op jit(solution)/shard_map/all_gather | solution.py:55
  52.0 2.4 copy-start.1
  54.4 5.4 %copy-start = (bf16[512,512]{1,0:T(8,128)(2,1)S(1)}, bf16[512,512]{1,0:T(8,128)(2,1)}, u32[]{:S(2)}) copy-start(bf16[512,512]{1,0:T(8,128)(2,1)} %param.8) | copy-start | bytes 1572868
  56.2 59.4 %all-to-all-start.2 = ((bf16[16,8,75,75]{3,1,2,0:T(8,128)(2,1)}), bf16[16,8,75,75]{3,1,2,0:T(8,128)(2,1)S(1)}, u32[]{:S(2)}, u32[]{:S(2)}) async-start(bf16[16,8,75,75]{3,1,2,0:T(8,128)(2,1)} %broadcast_in_dim.5), calls=%async_computation.2 | async-start | bytes 4915200 | tf_op jit(solution)/shard_map/all_to_all | solution.py:15
  115.6 105.1 %all-to-all-start = ((bf16[512,16,32]{0,2,1:T(8,128)(2,1)}), bf16[512,16,32]{0,2,1:T(8,128)(2,1)S(1)}, u32[]{:S(2)}, u32[]{:S(2)}) async-start(bf16[512,16,32]{0,2,1:T(8,128)(2,1)} %bitcast), calls=%async_computation | async-start | bytes 1048576 | tf_op jit(solution)/shard_map/all_to_all | solution.py:65
  220.7 27.8 %all-to-all-start.3 = ((bf16[8,75,512]{1,0,2:T(8,128)(2,1)}), bf16[8,75,512]{1,0,2:T(8,128)(2,1)S(1)}, u32[]{:S(2)}, u32[]{:S(2)}) async-start(bf16[8,75,512]{1,0,2:T(8,128)(2,1)} %copy.33), calls=%async_computation.3 | async-start | bytes 2097152 | tf_op jit(solution)/shard_map/all_to_all | solution.py:71
  225.7 157.5 %all-gather.7.cloned.1.call-start = ((), (), s32[]{:S(2)}) async-start(), calls=%async_computation.6 | async-start | bytes 3481600 | tf_op jit(solution)/shard_map/all_gather | solution.py:38
  301.6 36.6 %copy-start.4 = (u32[256]{0:T(256)S(1)}, u32[256]{0:T(256)}, u32[]{:S(2)}) copy-start(u32[256]{0:T(256)} %constant.40) | copy-start | bytes 3076
  301.6 40.2 %copy-start.2 = (f32[1200]{0:T(1024)S(1)}, f32[1200]{0:T(1024)}, u32[]{:S(2)}) copy-start(f32[1200]{0:T(1024)} %param.10) | copy-start | bytes 14404
  334.7 6.1 %collective-permute-start = (f32[30,1200]{1,0:T(8,128)S(1)}, f32[30,1200]{1,0:T(8,128)S(1)}, u32[]{:S(2)}, u32[]{:S(2)}) collective-permute-start(f32[30,1200]{1,0:T(8,128)S(1)} %slice.5), channel_id=1, source_target_pairs={{0,1},{1,2},{2,3},{3,4},{4,5},{5,6},{6,7},{7,8},{8,9},{9,10},{10,1... | collective-permute-start | bytes 432008
  387.2 3.9 copy-start.3
Sparse Core Ops, SparseCore 0:
  54.5 139.8 all-gather.4
  341.9 41.3 all-gather.6
where the time goes:
time: 429 us; the launch traced here: 426 us
  waiting for transfers between devices  163 us (38%)
  blocking collectives  112 us (26%)
  local copies, waits for them, and re-layouts  87.1 us (20%)
  matrix products  22.5 us (5%)
  starting transfers between devices  18.9 us (4%)
  between operations  16.8 us (4%)
  other arithmetic  5.74 us (1%)
    all_gather x1, waiting for transfers between devices, shards(): factor_full = lax.all_gather(factor_rows, VPAIR, axis=0, tiled=True)  66.2 us
    unnamed x22, local copies, waits for them, and re-layouts  60.5 us
    all_to_all x1, waiting for transfers between devices, sent_to_all(): return lax.all_to_all(copies, axis, split_axis=0, concat_axis=0, tiled=True)  54.8 us
    all_to_all x1, blocking collectives, sent_to_all(): return lax.all_to_all(copies, axis, split_axis=0, concat_axis=0, tiled=True)  43.8 us
    all_gather x1, waiting for transfers between devices, total_of(): whole = lax.all_gather(own, axis, axis=0, tiled=True)  40.5 us
    unnamed x1, blocking collectives  33.1 us
    psum x2, blocking collectives, one_axis_at_a_time(): shard = lax.psum(shard, axis)  18.1 us
    dot_general x1, matrix products, shards(): jnp.einsum('ap,ipq->iaq', factor_full, weighted, preferred_element_type=j...  17.8 us
  transfers between devices with their start and end apart: 6, of which 4 were waited for; matrix products, arithmetic and copies ran while one was open for 14% of the time, Pallas kernels for 0%

commit v1 on v0

v1 whole, which is shorter than its diff:
```python
import jax
import jax.numpy as jnp
from jax import lax
from jax.experimental import pallas as pl
from jax.experimental.pallas import tpu as pltpu
from jax.sharding import Mesh
from jax.sharding import PartitionSpec as P

AXES = ("x", "y", "z", "c")
XY = ("x", "y")
RANK = ("z", "c")
BF = jnp.bfloat16
F32 = jnp.float32
epsilon = 1e-06

NX, NY, NZ, NC = 4, 4, 8, 2
NV = NX * NY
PAIRS = 8
ROW = 75
PAD = 80
BLK = 512
QC = 32
NVIR = 1200
LANE = 128


def core_swap(value):
    return lax.ppermute(value, "c", [(0, 1), (1, 0)])


def regroup(tiles, want):
    out = None
    lane = lax.broadcasted_iota(jnp.int32, (PAD, LANE), 1) // QC
    for group, tile in enumerate(tiles):
        shift = ((group - want) * QC) % LANE
        moved = pltpu.roll(tile, shift, 1) if shift else tile
        out = moved if out is None else jnp.where(lane == group, moved, out)
    return out


def half_kernel(core_ref, own_ref, oth_ref, xq_ref, out_ref, acc_ref):
    core = core_ref[0]
    dims = (((0,), (0,)), ((), ()))
    x_own = xq_ref[:, core].reshape(NZ * PAD, BLK)
    x_oth = xq_ref[:, 1 - core].reshape(NZ * PAD, BLK)
    acc_ref[...] = lax.dot_general(
        own_ref[...], x_own, dims, preferred_element_type=F32
    ) + lax.dot_general(oth_ref[...], x_oth, dims, preferred_element_type=F32)
    for xx in range(NX):
        for half in range(2):
            tiles = [
                acc_ref[pl.ds((half * 4 + g) * PAD, PAD), pl.ds(xx * LANE, LANE)]
                for g in range(4)
            ]
            for yy in range(NY):
                out_ref[xx * NY + yy, :, pl.ds(half * LANE, LANE)] = regroup(tiles, yy).astype(BF)


def make_half(core, t_own, t_oth, xq):
    return pl.pallas_call(
        half_kernel,
        out_shape=jax.ShapeDtypeStruct((NV, PAD, PAIRS * QC), BF),
        in_specs=[pl.BlockSpec(memory_space=pltpu.SMEM)]
        + [pl.BlockSpec(memory_space=pltpu.VMEM)] * 3,
        scratch_shapes=[pltpu.VMEM((PAIRS * PAD, BLK), F32)],
        name="half",
    )(core, t_own, t_oth, xq)


def main_kernel(core_ref, ho_ref, hx_ref, x_ref, zo_ref, zx_ref, bo_ref, bx_ref, h_ref, acc_ref):
    step = pl.program_id(0)
    half_m = PAIRS * QC

    @pl.when(step == 0)
    def _():
        h_ref[pl.ds(0, half_m), :] = ho_ref[...].astype(F32).T.astype(BF)
        h_ref[pl.ds(half_m, half_m), :] = hx_ref[...].astype(F32).T.astype(BF)
        acc_ref[...] = jnp.zeros_like(acc_ref)

    x = x_ref[...].reshape(NV * PAD, BLK)
    coupled = jnp.dot(h_ref[...], x, preferred_element_type=F32)
    z_own = zo_ref[...].reshape(1, QC, BLK).astype(F32)
    z_oth = zx_ref[...].reshape(1, QC, BLK).astype(F32)
    c_own = coupled[:half_m].reshape(PAIRS, QC, BLK) * z_own
    c_oth = coupled[half_m:].reshape(PAIRS, QC, BLK) * z_oth
    w = jnp.concatenate(
        [c_own.reshape(half_m, BLK), c_oth.reshape(half_m, BLK)], axis=0
    ).astype(BF)
    acc_ref[...] += lax.dot_general(x, w, (((1,), (1,)), ((), ())), preferred_element_type=F32)

    @pl.when(step == NZ - 1)
    def _():
        bo_ref[...] = acc_ref[:, :half_m]
        bx_ref[...] = acc_ref[:, half_m:].astype(BF)


def make_main(core, h_own, h_oth, x_all, z_own, z_oth):
    rows = NV * PAD
    half_m = PAIRS * QC
    return pl.pallas_call(
        main_kernel,
        out_shape=(
            jax.ShapeDtypeStruct((rows, half_m), F32),
            jax.ShapeDtypeStruct((rows, half_m), BF),
        ),
        grid_spec=pltpu.PrefetchScalarGridSpec(
            num_scalar_prefetch=1,
            grid=(NZ,),
            in_specs=[
                pl.BlockSpec((rows, half_m), lambda k, c: (0, 0)),
                pl.BlockSpec((rows, half_m), lambda k, c: (0, 0)),
                pl.BlockSpec((NV, 1, PAD, BLK), lambda k, c: (0, k, 0, 0)),
                pl.BlockSpec((1, 1, QC, BLK), lambda k, c: (k, c[0], 0, 0)),
                pl.BlockSpec((1, QC, BLK), lambda k, c: (k, 0, 0)),
            ],
            out_specs=(
                pl.BlockSpec((rows, half_m), lambda k, c: (0, 0)),
                pl.BlockSpec((rows, half_m), lambda k, c: (0, 0)),
            ),
            scratch_shapes=[
                pltpu.VMEM((2 * half_m, rows), BF),
                pltpu.VMEM((rows, 2 * half_m), F32),
            ],
        ),
        compiler_params=pltpu.CompilerParams(dimension_semantics=("arbitrary",)),
        cost_estimate=pl.CostEstimate(
            flops=4 * 512 * 1280 * 4096, bytes_accessed=14_000_000, transcendentals=0
        ),
        name="ladder_core",
    )(core, h_own, h_oth, x_all, z_own, z_oth)


def ladder_kernel(core_ref, b_ref, x_ref, own_ref, oth_ref, g_ref):
    core = core_ref[0]
    for xx in range(NX):
        for half in range(2):
            tiles = [
                b_ref[xx * NY + yy, :, pl.ds(half * LANE, LANE)].astype(F32) for yy in range(NY)
            ]
            for g in range(4):
                g_ref[half, pl.ds(g * PAD, PAD), pl.ds(xx * LANE, LANE)] = regroup(
                    tiles, g
                ).astype(BF)
    dims = (((1,), (1,)), ((), ()))
    own_ref[...] = lax.dot_general(g_ref[core], x_ref[...], dims, preferred_element_type=F32)
    oth_ref[...] = lax.dot_general(
        g_ref[1 - core], x_ref[...], dims, preferred_element_type=F32
    ).astype(BF)


def make_ladder(core, b_all, x_rows):
    return pl.pallas_call(
        ladder_kernel,
        out_shape=(
            jax.ShapeDtypeStruct((4 * PAD, NVIR), F32),
            jax.ShapeDtypeStruct((4 * PAD, NVIR), BF),
        ),
        in_specs=[pl.BlockSpec(memory_space=pltpu.SMEM)]
        + [pl.BlockSpec(memory_space=pltpu.VMEM)] * 2,
        scratch_shapes=[pltpu.VMEM((2, 4 * PAD, BLK), BF)],
        name="ladder_rank",
    )(core, b_all, x_rows)


def final_kernel(core_ref, pair_ref, own_ref, oth_ref, other_ref, row_ref, col_ref, out_ref, sq_ref):
    i = pl.program_id(0)
    mine = (i // 4) == core_ref[0]
    own = own_ref[0, :ROW, :].astype(F32)
    oth = oth_ref[0, :ROW, :].astype(F32)
    res = other_ref[0] + jnp.where(mine, own, oth)
    out_ref[0] = res
    upd = res / (row_ref[...] + col_ref[...] - pair_ref[i])
    part = jnp.sum(upd * upd, axis=0, keepdims=True)

    @pl.when(i == 0)
    def _():
        sq_ref[...] = jnp.zeros_like(sq_ref)

    sq_ref[...] += part


def make_final(core, pair_energy, l_own, l_oth, other_terms, row_energy, col_energy):
    def own_index(i, c, p):
        return (jnp.clip(i - 4 * c[0], 0, 3), 0, 0)

    def oth_index(i, c, p):
        return (jnp.clip(i - 4 * (1 - c[0]), 0, 3), 0, 0)

    return pl.pallas_call(
        final_kernel,
        out_shape=(
            jax.ShapeDtypeStruct((PAIRS, ROW, NVIR), F32),
            jax.ShapeDtypeStruct((1, NVIR), F32),
        ),
        grid_spec=pltpu.PrefetchScalarGridSpec(
            num_scalar_prefetch=2,
            grid=(PAIRS,),
            in_specs=[
                pl.BlockSpec((1, PAD, NVIR), own_index),
                pl.BlockSpec((1, PAD, NVIR), oth_index),
                pl.BlockSpec((1, ROW, NVIR), lambda i, c, p: (i, 0, 0)),
                pl.BlockSpec((ROW, 1), lambda i, c, p: (0, 0)),
                pl.BlockSpec((1, NVIR), lambda i, c, p: (0, 0)),
            ],
            out_specs=(
                pl.BlockSpec((1, ROW, NVIR), lambda i, c, p: (i, 0, 0)),
                pl.BlockSpec((1, NVIR), lambda i, c, p: (0, 0)),
            ),
        ),
        compiler_params=pltpu.CompilerParams(dimension_semantics=("arbitrary",)),
        name="residual",
    )(core, pair_energy, l_own, l_oth, other_terms, row_energy, col_energy)


def shards(amplitudes, factors, kernel, other_terms, virt_energy, pair_energy):
    core_id = lax.axis_index("c")
    core = core_id.astype(jnp.int32).reshape((1,))

    x_pad = jnp.pad(factors, ((0, PAD - ROW), (0, 0)))
    x_ranks = lax.all_gather(x_pad, "z", axis=0)
    x_all = lax.all_gather(x_ranks, XY, axis=0)

    t_cols = jnp.pad(amplitudes, ((0, 0), (0, PAD - ROW), (0, PAD - ROW)))
    t_cols = jnp.transpose(t_cols, (2, 0, 1)).reshape(PAD, PAIRS * PAD)
    t_cols, _ = lax.optimization_barrier((t_cols, x_ranks))
    t_own = lax.all_gather(t_cols, "z", axis=0, tiled=True)
    t_oth = core_swap(t_own)

    x_many = jnp.broadcast_to(x_pad[None], (NV, PAD, BLK))
    x_many, _ = lax.optimization_barrier((x_many, t_own))
    xq = lax.all_to_all(x_many, XY, split_axis=0, concat_axis=0, tiled=True)
    x_rows = xq[:, :ROW].reshape(NVIR, BLK)

    h_msg = make_half(core, t_own, t_oth, xq.reshape(NZ, NC, PAD, BLK))
    h_own = lax.all_to_all(h_msg, XY, split_axis=0, concat_axis=0, tiled=True)
    h_own = h_own.reshape(NV * PAD, PAIRS * QC)
    h_oth = core_swap(h_own)

    z_cols = kernel.T.reshape(NV, QC, BLK)
    z_all = lax.all_to_all(z_cols, XY, split_axis=0, concat_axis=0, tiled=True)
    z_all = z_all.reshape(NZ, NC, QC, BLK)
    z_oth = core_swap(lax.dynamic_index_in_dim(z_all, 1 - core_id, 1, keepdims=False))

    b_own, b_send = make_main(
        core, h_own, h_oth, x_all.reshape(NV, NZ, PAD, BLK), z_all, z_oth
    )
    b_sum = (b_own + core_swap(b_send).astype(F32)).astype(BF)
    b_all = lax.all_to_all(
        b_sum.reshape(NV, PAD, PAIRS * QC), XY, split_axis=0, concat_axis=0, tiled=True
    )

    l_own, l_send = make_ladder(core, b_all, x_rows)
    l_sum = (l_own + core_swap(l_send).astype(F32)).astype(BF)
    l_parts = lax.all_to_all(
        l_sum.reshape(NZ, PAD // 2, NVIR), "z", split_axis=0, concat_axis=0, tiled=True
    )
    l_chunk = jnp.sum(l_parts.astype(F32), axis=0).astype(BF)
    l_mine = lax.all_gather(l_chunk, "z", axis=0, tiled=True)
    l_rest = core_swap(l_mine)

    row_energy = lax.dynamic_slice_in_dim(virt_energy, lax.axis_index(XY) * ROW, ROW, 0)
    residual, squares = make_final(
        core,
        pair_energy,
        l_mine.reshape(4, PAD, NVIR),
        l_rest.reshape(4, PAD, NVIR),
        other_terms,
        row_energy[:, None],
        virt_energy[None, :],
    )
    total = jnp.broadcast_to(jnp.sum(squares), (NV, 8, LANE))
    totals = lax.all_to_all(total, XY, split_axis=0, concat_axis=0, tiled=True)
    count = PAIRS * NVIR * NVIR
    update_rms = jnp.sqrt(jnp.sum(totals[:, 0, 0]) / count + epsilon)
    return residual, update_rms


def solution(mesh):
    torus = Mesh(mesh.devices.reshape(NX, NY, NZ, NC), AXES)
    return jax.shard_map(
        shards,
        mesh=torus,
        in_specs=(
            P(None, XY, RANK),
            P(XY, RANK),
            P(XY, RANK),
            P(None, XY, None),
            P(),
            P(),
        ),
        out_specs=(P(None, XY, None), P()),
        check_vma=False,
    )
```

time: 429 us -> 289 us (0.67)
  waiting for transfers between devices: 163 us -> 42.5 us
  local copies, waits for them, and re-layouts: 87.1 us -> 20.6 us
  starting transfers between devices: 18.9 us -> 71.2 us
  Pallas kernels: 0 us -> 33.7 us
  matrix products: 22.5 us -> 0 us
  blocking collectives: 112 us -> 97.6 us
    all_gather x2 -> x1, waiting for transfers between devices: 107 us -> 8.17 us  [shards(): x_all = lax.all_gather(x_ranks, XY, axis=0)]
    all_gather x0 -> x3, blocking collectives: none -> 67.7 us  [the longest x1 26.6 us: shards(): x_ranks = lax.all_gather(x_pad, 'z', axis=0)]
    unnamed x22 -> x31, local copies, waits for them, and re-layouts: 60.5 us -> 14.1 us
    ppermute x0 -> x6, starting transfers between devices: none -> 43.2 us  [core_swap(): return lax.ppermute(value, 'c', [(0, 1), (1, 0)])]
    pallas_call x0 -> x4, Pallas kernels: none -> 33.7 us  [the longest x1 17.2 us: make_main(): pl.pallas_call(main_kernel, out_shape=(jax.ShapeDtypeStruct((rows, half_m...]
    unnamed x1 -> x0, blocking collectives: 33.1 us -> none
    all_to_all x2 -> x1, blocking collectives: 60.9 us -> 29.9 us  [shards(): lax.all_to_all(l_sum.reshape(NZ, PAD // 2, NVIR), 'z', split_axis=0, conc...]
    all_to_all x3 -> x5, waiting for transfers between devices: 54.8 us -> 27.1 us  [the longest x1 13.2 us: shards(): h_own = lax.all_to_all(h_msg, XY, split_axis=0, concat_axis=0, tiled=True)]
  transfers between devices with their start and end apart: 6 -> 12, of which waited for: 4 -> 9; matrix products, arithmetic and copies ran while one was open for 14% -> 5% of each run, Pallas kernels for 0% -> 2%
where the time goes in v1:
time: 289 us; the launch traced here: 288 us
  blocking collectives  97.6 us (34%)
  starting transfers between devices  71.2 us (25%)
  waiting for transfers between devices  42.5 us (15%)
  Pallas kernels  33.7 us (12%)
  local copies, waits for them, and re-layouts  20.6 us (7%)
  between operations  16 us (6%)
  other arithmetic  6.08 us (2%)
    ppermute x6, starting transfers between devices, core_swap(): return lax.ppermute(value, 'c', [(0, 1), (1, 0)])  43.2 us
    all_to_all x1, blocking collectives, shards(): lax.all_to_all(l_sum.reshape(NZ, PAD // 2, NVIR), 'z', split_axis=0, conc...  29.9 us
    all_gather x1, blocking collectives, shards(): x_ranks = lax.all_gather(x_pad, 'z', axis=0)  26.6 us
    all_gather x1, blocking collectives, shards(): t_own = lax.all_gather(t_cols, 'z', axis=0, tiled=True)  20.7 us
    all_gather x1, blocking collectives, shards(): l_mine = lax.all_gather(l_chunk, 'z', axis=0, tiled=True)  20.5 us
    pallas_call x1, Pallas kernels, make_main(): pl.pallas_call(main_kernel, out_shape=(jax.ShapeDtypeStruct((rows, half_m...  17.2 us
    unnamed x31, local copies, waits for them, and re-layouts  14.1 us
    all_to_all x1, waiting for transfers between devices, shards(): h_own = lax.all_to_all(h_msg, XY, split_axis=0, concat_axis=0, tiled=True)  13.2 us
  transfers between devices with their start and end apart: 12, of which 9 were waited for; matrix products, arithmetic and copies ran while one was open for 5% of the time, Pallas kernels for 2%

profile of v1, /device:TPU:1, one launch (start us, length us, event | category | flops | bytes accessed | tf_op | source)
XLA Modules:
  0.0 287.7 jit_solution(11357448714294148581)
XLA Ops:
  8.1 26.6 %all-gather = bf16[640,512]{1,0:T(8,128)(2,1)} all-gather(bf16[80,512]{1,0:T(8,128)(2,1)S(1)} %pad.9), channel_id=2, replica_groups=mesh['x'=4,'y'=4,'z'=8,'c'=2] {'z'}, dimensions={0}, use_global_device_ids=true | all-gather | bytes 737280 | tf_op jit(solution)/shard_map/all_gather | solution.py:220
  35.2 20.7 %all_gather.20.own_ref = bf16[640,640]{1,0:T(8,128)(2,1)S(1)} all-gather(bf16[80,640]{1,0:T(8,128)(2,1)S(1)} %reshape.39), channel_id=1, replica_groups=mesh['x'=4,'y'=4,'z'=8,'c'=2] {'z'}, dimensions={0}, use_global_device_ids=true | all-gather | bytes 921600 | tf_op jit(solution)/shard_map/all_gather | solution.py:226
  55.8 1.3 broadcast_in_dim.15
  57.1 7.0 %all-to-all-start = ((bf16[16,80,512]{2,1,0:T(8,128)(2,1)}), bf16[16,80,512]{2,1,0:T(8,128)(2,1)S(1)}, u32[]{:S(2)}, u32[]{:S(2)}) async-start(bf16[16,80,512]{2,1,0:T(8,128)(2,1)} %broadcast_in_dim.15), calls=%async_computation | async-start | bytes 2621440 | tf_op jit(solution)/shard_map/all_to_all | solution.py:231
  64.1 12.1 %collective-permute-start = (bf16[640,640]{1,0:T(8,128)(2,1)S(1)}, bf16[640,640]{1,0:T(8,128)(2,1)S(1)}, u32[]{:S(2)}, u32[]{:S(2)}) collective-permute-start(bf16[640,640]{1,0:T(8,128)(2,1)S(1)} %all_gather.20.own_ref), channel_id=1, source_target_pairs={{0,1},{1,0},{2,3},{3,2},{4,5},{5,4},{6,7},{7,6},{8,9},{9,8},{10,11... | collective-permute-start | bytes 2457608 | tf_op jit(solution)/shard_map/ppermute | solution.py:28
  76.2 2.0 collective-permute-done.oth_ref
  79.5 4.4 %half.1 = bf16[16,80,256]{2,1,0:T(8,128)(2,1)} custom-call(s32[1]{0:T(128)} %bitcast.core_ref, bf16[640,640]{1,0:T(8,128)(2,1)} %copy-done.3, bf16[640,640]{1,0:T(8,128)(2,1)} %copy-done.7, bf16[8,2,80,512]{3,2,1,0:T(8,128)(2,1)} %bitcast.20), custom_call_target="tpu_custom_call" | custom-call | tf_op jit(solution)/shard_map/half/pallas_call | solution.py:60
  83.9 6.9 %all-to-all-start.1 = ((bf16[16,80,256]{2,1,0:T(8,128)(2,1)}), bf16[16,80,256]{2,1,0:T(8,128)(2,1)S(1)}, u32[]{:S(2)}, u32[]{:S(2)}) async-start(bf16[16,80,256]{2,1,0:T(8,128)(2,1)} %half.1), calls=%async_computation.1 | async-start | bytes 1310720 | tf_op jit(solution)/shard_map/all_to_all | solution.py:235
  91.8 13.2 %all-to-all-done.1 = bf16[16,80,256]{2,1,0:T(8,128)(2,1)S(1)} async-done(((bf16[16,80,256]{2,1,0:T(8,128)(2,1)}), bf16[16,80,256]{2,1,0:T(8,128)(2,1)S(1)}, u32[]{:S(2)}, u32[]{:S(2)}) %all-to-all-start.1) | async-done | bytes 655392 | tf_op jit(solution)/shard_map/all_to_all | solution.py:235
  105.1 6.4 %all-to-all-start.2 = ((bf16[16,32,512]{2,1,0:T(8,128)(2,1)}), bf16[16,32,512]{2,1,0:T(8,128)(2,1)S(1)}, u32[]{:S(2)}, u32[]{:S(2)}) async-start(bf16[16,32,512]{2,1,0:T(8,128)(2,1)} %bitcast.7), calls=%async_computation.2 | async-start | bytes 1048576 | tf_op jit(solution)/shard_map/all_to_all | solution.py:240
  111.5 10.0 %collective-permute-start.1 = (bf16[1280,256]{1,0:T(8,128)(2,1)S(1)}, bf16[1280,256]{1,0:T(8,128)(2,1)S(1)}, u32[]{:S(2)}, u32[]{:S(2)}) collective-permute-start(bf16[1280,256]{1,0:T(8,128)(2,1)S(1)} %bitcast.28), channel_id=1, source_target_pairs={{0,1},{1,0},{2,3},{3,2},{4,5},{5,4},{6,7},{7,6},{8,9},{9,8},{10,11... | collective-permute-start | bytes 1966088 | tf_op jit(solution)/shard_map/ppermute | solution.py:28
  121.5 2.6 all-to-all-done.2
  124.1 11.1 %collective-permute-start.2 = (bf16[8,32,512]{2,1,0:T(8,128)(2,1)S(1)}, bf16[8,32,512]{2,1,0:T(8,128)(2,1)S(1)}, u32[]{:S(2)}, u32[]{:S(2)}) collective-permute-start(bf16[8,32,512]{2,1,0:T(8,128)(2,1)S(1)} %dynamic-slice_bitcast_fusion), channel_id=1, source_target_pairs={{0,1},{1,0},{2,3},{3,2},{4,5},{5,4},{6,7},{7,6},{8,9},{9,8},{10,11... | collective-permute-start | bytes 786440 | tf_op jit(solution)/shard_map/ppermute | solution.py:28
  136.4 8.2 %all-gather.4.cloned.1.call-done = bf16[128,80,512]{2,1,0:T(8,128)(2,1)} async-done(((bf16[8,80,512]{2,1,0:T(8,128)(2,1)}), bf16[128,80,512]{2,1,0:T(8,128)(2,1)}) %all-gather.4.cloned.1.call-update) | async-done | bytes 10485776 | tf_op jit(solution)/shard_map/all_gather | solution.py:221
  144.6 17.2 %ladder_core.1 = (f32[1280,256]{1,0:T(8,128)}, bf16[1280,256]{1,0:T(8,128)(2,1)}) custom-call(s32[1]{0:T(128)} %bitcast.core_ref, bf16[1280,256]{1,0:T(8,128)(2,1)} %bitcast.29, bf16[1280,256]{1,0:T(8,128)(2,1)} %copy-done.12, bf16[16,8,80,512]{3,2,1,0:T(8,128)(2,1)} %bitcast.30, bf16[8,2,32,512]{3,2,1,0:T(8,128)(2,1)} %bitcast.26, ...), custom_call_target="tpu_custom_call" | custom-call | flops 10737418240 | bytes 14000000 | tf_op jit(solution)/shard_map/ladder_core/pallas_call | solution.py:100
  162.4 1.9 collective-permute-done.3
  164.3 2.4 add_convert_fusion.1
  166.7 4.2 %all-to-all-start.3 = ((bf16[16,80,256]{2,1,0:T(8,128)(2,1)}), bf16[16,80,256]{2,1,0:T(8,128)(2,1)S(1)}, u32[]{:S(2)}, u32[]{:S(2)}) async-start(bf16[16,80,256]{2,1,0:T(8,128)(2,1)} %bitcast.10), calls=%async_computation.3 | async-start | bytes 1310720 | tf_op jit(solution)/shard_map/all_to_all | solution.py:248
  170.9 1.3 reshape.45.x_ref
  172.2 10.2 %all-to-all-done.3.b_ref = bf16[16,80,256]{2,1,0:T(8,128)(2,1)S(1)} async-done(((bf16[16,80,256]{2,1,0:T(8,128)(2,1)}), bf16[16,80,256]{2,1,0:T(8,128)(2,1)S(1)}, u32[]{:S(2)}, u32[]{:S(2)}) %all-to-all-start.3) | async-done | bytes 655392 | tf_op jit(solution)/shard_map/all_to_all | solution.py:248
  183.2 4.2 %ladder_rank.1 = (f32[320,1200]{1,0:T(8,128)}, bf16[320,1200]{1,0:T(8,128)(2,1)}) custom-call(s32[1]{0:T(128)} %bitcast.core_ref, bf16[16,80,256]{2,1,0:T(8,128)(2,1)} %copy-done.4, bf16[1200,512]{1,0:T(8,128)(2,1)} %reshape.45.x_ref), custom_call_target="tpu_custom_call" | custom-call | tf_op jit(solution)/shard_map/ladder_rank/pallas_call | solution.py:152
  187.4 2.4 collective-permute-start.4
  189.8 2.2 collective-permute-done.4
  192.0 1.6 add_convert_fusion
  193.6 29.9 %all_to_all.30 = bf16[8,40,1200]{2,1,0:T(8,128)(2,1)S(1)} all-to-all(bf16[8,40,1200]{2,1,0:T(8,128)(2,1)S(1)} %bitcast.22), channel_id=1, replica_groups=mesh['x'=4,'y'=4,'z'=8,'c'=2] {'z'}, dimensions={0} | all-to-all | bytes 1536000 | tf_op jit(solution)/shard_map/all_to_all | solution.py:254
  223.6 20.5 %all_gather.23 = bf16[320,1200]{1,0:T(8,128)(2,1)S(1)} all-gather(bf16[40,1200]{1,0:T(8,128)(2,1)S(1)} %reduce_sum.30), channel_id=1, replica_groups=mesh['x'=4,'y'=4,'z'=8,'c'=2] {'z'}, dimensions={0}, use_global_device_ids=true | all-gather | bytes 864000 | tf_op jit(solution)/shard_map/all_gather | solution.py:258
  244.1 7.0 %collective-permute-start.5 = (bf16[320,1200]{1,0:T(8,128)(2,1)S(1)}, bf16[320,1200]{1,0:T(8,128)(2,1)S(1)}, u32[]{:S(2)}, u32[]{:S(2)}) collective-permute-start(bf16[320,1200]{1,0:T(8,128)(2,1)S(1)} %all_gather.23), channel_id=1, source_target_pairs={{0,1},{1,0},{2,3},{3,2},{4,5},{5,4},{6,7},{7,6},{8,9},{9,8},{10,11... | collective-permute-start | bytes 2304008 | tf_op jit(solution)/shard_map/ppermute | solution.py:28
  252.4 4.6 %copy.30.other_ref = f32[8,75,1200]{2,1,0:T(8,128)} copy(f32[8,75,1200]{2,0,1:T(8,128)} %param.9) | data formatting | bytes 5760000 | tf_op args[3]
  257.9 7.9 %residual.1 = (f32[8,75,1200]{2,1,0:T(8,128)}, f32[1,1200]{1,0:T(1,128)}) custom-call(s32[1]{0:T(128)} %bitcast.core_ref, f32[8]{0:T(128)} %pair_ref.1, bf16[4,80,1200]{2,1,0:T(8,128)(2,1)} %bitcast.23, bf16[4,80,1200]{2,1,0:T(8,128)(2,1)} %bitcast.27, f32[8,75,1200]{2,1,0:T(8,128)} %copy.30.other_ref, f32[75,1]{1,0:T(8,128)} %copy.31.row_ref, ...), custom_call_target="tpu_custom_call" | custom-call | tf_op jit(solution)/shard_map/residual/pallas_call | solution.py:189
  265.9 1.3 reduce_sum.31
  268.4 3.5 %all-to-all-start.5 = ((f32[16,8,128]{2,1,0:T(8,128)}), f32[16,8,128]{2,1,0:T(8,128)S(1)}, u32[]{:S(2)}, u32[]{:S(2)}) async-start(f32[16,8,128]{2,1,0:T(8,128)} %broadcast_in_dim.18), calls=%async_computation.5 | async-start | bytes 131072 | tf_op jit(solution)/shard_map/all_to_all | solution.py:272
  271.9 5.3 %copy.33 = f32[8,75,1200]{2,0,1:T(8,128)} copy(f32[8,75,1200]{2,1,0:T(8,128)} %get-tuple-element.26) | data formatting | bytes 5760000
  (48 shorter events, 11.7 us)
Async XLA Ops:
  7.2 27.6 %copy-start.10 = (bf16[8,75,75]{2,0,1:T(8,128)(2,1)S(1)}, bf16[8,75,75]{2,0,1:T(8,128)(2,1)}, u32[]{:S(2)}) copy-start(bf16[8,75,75]{2,0,1:T(8,128)(2,1)} %param.6) | copy-start | bytes 270004
  7.2 137.4 %all-gather.4.cloned.1.call-start = ((), (), s32[]{:S(2)}) async-start(), calls=%async_computation.6 | async-start | bytes 11141120 | tf_op jit(solution)/shard_map/all_gather | solution.py:221
  55.8 8.3 %copy-start.3 = (bf16[640,640]{1,0:T(8,128)(2,1)}, bf16[640,640]{1,0:T(8,128)(2,1)S(1)}, u32[]{:S(2)}) copy-start(bf16[640,640]{1,0:T(8,128)(2,1)S(1)} %all_gather.20.own_ref) | copy-start | bytes 2457604
  57.1 21.1 %all-to-all-start = ((bf16[16,80,512]{2,1,0:T(8,128)(2,1)}), bf16[16,80,512]{2,1,0:T(8,128)(2,1)S(1)}, u32[]{:S(2)}, u32[]{:S(2)}) async-start(bf16[16,80,512]{2,1,0:T(8,128)(2,1)} %broadcast_in_dim.15), calls=%async_computation | async-start | bytes 2621440 | tf_op jit(solution)/shard_map/all_to_all | solution.py:231
  64.1 14.1 %collective-permute-start = (bf16[640,640]{1,0:T(8,128)(2,1)S(1)}, bf16[640,640]{1,0:T(8,128)(2,1)S(1)}, u32[]{:S(2)}, u32[]{:S(2)}) collective-permute-start(bf16[640,640]{1,0:T(8,128)(2,1)S(1)} %all_gather.20.own_ref), channel_id=1, source_target_pairs={{0,1},{1,0},{2,3},{3,2},{4,5},{5,4},{6,7},{7,6},{8,9},{9,8},{10,11... | collective-permute-start | bytes 2457608 | tf_op jit(solution)/shard_map/ppermute | solution.py:28
  78.1 1.0 copy-start.7
  78.2 1.3 copy-start
  79.5 11.3 %copy-start.9 = (bf16[512,512]{1,0:T(8,128)(2,1)S(1)}, bf16[512,512]{1,0:T(8,128)(2,1)}, u32[]{:S(2)}) copy-start(bf16[512,512]{1,0:T(8,128)(2,1)} %param.8) | copy-start | bytes 1572868
  83.9 21.2 %all-to-all-start.1 = ((bf16[16,80,256]{2,1,0:T(8,128)(2,1)}), bf16[16,80,256]{2,1,0:T(8,128)(2,1)S(1)}, u32[]{:S(2)}, u32[]{:S(2)}) async-start(bf16[16,80,256]{2,1,0:T(8,128)(2,1)} %half.1), calls=%async_computation.1 | async-start | bytes 1310720 | tf_op jit(solution)/shard_map/all_to_all | solution.py:235
  105.1 39.5 %copy-start.8 = (bf16[16,80,256]{2,1,0:T(8,128)(2,1)}, bf16[16,80,256]{2,1,0:T(8,128)(2,1)S(1)}, u32[]{:S(2)}) copy-start(bf16[16,80,256]{2,1,0:T(8,128)(2,1)S(1)} %all-to-all-done.1) | copy-start | bytes 1966084
  105.1 19.0 %all-to-all-start.2 = ((bf16[16,32,512]{2,1,0:T(8,128)(2,1)}), bf16[16,32,512]{2,1,0:T(8,128)(2,1)S(1)}, u32[]{:S(2)}, u32[]{:S(2)}) async-start(bf16[16,32,512]{2,1,0:T(8,128)(2,1)} %bitcast.7), calls=%async_computation.2 | async-start | bytes 1048576 | tf_op jit(solution)/shard_map/all_to_all | solution.py:240
  111.5 24.9 %collective-permute-start.1 = (bf16[1280,256]{1,0:T(8,128)(2,1)S(1)}, bf16[1280,256]{1,0:T(8,128)(2,1)S(1)}, u32[]{:S(2)}, u32[]{:S(2)}) collective-permute-start(bf16[1280,256]{1,0:T(8,128)(2,1)S(1)} %bitcast.28), channel_id=1, source_target_pairs={{0,1},{1,0},{2,3},{3,2},{4,5},{5,4},{6,7},{7,6},{8,9},{9,8},{10,11... | collective-permute-start | bytes 1966088 | tf_op jit(solution)/shard_map/ppermute | solution.py:28
  124.1 20.5 %copy-start.5 = (bf16[16,32,512]{2,1,0:T(8,128)(2,1)}, bf16[16,32,512]{2,1,0:T(8,128)(2,1)S(1)}, u32[]{:S(2)}) copy-start(bf16[16,32,512]{2,1,0:T(8,128)(2,1)S(1)} %all-to-all-done.2) | copy-start | bytes 1572868
  124.1 12.3 %collective-permute-start.2 = (bf16[8,32,512]{2,1,0:T(8,128)(2,1)S(1)}, bf16[8,32,512]{2,1,0:T(8,128)(2,1)S(1)}, u32[]{:S(2)}, u32[]{:S(2)}) collective-permute-start(bf16[8,32,512]{2,1,0:T(8,128)(2,1)S(1)} %dynamic-slice_bitcast_fusion), channel_id=1, source_target_pairs={{0,1},{1,0},{2,3},{3,2},{4,5},{5,4},{6,7},{7,6},{8,9},{9,8},{10,11... | collective-permute-start | bytes 786440 | tf_op jit(solution)/shard_map/ppermute | solution.py:28
  136.4 8.2 %copy-start.13 = (bf16[8,32,512]{2,1,0:T(8,128)(2,1)}, bf16[8,32,512]{2,1,0:T(8,128)(2,1)S(1)}, u32[]{:S(2)}) copy-start(bf16[8,32,512]{2,1,0:T(8,128)(2,1)S(1)} %collective-permute-done.2.zx_ref) | copy-start | bytes 786436
  136.4 8.2 %copy-start.12 = (bf16[1280,256]{1,0:T(8,128)(2,1)}, bf16[1280,256]{1,0:T(8,128)(2,1)S(1)}, u32[]{:S(2)}) copy-start(bf16[1280,256]{1,0:T(8,128)(2,1)S(1)} %collective-permute-done.1.hx_ref) | copy-start | bytes 1966084
  161.8 2.4 collective-permute-start.3
  164.3 6.6 %copy-start.1 = (bf16[16,80,512]{2,1,0:T(8,128)(2,1)S(1)}, bf16[16,80,512]{2,1,0:T(8,128)(2,1)}, u32[]{:S(2)}) copy-start(bf16[16,80,512]{2,1,0:T(8,128)(2,1)} %copy-done) | copy-start | bytes 3932164
  166.7 15.6 %all-to-all-start.3 = ((bf16[16,80,256]{2,1,0:T(8,128)(2,1)}), bf16[16,80,256]{2,1,0:T(8,128)(2,1)S(1)}, u32[]{:S(2)}, u32[]{:S(2)}) async-start(bf16[16,80,256]{2,1,0:T(8,128)(2,1)} %bitcast.10), calls=%async_computation.3 | async-start | bytes 1310720 | tf_op jit(solution)/shard_map/all_to_all | solution.py:248
  182.3 0.9 copy-start.4
  187.4 4.6 %collective-permute-start.4 = (bf16[320,1200]{1,0:T(8,128)(2,1)}, bf16[320,1200]{1,0:T(8,128)(2,1)S(1)}, u32[]{:S(2)}, u32[]{:S(2)}) collective-permute-start(bf16[320,1200]{1,0:T(8,128)(2,1)} %get-tuple-element.15), channel_id=1, source_target_pairs={{0,1},{1,0},{2,3},{3,2},{4,5},{5,4},{6,7},{7,6},{8,9},{9,8},{10,11... | collective-permute-start | bytes 2304008 | tf_op jit(solution)/shard_map/ppermute | solution.py:28
  193.6 57.5 %copy-start.11 = (f32[1200]{0:T(1024)S(1)}, f32[1200]{0:T(1024)}, u32[]{:S(2)}) copy-start(f32[1200]{0:T(1024)} %param.10) | copy-start | bytes 14404
  244.1 13.0 %copy-start.2 = (bf16[320,1200]{1,0:T(8,128)(2,1)}, bf16[320,1200]{1,0:T(8,128)(2,1)S(1)}, u32[]{:S(2)}) copy-start(bf16[320,1200]{1,0:T(8,128)(2,1)S(1)} %all_gather.23) | copy-start | bytes 2304004
  244.1 13.0 %collective-permute-start.5 = (bf16[320,1200]{1,0:T(8,128)(2,1)S(1)}, bf16[320,1200]{1,0:T(8,128)(2,1)S(1)}, u32[]{:S(2)}, u32[]{:S(2)}) collective-permute-start(bf16[320,1200]{1,0:T(8,128)(2,1)S(1)} %all_gather.23), channel_id=1, source_target_pairs={{0,1},{1,0},{2,3},{3,2},{4,5},{5,4},{6,7},{7,6},{8,9},{9,8},{10,11... | collective-permute-start | bytes 2304008 | tf_op jit(solution)/shard_map/ppermute | solution.py:28
  257.0 0.9 copy-start.6
  268.4 10.0 %all-to-all-start.5 = ((f32[16,8,128]{2,1,0:T(8,128)}), f32[16,8,128]{2,1,0:T(8,128)S(1)}, u32[]{:S(2)}, u32[]{:S(2)}) async-start(f32[16,8,128]{2,1,0:T(8,128)} %broadcast_in_dim.18), calls=%async_computation.5 | async-start | bytes 131072 | tf_op jit(solution)/shard_map/all_to_all | solution.py:272
Sparse Core Ops, SparseCore 0:
  34.9 109.6 all-gather.3

commit v2 on v1

v2 whole, which is shorter than its diff:
```python
import jax
import jax.numpy as jnp
from jax import lax
from jax.experimental import pallas as pl
from jax.experimental.pallas import tpu as pltpu
from jax.sharding import Mesh
from jax.sharding import PartitionSpec as P

AXES = ("x", "y", "z", "c")
XY = ("x", "y")
RANK = ("z", "c")
BF = jnp.bfloat16
F32 = jnp.float32
epsilon = 1e-06

NX, NY, NZ, NC = 4, 4, 8, 2
NV = NX * NY
PAIRS = 8
ROW = 75
PAD = 80
BLK = 512
QC = 32
NVIR = 1200
LANE = 128
HALF = PAD // 2
CHUNK = 5
WIDE = 1280


def core_swap(value):
    return lax.ppermute(value, "c", [(0, 1), (1, 0)])


def regroup(tiles, want):
    out = None
    lane = lax.broadcasted_iota(jnp.int32, (PAD, LANE), 1) // QC
    for group, tile in enumerate(tiles):
        shift = ((group - want) * QC) % LANE
        moved = pltpu.roll(tile, shift, 1) if shift else tile
        out = moved if out is None else jnp.where(lane == group, moved, out)
    return out


def half_kernel(core_ref, own_ref, oth_ref, xz_ref, out_ref, acc_ref):
    core = core_ref[0]
    dims = (((0,), (0,)), ((), ()))
    x_own = xz_ref[:, core, :PAD, :].reshape(NZ * PAD, BLK)
    x_oth = xz_ref[:, 1 - core, :PAD, :].reshape(NZ * PAD, BLK)
    acc_ref[...] = lax.dot_general(
        own_ref[...], x_own, dims, preferred_element_type=F32
    ) + lax.dot_general(oth_ref[...], x_oth, dims, preferred_element_type=F32)
    for xx in range(NX):
        for half in range(2):
            tiles = [
                acc_ref[pl.ds((half * 4 + g) * PAD, PAD), pl.ds(xx * LANE, LANE)]
                for g in range(4)
            ]
            for yy in range(NY):
                out_ref[xx * NY + yy, :, pl.ds(half * LANE, LANE)] = regroup(tiles, yy).astype(BF)


def make_half(place, t_own, t_oth, xz):
    return pl.pallas_call(
        half_kernel,
        out_shape=jax.ShapeDtypeStruct((NV, PAD, PAIRS * QC), BF),
        in_specs=[pl.BlockSpec(memory_space=pltpu.SMEM)]
        + [pl.BlockSpec(memory_space=pltpu.VMEM)] * 3,
        scratch_shapes=[pltpu.VMEM((PAIRS * PAD, BLK), F32)],
        name="half",
    )(place, t_own, t_oth, xz)


def main_kernel(
    place_ref, ho_ref, hx_ref, xq_ref, x_ref, zo_ref, zx_ref, bo_ref, bx_ref, h_ref, acc_ref
):
    step = pl.program_id(0)
    half_m = PAIRS * QC

    def block(x):
        coupled = jnp.dot(h_ref[...], x, preferred_element_type=F32)
        z_own = zo_ref[0, 0, PAD:, :].reshape(1, QC, BLK).astype(F32)
        z_oth = zx_ref[...].reshape(1, QC, BLK).astype(F32)
        c_own = coupled[:half_m].reshape(PAIRS, QC, BLK) * z_own
        c_oth = coupled[half_m:].reshape(PAIRS, QC, BLK) * z_oth
        w = jnp.concatenate(
            [c_own.reshape(half_m, BLK), c_oth.reshape(half_m, BLK)], axis=0
        ).astype(BF)
        return lax.dot_general(x, w, (((1,), (1,)), ((), ())), preferred_element_type=F32)

    @pl.when(step == 0)
    def _():
        h_ref[pl.ds(0, half_m), :] = ho_ref[...].astype(F32).T.astype(BF)
        h_ref[pl.ds(half_m, half_m), :] = hx_ref[...].astype(F32).T.astype(BF)
        acc_ref[...] = block(xq_ref[:, :PAD, :].reshape(NV * PAD, BLK))

    @pl.when(step > 0)
    def _():
        acc_ref[...] += block(x_ref[...].reshape(NV * PAD, BLK))

    @pl.when(step == NZ - 1)
    def _():
        bo_ref[...] = acc_ref[:, :half_m]
        bx_ref[...] = acc_ref[:, half_m:].astype(BF)


def make_main(place, h_own, h_oth, xz, x_all, z_oth):
    rows = NV * PAD
    half_m = PAIRS * QC
    return pl.pallas_call(
        main_kernel,
        out_shape=(
            jax.ShapeDtypeStruct((rows, half_m), F32),
            jax.ShapeDtypeStruct((rows, half_m), BF),
        ),
        grid_spec=pltpu.PrefetchScalarGridSpec(
            num_scalar_prefetch=1,
            grid=(NZ,),
            in_specs=[
                pl.BlockSpec((rows, half_m), lambda k, p: (0, 0)),
                pl.BlockSpec((rows, half_m), lambda k, p: (0, 0)),
                pl.BlockSpec((NV, PAD + QC, BLK), lambda k, p: (0, 0, 0)),
                pl.BlockSpec((NV, 1, PAD, BLK), lambda k, p: (0, jnp.maximum(k - 1, 0), 0, 0)),
                pl.BlockSpec((1, 1, PAD + QC, BLK), lambda k, p: ((p[1] + k) % NZ, p[0], 0, 0)),
                pl.BlockSpec((1, QC, BLK), lambda k, p: ((p[1] + k) % NZ, 0, 0)),
            ],
            out_specs=(
                pl.BlockSpec((rows, half_m), lambda k, p: (0, 0)),
                pl.BlockSpec((rows, half_m), lambda k, p: (0, 0)),
            ),
            scratch_shapes=[
                pltpu.VMEM((2 * half_m, rows), BF),
                pltpu.VMEM((rows, 2 * half_m), F32),
            ],
        ),
        compiler_params=pltpu.CompilerParams(dimension_semantics=("arbitrary",)),
        cost_estimate=pl.CostEstimate(
            flops=4 * 512 * 1280 * 4096, bytes_accessed=14_000_000, transcendentals=0
        ),
        name="ladder_core",
    )(place, h_own, h_oth, xz, x_all, xz.reshape(NZ, NC, PAD + QC, BLK), z_oth)


def ladder_kernel(place_ref, b_ref, x_ref, own_ref, oth_ref, g_ref):
    core = place_ref[0]
    for xx in range(NX):
        for half in range(2):
            tiles = [
                b_ref[xx * NY + yy, :, pl.ds(half * LANE, LANE)].astype(F32) for yy in range(NY)
            ]
            for g in range(4):
                g_ref[xx, pl.ds(half * 4 + g, PAD, stride=PAIRS), :] = regroup(tiles, g)
    dims = (((1,), (1,)), ((), ()))
    rows = HALF * PAIRS

    def gathered(which):
        start = pl.multiple_of(which * rows, rows)
        return jnp.concatenate([g_ref[xx, pl.ds(start, rows), :] for xx in range(NX)], axis=1)

    own = gathered(core).astype(BF)
    oth = gathered(1 - core).astype(BF)
    own_ref[...] = lax.dot_general(own, x_ref[...], dims, preferred_element_type=F32)
    oth_ref[...] = lax.dot_general(oth, x_ref[...], dims, preferred_element_type=F32).astype(BF)


def make_ladder(place, b_all, x_rows):
    return pl.pallas_call(
        ladder_kernel,
        out_shape=(
            jax.ShapeDtypeStruct((HALF * PAIRS, NVIR), F32),
            jax.ShapeDtypeStruct((HALF * PAIRS, NVIR), BF),
        ),
        in_specs=[pl.BlockSpec(memory_space=pltpu.SMEM)]
        + [pl.BlockSpec(memory_space=pltpu.VMEM)] * 2,
        scratch_shapes=[pltpu.VMEM((NX, PAIRS * PAD, LANE), F32)],
        name="ladder_rank",
    )(place, b_all, x_rows)


def chunk_kernel(place_ref, parts_ref, other_ref, col_ref, low_ref, out_ref):
    total = jnp.sum(parts_ref[...].astype(F32), axis=0)
    res = total + other_ref[...].reshape(CHUNK * PAIRS, NVIR)
    upd = res / (low_ref[...] + col_ref[...])
    squares = jnp.sum(upd * upd, axis=1, keepdims=True)
    squares = jnp.sum(squares, axis=0, keepdims=True)
    real = NC * NZ - 1
    squares = jnp.where(place_ref[2] < real, squares, 0.0)
    high = squares.astype(BF)
    rest = squares - high.astype(F32)
    mid = rest.astype(BF)
    low = (rest - mid.astype(F32)).astype(BF)
    out_ref[:, :NVIR] = total.astype(BF)
    lanes = WIDE - NVIR
    lane = lax.broadcasted_iota(jnp.int32, (CHUNK * PAIRS, lanes), 1)
    row = lax.broadcasted_iota(jnp.int32, (CHUNK * PAIRS, lanes), 0)
    kept = jnp.where(
        lane == 0, high.astype(F32), jnp.where(lane == 1, mid.astype(F32), low.astype(F32))
    )
    kept = jnp.where((row == 0) & (lane < 3), kept, 0.0)
    out_ref[:, NVIR:] = kept.astype(BF)


def make_chunk(place, parts, other_rows, col_energy, low_energy):
    last = ROW // CHUNK - 1
    return pl.pallas_call(
        chunk_kernel,
        out_shape=jax.ShapeDtypeStruct((CHUNK * PAIRS, WIDE), BF),
        grid_spec=pltpu.PrefetchScalarGridSpec(
            num_scalar_prefetch=1,
            grid=(1,),
            in_specs=[
                pl.BlockSpec((NZ, CHUNK * PAIRS, NVIR), lambda k, p: (0, 0, 0)),
                pl.BlockSpec((CHUNK, PAIRS, NVIR), lambda k, p: (jnp.minimum(p[2], last), 0, 0)),
                pl.BlockSpec((1, NVIR), lambda k, p: (0, 0)),
                pl.BlockSpec((CHUNK * PAIRS, 1), lambda k, p: (jnp.minimum(p[2], last), 0)),
            ],
            out_specs=pl.BlockSpec((CHUNK * PAIRS, WIDE), lambda k, p: (0, 0)),
        ),
        name="chunk",
    )(place, parts, other_rows, col_energy, low_energy)


def final_kernel(place_ref, own_ref, oth_ref, other_ref, out_ref):
    def fill(first, second):
        top = first[:, :NVIR].astype(F32).reshape(HALF, PAIRS, NVIR)
        out_ref[:HALF] = other_ref[:HALF] + top
        left = ROW - HALF
        end = second[: left * PAIRS, :NVIR].astype(F32).reshape(left, PAIRS, NVIR)
        out_ref[HALF:] = other_ref[HALF:] + end

    @pl.when(place_ref[0] == 0)
    def _():
        fill(own_ref, oth_ref)

    @pl.when(place_ref[0] == 1)
    def _():
        fill(oth_ref, own_ref)


def make_final(place, l_own, l_oth, other_rows):
    return pl.pallas_call(
        final_kernel,
        out_shape=jax.ShapeDtypeStruct((ROW, PAIRS, NVIR), F32),
        in_specs=[pl.BlockSpec(memory_space=pltpu.SMEM)]
        + [pl.BlockSpec(memory_space=pltpu.VMEM)] * 3,
        name="residual",
    )(place, l_own, l_oth, other_rows)


def shards(amplitudes, factors, kernel, other_terms, virt_energy, pair_energy):
    core = lax.axis_index("c").astype(jnp.int32)
    level = lax.axis_index("z").astype(jnp.int32)
    place = jnp.stack([core, level, core * NZ + level])

    x_pad = jnp.pad(factors, ((0, PAD - ROW), (0, 0)))
    x_far = [
        lax.ppermute(x_pad, "z", [(s, (s - j) % NZ) for s in range(NZ)]) for j in range(1, NZ)
    ]
    x_far = jnp.stack(x_far)
    x_all = lax.all_gather(x_far, XY, axis=0)

    z_cols = kernel.T.reshape(NV, QC, BLK)
    xz = jnp.concatenate([jnp.broadcast_to(x_pad[None], (NV, PAD, BLK)), z_cols], axis=1)
    t_cols = jnp.pad(amplitudes, ((0, 0), (0, PAD - ROW), (0, PAD - ROW)))
    t_cols = jnp.transpose(t_cols, (2, 0, 1)).reshape(PAD, PAIRS * PAD)
    t_cols, xz, _ = lax.optimization_barrier((t_cols, xz, x_far))
    xz = lax.all_to_all(xz, XY, split_axis=0, concat_axis=0, tiled=True)
    t_own = lax.all_gather(t_cols, "z", axis=0, tiled=True)
    t_oth = core_swap(t_own)
    x_rows = xz[:, :ROW].reshape(NVIR, BLK)

    h_msg = make_half(place, t_own, t_oth, xz.reshape(NZ, NC, PAD + QC, BLK))
    h_own = lax.all_to_all(h_msg, XY, split_axis=0, concat_axis=0, tiled=True)
    h_own = h_own.reshape(NV * PAD, PAIRS * QC)
    h_oth = core_swap(h_own)
    z_all = xz.reshape(NZ, NC, PAD + QC, BLK)
    z_oth = lax.dynamic_index_in_dim(z_all, 1 - core, 1, keepdims=False)[:, PAD:]
    z_oth = core_swap(z_oth)

    b_own, b_send = make_main(place, h_own, h_oth, xz, x_all, z_oth)
    b_sum = (b_own + core_swap(b_send).astype(F32)).astype(BF)
    b_all = lax.all_to_all(
        b_sum.reshape(NV, PAD, PAIRS * QC), XY, split_axis=0, concat_axis=0, tiled=True
    )

    l_own, l_send = make_ladder(place, b_all, x_rows)
    l_sum = (l_own + core_swap(l_send).astype(F32)).astype(BF)
    l_parts = lax.all_to_all(
        l_sum.reshape(NZ, CHUNK * PAIRS, NVIR), "z", split_axis=0, concat_axis=0, tiled=True
    )
    other_rows = jnp.transpose(other_terms, (1, 0, 2))
    row_energy = lax.dynamic_slice_in_dim(virt_energy, lax.axis_index(XY) * ROW, ROW, 0)
    low_energy = (row_energy[:, None] - pair_energy[None, :]).reshape(ROW * PAIRS, 1)
    chunk = make_chunk(place, l_parts, other_rows, virt_energy[None, :], low_energy)
    l_mine = lax.all_gather(chunk, "z", axis=0, tiled=True)
    l_rest = core_swap(l_mine)

    marks = jnp.concatenate([l_mine, l_rest]).reshape(NC * NZ, CHUNK * PAIRS, WIDE)
    squares = jnp.sum(marks[:, 0, NVIR : NVIR + 3].astype(F32))
    total = jnp.broadcast_to(squares, (NV, 8, LANE))
    totals = lax.all_to_all(total, XY, split_axis=0, concat_axis=0, tiled=True)
    residual = jnp.transpose(make_final(place, l_mine, l_rest, other_rows), (1, 0, 2))
    count = PAIRS * NVIR * NVIR
    update_rms = jnp.sqrt(jnp.sum(totals[:, 0, 0]) / count + epsilon)
    return residual, update_rms


def solution(mesh):
    torus = Mesh(mesh.devices.reshape(NX, NY, NZ, NC), AXES)
    return jax.shard_map(
        shards,
        mesh=torus,
        in_specs=(
            P(None, XY, RANK),
            P(XY, RANK),
            P(XY, RANK),
            P(None, XY, None),
            P(),
            P(),
        ),
        out_specs=(P(None, XY, None), P()),
        check_vma=False,
    )
```

time: 289 us -> 272 us (0.941)
  waiting for transfers between devices: 42.5 us -> 77.4 us
  blocking collectives: 97.6 us -> 68.4 us
  starting transfers between devices: 71.2 us -> 55.5 us
  local copies, waits for them, and re-layouts: 20.6 us -> 11 us
    all_gather x2 -> x1, blocking collectives: 47.1 us -> 20.6 us  [shards(): l_mine = lax.all_gather(chunk, 'z', axis=0, tiled=True)]
    ppermute x6, starting transfers between devices: 43.2 us -> 19.2 us  [core_swap(): return lax.ppermute(value, 'c', [(0, 1), (1, 0)])]
    ppermute x0 -> x7, starting transfers between devices: none -> 16.1 us  [shards(): lax.ppermute(x_pad, 'z', [(s, (s - j) % NZ) for s in range(NZ)])]
    all_gather x1, waiting for transfers between devices: 8.17 us -> 21.6 us  [shards(): x_all = lax.all_gather(x_far, XY, axis=0)]
    ppermute x0 -> x7, waiting for transfers between devices: none -> 11.8 us  [shards(): lax.ppermute(x_pad, 'z', [(s, (s - j) % NZ) for s in range(NZ)])]
    unnamed x31 -> x36, local copies, waits for them, and re-layouts: 14.1 us -> 3.84 us
    all_to_all x3 -> x2, starting transfers between devices: 20.3 us -> 11.7 us  [the longest x1 6.75 us: shards(): xz = lax.all_to_all(xz, XY, split_axis=0, concat_axis=0, tiled=True)]
    all_to_all x3 -> x2, waiting for transfers between devices: 15.8 us -> 23 us  [the longest x1 22.7 us: shards(): lax.all_to_all(l_sum.reshape(NZ, CHUNK * PAIRS, NVIR), 'z', split_axis=0,...]
  transfers between devices with their start and end apart: 12 -> 18, of which waited for: 9 -> 14; matrix products, arithmetic and copies ran while one was open for 5% -> 3% of each run, Pallas kernels for 2% -> 3%
where the time goes in v2:
time: 272 us; the launch traced here: 271 us
  waiting for transfers between devices  77.4 us (28%)
  blocking collectives  68.4 us (25%)
  starting transfers between devices  55.5 us (20%)
  Pallas kernels  34.3 us (13%)
  between operations  16 us (6%)
  local copies, waits for them, and re-layouts  11 us (4%)
  other arithmetic  8.44 us (3%)
    all_to_all x1, blocking collectives, shards(): h_own = lax.all_to_all(h_msg, XY, split_axis=0, concat_axis=0, tiled=True)  25.6 us
    all_to_all x1, waiting for transfers between devices, shards(): lax.all_to_all(l_sum.reshape(NZ, CHUNK * PAIRS, NVIR), 'z', split_axis=0,...  22.7 us
    all_gather x1, blocking collectives, shards(): t_own = lax.all_gather(t_cols, 'z', axis=0, tiled=True)  22.3 us
    all_gather x1, waiting for transfers between devices, shards(): x_all = lax.all_gather(x_far, XY, axis=0)  21.6 us
    all_gather x1, blocking collectives, shards(): l_mine = lax.all_gather(chunk, 'z', axis=0, tiled=True)  20.6 us
    ppermute x6, starting transfers between devices, core_swap(): return lax.ppermute(value, 'c', [(0, 1), (1, 0)])  19.2 us
    pallas_call x1, Pallas kernels, make_main(): pl.pallas_call(main_kernel, out_shape=(jax.ShapeDtypeStruct((rows, half_m...  18.3 us
    ppermute x7, starting transfers between devices, shards(): lax.ppermute(x_pad, 'z', [(s, (s - j) % NZ) for s in range(NZ)])  16.1 us
  transfers between devices with their start and end apart: 18, of which 14 were waited for; matrix products, arithmetic and copies ran while one was open for 3% of the time, Pallas kernels for 3%

profile of v2, /device:TPU:1, one launch (start us, length us, event | category | flops | bytes accessed | tf_op | source)
XLA Modules:
  0.0 271.2 jit_solution(7232159431799599963)
XLA Ops:
  8.2 6.4 %collective-permute-start = (bf16[80,512]{1,0:T(8,128)(2,1)S(1)}, bf16[80,512]{1,0:T(8,128)(2,1)S(1)}, u32[]{:S(2)}, u32[]{:S(2)}) collective-permute-start(bf16[80,512]{1,0:T(8,128)(2,1)S(1)} %pad.9), channel_id=1, source_target_pairs={{0,14},{2,0},{4,2},{6,4},{8,6},{10,8},{12,10},{14,12},{1,15},{3,1}... | collective-permute-start | bytes 245768 | tf_op jit(solution)/shard_map/ppermute | solution.py:256
  16.2 4.5 %collective-permute-start.3 = (bf16[80,512]{1,0:T(8,128)(2,1)S(1)}, bf16[80,512]{1,0:T(8,128)(2,1)S(1)}, u32[]{:S(2)}, u32[]{:S(2)}) collective-permute-start(bf16[80,512]{1,0:T(8,128)(2,1)S(1)} %pad.9), channel_id=1, source_target_pairs={{0,8},{2,10},{4,12},{6,14},{8,0},{10,2},{12,4},{14,6},{1,9},{3,11}... | collective-permute-start | bytes 245768 | tf_op jit(solution)/shard_map/ppermute | solution.py:256
  20.7 2.2 collective-permute-start.5
  22.8 1.5 collective-permute-start.6
  24.6 3.4 %collective-permute-done.4 = bf16[80,512]{1,0:T(8,128)(2,1)S(1)} collective-permute-done((bf16[80,512]{1,0:T(8,128)(2,1)S(1)}, bf16[80,512]{1,0:T(8,128)(2,1)S(1)}, u32[]{:S(2)}, u32[]{:S(2)}) %collective-permute-start.4) | collective-permute-done | bytes 81952 | tf_op jit(solution)/shard_map/ppermute | solution.py:256
  28.1 6.2 %collective-permute-done.5 = bf16[80,512]{1,0:T(8,128)(2,1)S(1)} collective-permute-done((bf16[80,512]{1,0:T(8,128)(2,1)S(1)}, bf16[80,512]{1,0:T(8,128)(2,1)S(1)}, u32[]{:S(2)}, u32[]{:S(2)}) %collective-permute-start.5) | collective-permute-done | bytes 81952 | tf_op jit(solution)/shard_map/ppermute | solution.py:256
  34.3 1.9 collective-permute-done.6
  39.2 6.8 %all-to-all-start = ((bf16[16,112,512]{2,1,0:T(8,128)(2,1)}), bf16[16,112,512]{2,1,0:T(8,128)(2,1)S(1)}, u32[]{:S(2)}, u32[]{:S(2)}) async-start(bf16[16,112,512]{2,1,0:T(8,128)(2,1)} %pad_maximum_fusion), calls=%async_computation | async-start | bytes 3670016 | tf_op jit(solution)/shard_map/all_to_all | solution.py:266
  45.9 22.3 %all_gather.12.own_ref = bf16[640,640]{1,0:T(8,128)(2,1)S(1)} all-gather(bf16[80,640]{1,0:T(8,128)(2,1)S(1)} %reshape.57), channel_id=1, replica_groups=mesh['x'=4,'y'=4,'z'=8,'c'=2] {'z'}, dimensions={0}, use_global_device_ids=true | all-gather | bytes 921600 | tf_op jit(solution)/shard_map/all_gather | solution.py:267
  68.2 5.1 %collective-permute-start.7 = (bf16[640,640]{1,0:T(8,128)(2,1)S(1)}, bf16[640,640]{1,0:T(8,128)(2,1)S(1)}, u32[]{:S(2)}, u32[]{:S(2)}) collective-permute-start(bf16[640,640]{1,0:T(8,128)(2,1)S(1)} %all_gather.12.own_ref), channel_id=1, source_target_pairs={{0,1},{1,0},{2,3},{3,2},{4,5},{5,4},{6,7},{7,6},{8,9},{9,8},{10,11... | collective-permute-start | bytes 2457608 | tf_op jit(solution)/shard_map/ppermute | solution.py:31
  76.9 4.5 %half.1 = bf16[16,80,256]{2,1,0:T(8,128)(2,1)} custom-call(s32[3]{0:T(128)} %pad_add_fusion.core_ref.place_ref, bf16[640,640]{1,0:T(8,128)(2,1)} %copy-done.4, bf16[640,640]{1,0:T(8,128)(2,1)} %copy-done.6, bf16[8,2,112,512]{3,2,1,0:T(8,128)(2,1)} %bitcast.31), custom_call_target="tpu_custom_call" | custom-call | tf_op jit(solution)/shard_map/half/pallas_call | solution.py:63
  81.5 25.6 %all_to_all.25 = bf16[16,80,256]{2,1,0:T(8,128)(2,1)S(1)} all-to-all(bf16[16,80,256]{2,1,0:T(8,128)(2,1)} %half.1), channel_id=1, replica_groups=mesh['x'=4,'y'=4,'z'=8,'c'=2] {'x','y'}, dimensions={0} | all-to-all | bytes 1310720 | tf_op jit(solution)/shard_map/all_to_all | solution.py:272
  107.0 4.0 %collective-permute-start.8 = (bf16[1280,256]{1,0:T(8,128)(2,1)S(1)}, bf16[1280,256]{1,0:T(8,128)(2,1)S(1)}, u32[]{:S(2)}, u32[]{:S(2)}) collective-permute-start(bf16[1280,256]{1,0:T(8,128)(2,1)S(1)} %bitcast.39), channel_id=1, source_target_pairs={{0,1},{1,0},{2,3},{3,2},{4,5},{5,4},{6,7},{7,6},{8,9},{9,8},{10,11... | collective-permute-start | bytes 1966088 | tf_op jit(solution)/shard_map/ppermute | solution.py:31
  114.1 21.6 %all-gather.3.cloned.1.call-done = bf16[112,80,512]{2,1,0:T(8,128)(2,1)} async-done(((bf16[7,80,512]{2,1,0:T(8,128)(2,1)}), bf16[112,80,512]{2,1,0:T(8,128)(2,1)}) %all-gather.3.cloned.1.call-update) | async-done | bytes 9175056 | tf_op jit(solution)/shard_map/all_gather | solution.py:259
  135.7 18.3 %ladder_core.1 = (f32[1280,256]{1,0:T(8,128)}, bf16[1280,256]{1,0:T(8,128)(2,1)}) custom-call(s32[3]{0:T(128)} %pad_add_fusion.core_ref.place_ref, bf16[1280,256]{1,0:T(8,128)(2,1)} %bitcast.40, bf16[1280,256]{1,0:T(8,128)(2,1)} %copy-done.13, bf16[16,112,512]{2,1,0:T(8,128)(2,1)} %copy-done, bf16[16,7,80,512]{3,2,1,0:T(8,128)(2,1)} %bitcast.42, ...), custom_call_target="tpu_custom_call" | custom-call | flops 10737418240 | bytes 14000000 | tf_op jit(solution)/shard_map/ladder_core/pallas_call | solution.py:109
  154.8 1.9 collective-permute-done.10
  156.8 2.5 add_convert_fusion.1
  159.2 5.0 %all-to-all-start.2 = ((bf16[16,80,256]{2,1,0:T(8,128)(2,1)}), bf16[16,80,256]{2,1,0:T(8,128)(2,1)}, u32[]{:S(2)}, u32[]{:S(2)}) async-start(bf16[16,80,256]{2,1,0:T(8,128)(2,1)} %bitcast.17), calls=%async_computation.2 | async-start | bytes 1310720 | tf_op jit(solution)/shard_map/all_to_all | solution.py:281
  165.7 10.1 %all-to-all-done.2.b_ref = bf16[16,80,256]{2,1,0:T(8,128)(2,1)} async-done(((bf16[16,80,256]{2,1,0:T(8,128)(2,1)}), bf16[16,80,256]{2,1,0:T(8,128)(2,1)}, u32[]{:S(2)}, u32[]{:S(2)}) %all-to-all-start.2) | async-done | bytes 655392 | tf_op jit(solution)/shard_map/all_to_all | solution.py:281
  175.8 4.4 %ladder_rank.1 = (f32[320,1200]{1,0:T(8,128)}, bf16[320,1200]{1,0:T(8,128)(2,1)}) custom-call(s32[3]{0:T(128)} %pad_add_fusion.core_ref.place_ref, bf16[16,80,256]{2,1,0:T(8,128)(2,1)} %all-to-all-done.2.b_ref, bf16[1200,512]{1,0:T(8,128)(2,1)} %reshape.62.x_ref), custom_call_target="tpu_custom_call" | custom-call | tf_op jit(solution)/shard_map/ladder_rank/pallas_call | solution.py:166
  180.1 2.4 collective-permute-start.11
  182.6 2.2 collective-permute-done.11
  184.7 2.5 add_convert_fusion
  187.2 4.9 %all-to-all-start.3 = ((bf16[8,40,1200]{2,1,0:T(8,128)(2,1)}), bf16[8,40,1200]{2,1,0:T(8,128)(2,1)S(1)}, u32[]{:S(2)}, u32[]{:S(2)}) async-start(bf16[8,40,1200]{2,1,0:T(8,128)(2,1)} %bitcast.18), calls=%async_computation.3 | async-start | bytes 1638400 | tf_op jit(solution)/shard_map/all_to_all | solution.py:287
  193.8 22.7 %all-to-all-done.3.parts_ref = bf16[8,40,1200]{2,1,0:T(8,128)(2,1)S(1)} async-done(((bf16[8,40,1200]{2,1,0:T(8,128)(2,1)}), bf16[8,40,1200]{2,1,0:T(8,128)(2,1)S(1)}, u32[]{:S(2)}, u32[]{:S(2)}) %all-to-all-start.3) | async-done | bytes 768032 | tf_op jit(solution)/shard_map/all_to_all | solution.py:287
  217.3 2.8 %chunk.1 = bf16[40,1280]{1,0:T(8,128)(2,1)} custom-call(s32[3]{0:T(128)} %pad_add_fusion.core_ref.place_ref, bf16[8,40,1200]{2,1,0:T(8,128)(2,1)} %copy-done.3, f32[75,8,1200]{2,1,0:T(8,128)} %bitcast.34, f32[1,1200]{1,0:T(1,128)} %broadcast_in_dim.7.col_ref, f32[600,1]{1,0:T(8,128)} %sub.31.low_ref), custom_call_target="tpu_custom_call" | custom-call | tf_op jit(solution)/shard_map/chunk/pallas_call | solution.py:204
  220.1 20.6 %all_gather.15.own_ref = bf16[320,1280]{1,0:T(8,128)(2,1)S(1)} all-gather(bf16[40,1280]{1,0:T(8,128)(2,1)} %chunk.1), channel_id=1, replica_groups=mesh['x'=4,'y'=4,'z'=8,'c'=2] {'z'}, dimensions={0}, use_global_device_ids=true | all-gather | bytes 921600 | tf_op jit(solution)/shard_map/all_gather | solution.py:294
  240.7 6.3 %collective-permute-start.12 = (bf16[320,1280]{1,0:T(8,128)(2,1)S(1)}, bf16[320,1280]{1,0:T(8,128)(2,1)S(1)}, u32[]{:S(2)}, u32[]{:S(2)}) collective-permute-start(bf16[320,1280]{1,0:T(8,128)(2,1)S(1)} %all_gather.15.own_ref), channel_id=1, source_target_pairs={{0,1},{1,0},{2,3},{3,2},{4,5},{5,4},{6,7},{7,6},{8,9},{9,8},{10,11... | collective-permute-start | bytes 2457608 | tf_op jit(solution)/shard_map/ppermute | solution.py:31
  247.1 2.0 collective-permute-done.12.oth_ref
  251.9 3.5 %all-to-all-start.4 = ((f32[16,8,128]{2,1,0:T(8,128)}), f32[16,8,128]{2,1,0:T(8,128)S(1)}, u32[]{:S(2)}, u32[]{:S(2)}) async-start(f32[16,8,128]{2,1,0:T(8,128)} %broadcast_in_dim.16), calls=%async_computation.4 | async-start | bytes 131072 | tf_op jit(solution)/shard_map/all_to_all | solution.py:300
  255.4 4.3 %residual.1 = f32[75,8,1200]{2,1,0:T(8,128)} custom-call(s32[3]{0:T(128)} %pad_add_fusion.core_ref.place_ref, bf16[320,1280]{1,0:T(8,128)(2,1)} %copy-done.2, bf16[320,1280]{1,0:T(8,128)(2,1)} %copy-done.5, f32[75,8,1200]{2,1,0:T(8,128)} %bitcast.35), custom_call_target="tpu_custom_call" | custom-call | tf_op jit(solution)/shard_map/residual/pallas_call | solution.py:240
  259.7 2.2 all-to-all-done.4
  (72 shorter events, 20.8 us)
Async XLA Ops:
  7.2 29.9 %copy-start.9 = (bf16[512,512]{1,0:T(8,128)(2,1)S(1)}, bf16[512,512]{1,0:T(8,128)(2,1)}, u32[]{:S(2)}) copy-start(bf16[512,512]{1,0:T(8,128)(2,1)} %param.8) | copy-start | bytes 1572868
  7.2 30.1 %copy-start.10 = (bf16[8,75,75]{2,0,1:T(8,128)(2,1)S(1)}, bf16[8,75,75]{2,0,1:T(8,128)(2,1)}, u32[]{:S(2)}) copy-start(bf16[8,75,75]{2,0,1:T(8,128)(2,1)} %param.6) | copy-start | bytes 270004
  7.2 128.5 %all-gather.3.cloned.1.call-start = ((), (), s32[]{:S(2)}) async-start(), calls=%async_computation.5 | async-start | bytes 9748480 | tf_op jit(solution)/shard_map/all_gather | solution.py:259
  8.2 12.5 %collective-permute-start = (bf16[80,512]{1,0:T(8,128)(2,1)S(1)}, bf16[80,512]{1,0:T(8,128)(2,1)S(1)}, u32[]{:S(2)}, u32[]{:S(2)}) collective-permute-start(bf16[80,512]{1,0:T(8,128)(2,1)S(1)} %pad.9), channel_id=1, source_target_pairs={{0,14},{2,0},{4,2},{6,4},{8,6},{10,8},{12,10},{14,12},{1,15},{3,1}... | collective-permute-start | bytes 245768 | tf_op jit(solution)/shard_map/ppermute | solution.py:256
  14.6 8.3 %collective-permute-start.1 = (bf16[80,512]{1,0:T(8,128)(2,1)S(1)}, bf16[80,512]{1,0:T(8,128)(2,1)S(1)}, u32[]{:S(2)}, u32[]{:S(2)}) collective-permute-start(bf16[80,512]{1,0:T(8,128)(2,1)S(1)} %pad.9), channel_id=1, source_target_pairs={{0,12},{2,14},{4,0},{6,2},{8,4},{10,6},{12,8},{14,10},{1,13},{3,15... | collective-permute-start | bytes 245768 | tf_op jit(solution)/shard_map/ppermute | solution.py:256
  15.7 8.6 %collective-permute-start.2 = (bf16[80,512]{1,0:T(8,128)(2,1)S(1)}, bf16[80,512]{1,0:T(8,128)(2,1)S(1)}, u32[]{:S(2)}, u32[]{:S(2)}) collective-permute-start(bf16[80,512]{1,0:T(8,128)(2,1)S(1)} %pad.9), channel_id=1, source_target_pairs={{0,10},{2,12},{4,14},{6,0},{8,2},{10,4},{12,6},{14,8},{1,11},{3,13... | collective-permute-start | bytes 245768 | tf_op jit(solution)/shard_map/ppermute | solution.py:256
  16.2 8.4 %collective-permute-start.3 = (bf16[80,512]{1,0:T(8,128)(2,1)S(1)}, bf16[80,512]{1,0:T(8,128)(2,1)S(1)}, u32[]{:S(2)}, u32[]{:S(2)}) collective-permute-start(bf16[80,512]{1,0:T(8,128)(2,1)S(1)} %pad.9), channel_id=1, source_target_pairs={{0,8},{2,10},{4,12},{6,14},{8,0},{10,2},{12,4},{14,6},{1,9},{3,11}... | collective-permute-start | bytes 245768 | tf_op jit(solution)/shard_map/ppermute | solution.py:256
  20.7 7.4 %collective-permute-start.4 = (bf16[80,512]{1,0:T(8,128)(2,1)S(1)}, bf16[80,512]{1,0:T(8,128)(2,1)S(1)}, u32[]{:S(2)}, u32[]{:S(2)}) collective-permute-start(bf16[80,512]{1,0:T(8,128)(2,1)S(1)} %pad.9), channel_id=1, source_target_pairs={{0,6},{2,8},{4,10},{6,12},{8,14},{10,0},{12,2},{14,4},{1,7},{3,9},... | collective-permute-start | bytes 245768 | tf_op jit(solution)/shard_map/ppermute | solution.py:256
  20.7 13.6 %collective-permute-start.5 = (bf16[80,512]{1,0:T(8,128)(2,1)S(1)}, bf16[80,512]{1,0:T(8,128)(2,1)S(1)}, u32[]{:S(2)}, u32[]{:S(2)}) collective-permute-start(bf16[80,512]{1,0:T(8,128)(2,1)S(1)} %pad.9), channel_id=1, source_target_pairs={{0,4},{2,6},{4,8},{6,10},{8,12},{10,14},{12,0},{14,2},{1,5},{3,7},... | collective-permute-start | bytes 245768 | tf_op jit(solution)/shard_map/ppermute | solution.py:256
  22.8 13.3 %collective-permute-start.6 = (bf16[80,512]{1,0:T(8,128)(2,1)S(1)}, bf16[80,512]{1,0:T(8,128)(2,1)S(1)}, u32[]{:S(2)}, u32[]{:S(2)}) collective-permute-start(bf16[80,512]{1,0:T(8,128)(2,1)S(1)} %pad.9), channel_id=1, source_target_pairs={{0,2},{2,4},{4,6},{6,8},{8,10},{10,12},{12,14},{14,0},{1,3},{3,5},... | collective-permute-start | bytes 245768 | tf_op jit(solution)/shard_map/ppermute | solution.py:256
  39.2 36.5 %all-to-all-start = ((bf16[16,112,512]{2,1,0:T(8,128)(2,1)}), bf16[16,112,512]{2,1,0:T(8,128)(2,1)S(1)}, u32[]{:S(2)}, u32[]{:S(2)}) async-start(bf16[16,112,512]{2,1,0:T(8,128)(2,1)} %pad_maximum_fusion), calls=%async_computation | async-start | bytes 3670016 | tf_op jit(solution)/shard_map/all_to_all | solution.py:266
  68.2 7.5 %copy-start.4 = (bf16[640,640]{1,0:T(8,128)(2,1)}, bf16[640,640]{1,0:T(8,128)(2,1)S(1)}, u32[]{:S(2)}) copy-start(bf16[640,640]{1,0:T(8,128)(2,1)S(1)} %all_gather.12.own_ref) | copy-start | bytes 2457604
  68.2 7.1 %collective-permute-start.7 = (bf16[640,640]{1,0:T(8,128)(2,1)S(1)}, bf16[640,640]{1,0:T(8,128)(2,1)S(1)}, u32[]{:S(2)}, u32[]{:S(2)}) collective-permute-start(bf16[640,640]{1,0:T(8,128)(2,1)S(1)} %all_gather.12.own_ref), channel_id=1, source_target_pairs={{0,1},{1,0},{2,3},{3,2},{4,5},{5,4},{6,7},{7,6},{8,9},{9,8},{10,11... | collective-permute-start | bytes 2457608 | tf_op jit(solution)/shard_map/ppermute | solution.py:31
  75.3 0.9 copy-start.6
  75.7 1.2 copy-start
  107.0 28.7 %copy-start.8 = (bf16[16,80,256]{2,1,0:T(8,128)(2,1)}, bf16[16,80,256]{2,1,0:T(8,128)(2,1)S(1)}, u32[]{:S(2)}) copy-start(bf16[16,80,256]{2,1,0:T(8,128)(2,1)S(1)} %all_to_all.25) | copy-start | bytes 1966084
  107.0 7.1 %collective-permute-start.8 = (bf16[1280,256]{1,0:T(8,128)(2,1)S(1)}, bf16[1280,256]{1,0:T(8,128)(2,1)S(1)}, u32[]{:S(2)}, u32[]{:S(2)}) collective-permute-start(bf16[1280,256]{1,0:T(8,128)(2,1)S(1)} %bitcast.39), channel_id=1, source_target_pairs={{0,1},{1,0},{2,3},{3,2},{4,5},{5,4},{6,7},{7,6},{8,9},{9,8},{10,11... | collective-permute-start | bytes 1966088 | tf_op jit(solution)/shard_map/ppermute | solution.py:31
  112.3 1.8 collective-permute-start.9
  114.1 21.6 %copy-start.14 = (bf16[8,32,512]{2,1,0:T(8,128)(2,1)}, bf16[8,32,512]{2,1,0:T(8,128)(2,1)S(1)}, u32[]{:S(2)}) copy-start(bf16[8,32,512]{2,1,0:T(8,128)(2,1)S(1)} %collective-permute-done.9.zx_ref) | copy-start | bytes 786436
  114.1 21.6 %copy-start.13 = (bf16[1280,256]{1,0:T(8,128)(2,1)}, bf16[1280,256]{1,0:T(8,128)(2,1)S(1)}, u32[]{:S(2)}) copy-start(bf16[1280,256]{1,0:T(8,128)(2,1)S(1)} %collective-permute-done.8.hx_ref) | copy-start | bytes 1966084
  154.0 2.8 %collective-permute-start.10 = (bf16[1280,256]{1,0:T(8,128)(2,1)}, bf16[1280,256]{1,0:T(8,128)(2,1)S(1)}, u32[]{:S(2)}, u32[]{:S(2)}) collective-permute-start(bf16[1280,256]{1,0:T(8,128)(2,1)} %get-tuple-element.11), channel_id=1, source_target_pairs={{0,1},{1,0},{2,3},{3,2},{4,5},{5,4},{6,7},{7,6},{8,9},{9,8},{10,11... | collective-permute-start | bytes 1966088 | tf_op jit(solution)/shard_map/ppermute | solution.py:31
  156.8 7.5 %copy-start.1 = (bf16[16,112,512]{2,1,0:T(8,128)(2,1)S(1)}, bf16[16,112,512]{2,1,0:T(8,128)(2,1)}, u32[]{:S(2)}) copy-start(bf16[16,112,512]{2,1,0:T(8,128)(2,1)} %copy-done) | copy-start | bytes 5505028
  159.2 16.5 %all-to-all-start.2 = ((bf16[16,80,256]{2,1,0:T(8,128)(2,1)}), bf16[16,80,256]{2,1,0:T(8,128)(2,1)}, u32[]{:S(2)}, u32[]{:S(2)}) async-start(bf16[16,80,256]{2,1,0:T(8,128)(2,1)} %bitcast.17), calls=%async_computation.2 | async-start | bytes 1310720 | tf_op jit(solution)/shard_map/all_to_all | solution.py:281
  180.1 4.6 %collective-permute-start.11 = (bf16[320,1200]{1,0:T(8,128)(2,1)}, bf16[320,1200]{1,0:T(8,128)(2,1)S(1)}, u32[]{:S(2)}, u32[]{:S(2)}) collective-permute-start(bf16[320,1200]{1,0:T(8,128)(2,1)} %get-tuple-element.13), channel_id=1, source_target_pairs={{0,1},{1,0},{2,3},{3,2},{4,5},{5,4},{6,7},{7,6},{8,9},{9,8},{10,11... | collective-permute-start | bytes 2304008 | tf_op jit(solution)/shard_map/ppermute | solution.py:31
  187.2 4.9 %copy-start.11 = (f32[1200]{0:T(1024)S(1)}, f32[1200]{0:T(1024)}, u32[]{:S(2)}) copy-start(f32[1200]{0:T(1024)} %param.10) | copy-start | bytes 14404
  187.2 5.6 %copy-start.12 = (f32[8]{0:T(128)S(1)}, f32[8]{0:T(128)}, u32[]{:S(2)}) copy-start(f32[8]{0:T(128)} %param.11) | copy-start | bytes 100
  187.2 29.2 %all-to-all-start.3 = ((bf16[8,40,1200]{2,1,0:T(8,128)(2,1)}), bf16[8,40,1200]{2,1,0:T(8,128)(2,1)S(1)}, u32[]{:S(2)}, u32[]{:S(2)}) async-start(bf16[8,40,1200]{2,1,0:T(8,128)(2,1)} %bitcast.18), calls=%async_computation.3 | async-start | bytes 1638400 | tf_op jit(solution)/shard_map/all_to_all | solution.py:287
  216.5 0.9 copy-start.3
  240.7 8.4 %copy-start.2 = (bf16[320,1280]{1,0:T(8,128)(2,1)}, bf16[320,1280]{1,0:T(8,128)(2,1)S(1)}, u32[]{:S(2)}) copy-start(bf16[320,1280]{1,0:T(8,128)(2,1)S(1)} %all_gather.15.own_ref) | copy-start | bytes 2457604
  240.7 8.3 %collective-permute-start.12 = (bf16[320,1280]{1,0:T(8,128)(2,1)S(1)}, bf16[320,1280]{1,0:T(8,128)(2,1)S(1)}, u32[]{:S(2)}, u32[]{:S(2)}) collective-permute-start(bf16[320,1280]{1,0:T(8,128)(2,1)S(1)} %all_gather.15.own_ref), channel_id=1, source_target_pairs={{0,1},{1,0},{2,3},{3,2},{4,5},{5,4},{6,7},{7,6},{8,9},{9,8},{10,11... | collective-permute-start | bytes 2457608 | tf_op jit(solution)/shard_map/ppermute | solution.py:31
  249.0 0.9 copy-start.5
  251.9 10.0 %all-to-all-start.4 = ((f32[16,8,128]{2,1,0:T(8,128)}), f32[16,8,128]{2,1,0:T(8,128)S(1)}, u32[]{:S(2)}, u32[]{:S(2)}) async-start(f32[16,8,128]{2,1,0:T(8,128)} %broadcast_in_dim.16), calls=%async_computation.4 | async-start | bytes 131072 | tf_op jit(solution)/shard_map/all_to_all | solution.py:300
  (1 other events, 0.8 us)
Sparse Core Ops, SparseCore 0:
  37.2 98.4 all-gather.2

commit v3 on v2

--- a/solution.py
+++ b/solution.py
@@ -70,13 +70,32 @@
     )(place, t_own, t_oth, xz)
 
 
+def level_of(step, place):
+    far = jnp.where(step == 2, NZ - 1, jnp.where(step > 2, step - 1, step))
+    return (place[1] + far) % NZ
+
+
 def main_kernel(
-    place_ref, ho_ref, hx_ref, xq_ref, x_ref, zo_ref, zx_ref, bo_ref, bx_ref, h_ref, acc_ref
+    place_ref,
+    ho_ref,
+    hx_ref,
+    xq_ref,
+    xu_ref,
+    xd_ref,
+    x_ref,
+    zo_ref,
+    zx_ref,
+    bo_ref,
+    bx_ref,
+    h_ref,
+    acc_ref,
+    now_ref,
 ):
     step = pl.program_id(0)
     half_m = PAIRS * QC
 
-    def block(x):
+    def block():
+        x = now_ref[...]
         coupled = jnp.dot(h_ref[...], x, preferred_element_type=F32)
         z_own = zo_ref[0, 0, PAD:, :].reshape(1, QC, BLK).astype(F32)
         z_oth = zx_ref[...].reshape(1, QC, BLK).astype(F32)
@@ -91,11 +110,22 @@
     def _():
         h_ref[pl.ds(0, half_m), :] = ho_ref[...].astype(F32).T.astype(BF)
         h_ref[pl.ds(half_m, half_m), :] = hx_ref[...].astype(F32).T.astype(BF)
-        acc_ref[...] = block(xq_ref[:, :PAD, :].reshape(NV * PAD, BLK))
-
-    @pl.when(step > 0)
-    def _():
-        acc_ref[...] += block(x_ref[...].reshape(NV * PAD, BLK))
+        acc_ref[...] = jnp.zeros_like(acc_ref)
+        now_ref[...] = xq_ref[:, :PAD, :].reshape(NV * PAD, BLK)
+
+    @pl.when(step == 1)
+    def _():
+        now_ref[...] = xu_ref[...].reshape(NV * PAD, BLK)
+
+    @pl.when(step == 2)
+    def _():
+        now_ref[...] = xd_ref[...].reshape(NV * PAD, BLK)
+
+    @pl.when(step > 2)
+    def _():
+        now_ref[...] = x_ref[...].reshape(NV * PAD, BLK)
+
+    acc_ref[...] += block()
 
     @pl.when(step == NZ - 1)
     def _():
@@ -103,7 +133,7 @@
         bx_ref[...] = acc_ref[:, half_m:].astype(BF)
 
 
-def make_main(place, h_own, h_oth, xz, x_all, z_oth):
+def make_main(place, h_own, h_oth, xz, x_up, x_down, x_all, z_oth):
     rows = NV * PAD
     half_m = PAIRS * QC
     return pl.pallas_call(
@@ -119,9 +149,11 @@
                 pl.BlockSpec((rows, half_m), lambda k, p: (0, 0)),
                 pl.BlockSpec((rows, half_m), lambda k, p: (0, 0)),
                 pl.BlockSpec((NV, PAD + QC, BLK), lambda k, p: (0, 0, 0)),
-                pl.BlockSpec((NV, 1, PAD, BLK), lambda k, p: (0, jnp.maximum(k - 1, 0), 0, 0)),
-                pl.BlockSpec((1, 1, PAD + QC, BLK), lambda k, p: ((p[1] + k) % NZ, p[0], 0, 0)),
-                pl.BlockSpec((1, QC, BLK), lambda k, p: ((p[1] + k) % NZ, 0, 0)),
+                pl.BlockSpec((NV, PAD, BLK), lambda k, p: (0, 0, 0)),
+                pl.BlockSpec((NV, PAD, BLK), lambda k, p: (0, 0, 0)),
+                pl.BlockSpec((NV, 1, PAD, BLK), lambda k, p: (0, jnp.maximum(k - 3, 0), 0, 0)),
+                pl.BlockSpec((1, 1, PAD + QC, BLK), lambda k, p: (level_of(k, p), p[0], 0, 0)),
+                pl.BlockSpec((1, QC, BLK), lambda k, p: (level_of(k, p), 0, 0)),
             ],
             out_specs=(
                 pl.BlockSpec((rows, half_m), lambda k, p: (0, 0)),
@@ -130,6 +162,7 @@
             scratch_shapes=[
                 pltpu.VMEM((2 * half_m, rows), BF),
                 pltpu.VMEM((rows, 2 * half_m), F32),
+                pltpu.VMEM((rows, BLK), BF),
             ],
         ),
         compiler_params=pltpu.CompilerParams(dimension_semantics=("arbitrary",)),
@@ -137,7 +170,7 @@
             flops=4 * 512 * 1280 * 4096, bytes_accessed=14_000_000, transcendentals=0
         ),
         name="ladder_core",
-    )(place, h_own, h_oth, xz, x_all, xz.reshape(NZ, NC, PAD + QC, BLK), z_oth)
+    )(place, h_own, h_oth, xz, x_up, x_down, x_all, xz.reshape(NZ, NC, PAD + QC, BLK), z_oth)
 
 
 def ladder_kernel(place_ref, b_ref, x_ref, own_ref, oth_ref, g_ref):
@@ -253,7 +286,7 @@
 
     x_pad = jnp.pad(factors, ((0, PAD - ROW), (0, 0)))
     x_far = [
-        lax.ppermute(x_pad, "z", [(s, (s - j) % NZ) for s in range(NZ)]) for j in range(1, NZ)
+        lax.ppermute(x_pad, "z", [(s, (s - j) % NZ) for s in range(NZ)]) for j in range(2, NZ - 1)
     ]
     x_far = jnp.stack(x_far)
     x_all = lax.all_gather(x_far, XY, axis=0)
@@ -262,10 +295,13 @@
     xz = jnp.concatenate([jnp.broadcast_to(x_pad[None], (NV, PAD, BLK)), z_cols], axis=1)
     t_cols = jnp.pad(amplitudes, ((0, 0), (0, PAD - ROW), (0, PAD - ROW)))
     t_cols = jnp.transpose(t_cols, (2, 0, 1)).reshape(PAD, PAIRS * PAD)
-    t_cols, xz, _ = lax.optimization_barrier((t_cols, xz, x_far))
+    t_cols, _ = lax.optimization_barrier((t_cols, x_far))
     xz = lax.all_to_all(xz, XY, split_axis=0, concat_axis=0, tiled=True)
     t_own = lax.all_gather(t_cols, "z", axis=0, tiled=True)
     t_oth = core_swap(t_own)
+    x_own = xz[:, :PAD]
+    x_up = lax.ppermute(x_own, "z", [(s, (s - 1) % NZ) for s in range(NZ)])
+    x_down = lax.ppermute(x_own, "z", [(s, (s + 1) % NZ) for s in range(NZ)])
     x_rows = xz[:, :ROW].reshape(NVIR, BLK)
 
     h_msg = make_half(place, t_own, t_oth, xz.reshape(NZ, NC, PAD + QC, BLK))
@@ -276,7 +312,7 @@
     z_oth = lax.dynamic_index_in_dim(z_all, 1 - core, 1, keepdims=False)[:, PAD:]
     z_oth = core_swap(z_oth)
 
-    b_own, b_send = make_main(place, h_own, h_oth, xz, x_all, z_oth)
+    b_own, b_send = make_main(place, h_own, h_oth, xz, x_up, x_down, x_all, z_oth)
     b_sum = (b_own + core_swap(b_send).astype(F32)).astype(BF)
     b_all = lax.all_to_all(
         b_sum.reshape(NV, PAD, PAIRS * QC), XY, split_axis=0, concat_axis=0, tiled=True

time: 272 us -> 261 us (0.960)
  waiting for transfers between devices: 77.4 us -> 59.4 us
  starting transfers between devices: 55.5 us -> 58.3 us
    all_gather x1, waiting for transfers between devices: 21.6 us -> 8.3 us  [shards(): x_all = lax.all_gather(x_far, XY, axis=0)]
    ppermute x7 -> x5, waiting for transfers between devices: 11.8 us -> 8.81 us  [shards(): lax.ppermute(x_pad, 'z', [(s, (s - j) % NZ) for s in range(NZ)])]
    ppermute x7 -> x5, starting transfers between devices: 16.1 us -> 14.6 us  [shards(): lax.ppermute(x_pad, 'z', [(s, (s - j) % NZ) for s in range(NZ)])]
  transfers between devices with their start and end apart: 18 -> 18, of which waited for: 14 -> 12; matrix products, arithmetic and copies ran while one was open for 3% -> 3% of each run, Pallas kernels for 3% -> 3%
where the time goes in v3:
time: 261 us; the launch traced here: 260 us
  blocking collectives  69.8 us (27%)
  waiting for transfers between devices  59.4 us (23%)
  starting transfers between devices  58.3 us (22%)
  Pallas kernels  36.4 us (14%)
  between operations  16 us (6%)
  local copies, waits for them, and re-layouts  11.8 us (5%)
  other arithmetic  8.41 us (3%)
    all_to_all x1, blocking collectives, shards(): h_own = lax.all_to_all(h_msg, XY, split_axis=0, concat_axis=0, tiled=True)  25.8 us
    all_gather x1, blocking collectives, shards(): t_own = lax.all_gather(t_cols, 'z', axis=0, tiled=True)  23.4 us
    all_to_all x1, waiting for transfers between devices, shards(): lax.all_to_all(l_sum.reshape(NZ, CHUNK * PAIRS, NVIR), 'z', split_axis=0,...  22.7 us
    all_gather x1, blocking collectives, shards(): l_mine = lax.all_gather(chunk, 'z', axis=0, tiled=True)  20.6 us
    pallas_call x1, Pallas kernels, make_main(): pl.pallas_call(main_kernel, out_shape=(jax.ShapeDtypeStruct((rows, half_m...  20.4 us
    ppermute x6, starting transfers between devices, core_swap(): return lax.ppermute(value, 'c', [(0, 1), (1, 0)])  20 us
    ppermute x5, starting transfers between devices, shards(): lax.ppermute(x_pad, 'z', [(s, (s - j) % NZ) for s in range(NZ)])  14.6 us
    all_to_all x1, waiting for transfers between devices, shards(): lax.all_to_all(b_sum.reshape(NV, PAD, PAIRS * QC), XY, split_axis=0, conc...  10.1 us
  transfers between devices with their start and end apart: 18, of which 12 were waited for; matrix products, arithmetic and copies ran while one was open for 3% of the time, Pallas kernels for 3%

profile of v3, /device:TPU:1, one launch (start us, length us, event | category | flops | bytes accessed | tf_op | source)
XLA Modules:
  0.0 260.2 jit_solution(3198604938388411405)
XLA Ops:
  8.2 6.8 %collective-permute-start = (bf16[80,512]{1,0:T(8,128)(2,1)S(1)}, bf16[80,512]{1,0:T(8,128)(2,1)S(1)}, u32[]{:S(2)}, u32[]{:S(2)}) collective-permute-start(bf16[80,512]{1,0:T(8,128)(2,1)S(1)} %pad.9), channel_id=1, source_target_pairs={{0,12},{2,14},{4,0},{6,2},{8,4},{10,6},{12,8},{14,10},{1,13},{3,15... | collective-permute-start | bytes 245768 | tf_op jit(solution)/shard_map/ppermute | solution.py:289
  15.7 4.2 %collective-permute-start.2 = (bf16[80,512]{1,0:T(8,128)(2,1)S(1)}, bf16[80,512]{1,0:T(8,128)(2,1)S(1)}, u32[]{:S(2)}, u32[]{:S(2)}) collective-permute-start(bf16[80,512]{1,0:T(8,128)(2,1)S(1)} %pad.9), channel_id=1, source_target_pairs={{0,8},{2,10},{4,12},{6,14},{8,0},{10,2},{12,4},{14,6},{1,9},{3,11}... | collective-permute-start | bytes 245768 | tf_op jit(solution)/shard_map/ppermute | solution.py:289
  19.9 2.8 %collective-permute-start.4 = (bf16[80,512]{1,0:T(8,128)(2,1)S(1)}, bf16[80,512]{1,0:T(8,128)(2,1)S(1)}, u32[]{:S(2)}, u32[]{:S(2)}) collective-permute-start(bf16[80,512]{1,0:T(8,128)(2,1)S(1)} %pad.9), channel_id=1, source_target_pairs={{0,4},{2,6},{4,8},{6,10},{8,12},{10,14},{12,0},{14,2},{1,5},{3,7},... | collective-permute-start | bytes 245768 | tf_op jit(solution)/shard_map/ppermute | solution.py:289
  22.7 1.6 collective-permute-done.1
  25.1 6.2 %collective-permute-done.3 = bf16[80,512]{1,0:T(8,128)(2,1)S(1)} collective-permute-done((bf16[80,512]{1,0:T(8,128)(2,1)S(1)}, bf16[80,512]{1,0:T(8,128)(2,1)S(1)}, u32[]{:S(2)}, u32[]{:S(2)}) %collective-permute-start.3) | collective-permute-done | bytes 81952 | tf_op jit(solution)/shard_map/ppermute | solution.py:289
  32.7 1.4 pad_maximum_fusion
  34.1 6.9 %all-to-all-start = ((bf16[16,112,512]{2,1,0:T(8,128)(2,1)}), bf16[16,112,512]{2,1,0:T(8,128)(2,1)S(1)}, u32[]{:S(2)}, u32[]{:S(2)}) async-start(bf16[16,112,512]{2,1,0:T(8,128)(2,1)} %pad_maximum_fusion), calls=%async_computation | async-start | bytes 3670016 | tf_op jit(solution)/shard_map/all_to_all | solution.py:299
  41.4 23.4 %all_gather.12.own_ref = bf16[640,640]{1,0:T(8,128)(2,1)S(1)} all-gather(bf16[80,640]{1,0:T(8,128)(2,1)S(1)} %reshape.57), channel_id=1, replica_groups=mesh['x'=4,'y'=4,'z'=8,'c'=2] {'z'}, dimensions={0}, use_global_device_ids=true | all-gather | bytes 921600 | tf_op jit(solution)/shard_map/all_gather | solution.py:300
  64.8 6.8 %collective-permute-start.5 = (bf16[640,640]{1,0:T(8,128)(2,1)S(1)}, bf16[640,640]{1,0:T(8,128)(2,1)S(1)}, u32[]{:S(2)}, u32[]{:S(2)}) collective-permute-start(bf16[640,640]{1,0:T(8,128)(2,1)S(1)} %all_gather.12.own_ref), channel_id=1, source_target_pairs={{0,1},{1,0},{2,3},{3,2},{4,5},{5,4},{6,7},{7,6},{8,9},{9,8},{10,11... | collective-permute-start | bytes 2457608 | tf_op jit(solution)/shard_map/ppermute | solution.py:31
  73.0 1.4 collective-permute-start.8
  75.9 4.6 %half.1 = bf16[16,80,256]{2,1,0:T(8,128)(2,1)} custom-call(s32[3]{0:T(128)} %pad_add_fusion.core_ref.place_ref, bf16[640,640]{1,0:T(8,128)(2,1)} %copy-done.4, bf16[640,640]{1,0:T(8,128)(2,1)} %copy-done.6, bf16[8,2,112,512]{3,2,1,0:T(8,128)(2,1)} %bitcast.27), custom_call_target="tpu_custom_call" | custom-call | tf_op jit(solution)/shard_map/half/pallas_call | solution.py:63
  80.5 25.8 %all_to_all.25 = bf16[16,80,256]{2,1,0:T(8,128)(2,1)S(1)} all-to-all(bf16[16,80,256]{2,1,0:T(8,128)(2,1)} %half.1), channel_id=1, replica_groups=mesh['x'=4,'y'=4,'z'=8,'c'=2] {'x','y'}, dimensions={0} | all-to-all | bytes 1310720 | tf_op jit(solution)/shard_map/all_to_all | solution.py:308
  106.3 3.0 %collective-permute-start.6 = (bf16[1280,256]{1,0:T(8,128)(2,1)S(1)}, bf16[1280,256]{1,0:T(8,128)(2,1)S(1)}, u32[]{:S(2)}, u32[]{:S(2)}) collective-permute-start(bf16[1280,256]{1,0:T(8,128)(2,1)S(1)} %bitcast.35), channel_id=1, source_target_pairs={{0,1},{1,0},{2,3},{3,2},{4,5},{5,4},{6,7},{7,6},{8,9},{9,8},{10,11... | collective-permute-start | bytes 1966088 | tf_op jit(solution)/shard_map/ppermute | solution.py:31
  112.4 8.3 %all-gather.3.cloned.1.call-done = bf16[80,80,512]{2,1,0:T(8,128)(2,1)} async-done(((bf16[5,80,512]{2,1,0:T(8,128)(2,1)}), bf16[80,80,512]{2,1,0:T(8,128)(2,1)}) %all-gather.3.cloned.1.call-update) | async-done | bytes 6553616 | tf_op jit(solution)/shard_map/all_gather | solution.py:292
  120.7 20.4 %ladder_core.1 = (f32[1280,256]{1,0:T(8,128)}, bf16[1280,256]{1,0:T(8,128)(2,1)}) custom-call(s32[3]{0:T(128)} %pad_add_fusion.core_ref.place_ref, bf16[1280,256]{1,0:T(8,128)(2,1)} %bitcast.36, bf16[1280,256]{1,0:T(8,128)(2,1)} %copy-done.13, bf16[16,112,512]{2,1,0:T(8,128)(2,1)} %copy-done, bf16[16,80,512]{2,1,0:T(8,128)(2,1)} %collective-permute-done.7.xu_ref, ...), custom_call_target="tpu_custom_call" | custom-call | flops 10737418240 | bytes 14000000 | tf_op jit(solution)/shard_map/ladder_core/pallas_call | solution.py:139
  142.0 1.9 collective-permute-done.10
  143.9 2.5 add_convert_fusion.1
  146.4 5.0 %all-to-all-start.2 = ((bf16[16,80,256]{2,1,0:T(8,128)(2,1)}), bf16[16,80,256]{2,1,0:T(8,128)(2,1)}, u32[]{:S(2)}, u32[]{:S(2)}) async-start(bf16[16,80,256]{2,1,0:T(8,128)(2,1)} %bitcast.15), calls=%async_computation.2 | async-start | bytes 1310720 | tf_op jit(solution)/shard_map/all_to_all | solution.py:317
  152.8 10.1 %all-to-all-done.2.b_ref = bf16[16,80,256]{2,1,0:T(8,128)(2,1)} async-done(((bf16[16,80,256]{2,1,0:T(8,128)(2,1)}), bf16[16,80,256]{2,1,0:T(8,128)(2,1)}, u32[]{:S(2)}, u32[]{:S(2)}) %all-to-all-start.2) | async-done | bytes 655392 | tf_op jit(solution)/shard_map/all_to_all | solution.py:317
  162.9 4.4 %ladder_rank.1 = (f32[320,1200]{1,0:T(8,128)}, bf16[320,1200]{1,0:T(8,128)(2,1)}) custom-call(s32[3]{0:T(128)} %pad_add_fusion.core_ref.place_ref, bf16[16,80,256]{2,1,0:T(8,128)(2,1)} %all-to-all-done.2.b_ref, bf16[1200,512]{1,0:T(8,128)(2,1)} %reshape.62.x_ref), custom_call_target="tpu_custom_call" | custom-call | tf_op jit(solution)/shard_map/ladder_rank/pallas_call | solution.py:199
  167.3 2.4 collective-permute-start.11
  169.7 2.2 collective-permute-done.11
  171.9 2.5 add_convert_fusion
  174.4 6.9 %all-to-all-start.3 = ((bf16[8,40,1200]{2,1,0:T(8,128)(2,1)}), bf16[8,40,1200]{2,1,0:T(8,128)(2,1)S(1)}, u32[]{:S(2)}, u32[]{:S(2)}) async-start(bf16[8,40,1200]{2,1,0:T(8,128)(2,1)} %bitcast.16), calls=%async_computation.3 | async-start | bytes 1638400 | tf_op jit(solution)/shard_map/all_to_all | solution.py:323
  182.9 22.7 %all-to-all-done.3.parts_ref = bf16[8,40,1200]{2,1,0:T(8,128)(2,1)S(1)} async-done(((bf16[8,40,1200]{2,1,0:T(8,128)(2,1)}), bf16[8,40,1200]{2,1,0:T(8,128)(2,1)S(1)}, u32[]{:S(2)}, u32[]{:S(2)}) %all-to-all-start.3) | async-done | bytes 768032 | tf_op jit(solution)/shard_map/all_to_all | solution.py:323
  206.4 2.8 %chunk.1 = bf16[40,1280]{1,0:T(8,128)(2,1)} custom-call(s32[3]{0:T(128)} %pad_add_fusion.core_ref.place_ref, bf16[8,40,1200]{2,1,0:T(8,128)(2,1)} %copy-done.3, f32[75,8,1200]{2,1,0:T(8,128)} %bitcast.30, f32[1,1200]{1,0:T(1,128)} %broadcast_in_dim.7.col_ref, f32[600,1]{1,0:T(8,128)} %sub.31.low_ref), custom_call_target="tpu_custom_call" | custom-call | tf_op jit(solution)/shard_map/chunk/pallas_call | solution.py:237
  209.2 20.6 %all_gather.15.own_ref = bf16[320,1280]{1,0:T(8,128)(2,1)S(1)} all-gather(bf16[40,1280]{1,0:T(8,128)(2,1)} %chunk.1), channel_id=1, replica_groups=mesh['x'=4,'y'=4,'z'=8,'c'=2] {'z'}, dimensions={0}, use_global_device_ids=true | all-gather | bytes 921600 | tf_op jit(solution)/shard_map/all_gather | solution.py:330
  229.8 6.3 %collective-permute-start.12 = (bf16[320,1280]{1,0:T(8,128)(2,1)S(1)}, bf16[320,1280]{1,0:T(8,128)(2,1)S(1)}, u32[]{:S(2)}, u32[]{:S(2)}) collective-permute-start(bf16[320,1280]{1,0:T(8,128)(2,1)S(1)} %all_gather.15.own_ref), channel_id=1, source_target_pairs={{0,1},{1,0},{2,3},{3,2},{4,5},{5,4},{6,7},{7,6},{8,9},{9,8},{10,11... | collective-permute-start | bytes 2457608 | tf_op jit(solution)/shard_map/ppermute | solution.py:31
  236.1 2.0 collective-permute-done.12.oth_ref
  241.0 3.5 %all-to-all-start.4 = ((f32[16,8,128]{2,1,0:T(8,128)}), f32[16,8,128]{2,1,0:T(8,128)S(1)}, u32[]{:S(2)}, u32[]{:S(2)}) async-start(f32[16,8,128]{2,1,0:T(8,128)} %broadcast_in_dim.16), calls=%async_computation.4 | async-start | bytes 131072 | tf_op jit(solution)/shard_map/all_to_all | solution.py:336
  244.5 4.3 %residual.1 = f32[75,8,1200]{2,1,0:T(8,128)} custom-call(s32[3]{0:T(128)} %pad_add_fusion.core_ref.place_ref, bf16[320,1280]{1,0:T(8,128)(2,1)} %copy-done.2, bf16[320,1280]{1,0:T(8,128)(2,1)} %copy-done.5, f32[75,8,1200]{2,1,0:T(8,128)} %bitcast.31), custom_call_target="tpu_custom_call" | custom-call | tf_op jit(solution)/shard_map/residual/pallas_call | solution.py:273
  248.8 2.2 all-to-all-done.4
  (71 shorter events, 18.4 us)
Async XLA Ops:
  7.2 25.2 %copy-start.9 = (bf16[512,512]{1,0:T(8,128)(2,1)S(1)}, bf16[512,512]{1,0:T(8,128)(2,1)}, u32[]{:S(2)}) copy-start(bf16[512,512]{1,0:T(8,128)(2,1)} %param.8) | copy-start | bytes 1572868
  7.2 113.6 %all-gather.3.cloned.1.call-start = ((), (), s32[]{:S(2)}) async-start(), calls=%async_computation.5 | async-start | bytes 6963200 | tf_op jit(solution)/shard_map/all_gather | solution.py:292
  8.2 14.6 %collective-permute-start = (bf16[80,512]{1,0:T(8,128)(2,1)S(1)}, bf16[80,512]{1,0:T(8,128)(2,1)S(1)}, u32[]{:S(2)}, u32[]{:S(2)}) collective-permute-start(bf16[80,512]{1,0:T(8,128)(2,1)S(1)} %pad.9), channel_id=1, source_target_pairs={{0,12},{2,14},{4,0},{6,2},{8,4},{10,6},{12,8},{14,10},{1,13},{3,15... | collective-permute-start | bytes 245768 | tf_op jit(solution)/shard_map/ppermute | solution.py:289
  15.0 9.3 %collective-permute-start.1 = (bf16[80,512]{1,0:T(8,128)(2,1)S(1)}, bf16[80,512]{1,0:T(8,128)(2,1)S(1)}, u32[]{:S(2)}, u32[]{:S(2)}) collective-permute-start(bf16[80,512]{1,0:T(8,128)(2,1)S(1)} %pad.9), channel_id=1, source_target_pairs={{0,10},{2,12},{4,14},{6,0},{8,2},{10,4},{12,6},{14,8},{1,11},{3,13... | collective-permute-start | bytes 245768 | tf_op jit(solution)/shard_map/ppermute | solution.py:289
  15.7 9.4 %collective-permute-start.2 = (bf16[80,512]{1,0:T(8,128)(2,1)S(1)}, bf16[80,512]{1,0:T(8,128)(2,1)S(1)}, u32[]{:S(2)}, u32[]{:S(2)}) collective-permute-start(bf16[80,512]{1,0:T(8,128)(2,1)S(1)} %pad.9), channel_id=1, source_target_pairs={{0,8},{2,10},{4,12},{6,14},{8,0},{10,2},{12,4},{14,6},{1,9},{3,11}... | collective-permute-start | bytes 245768 | tf_op jit(solution)/shard_map/ppermute | solution.py:289
  19.9 11.4 %collective-permute-start.3 = (bf16[80,512]{1,0:T(8,128)(2,1)S(1)}, bf16[80,512]{1,0:T(8,128)(2,1)S(1)}, u32[]{:S(2)}, u32[]{:S(2)}) collective-permute-start(bf16[80,512]{1,0:T(8,128)(2,1)S(1)} %pad.9), channel_id=1, source_target_pairs={{0,6},{2,8},{4,10},{6,12},{8,14},{10,0},{12,2},{14,4},{1,7},{3,9},... | collective-permute-start | bytes 245768 | tf_op jit(solution)/shard_map/ppermute | solution.py:289
  19.9 11.6 %collective-permute-start.4 = (bf16[80,512]{1,0:T(8,128)(2,1)S(1)}, bf16[80,512]{1,0:T(8,128)(2,1)S(1)}, u32[]{:S(2)}, u32[]{:S(2)}) collective-permute-start(bf16[80,512]{1,0:T(8,128)(2,1)S(1)} %pad.9), channel_id=1, source_target_pairs={{0,4},{2,6},{4,8},{6,10},{8,12},{10,14},{12,0},{14,2},{1,5},{3,7},... | collective-permute-start | bytes 245768 | tf_op jit(solution)/shard_map/ppermute | solution.py:289
  34.1 6.9 %copy-start.10 = (bf16[8,75,75]{2,0,1:T(8,128)(2,1)S(1)}, bf16[8,75,75]{2,0,1:T(8,128)(2,1)}, u32[]{:S(2)}) copy-start(bf16[8,75,75]{2,0,1:T(8,128)(2,1)} %param.6) | copy-start | bytes 270004
  34.1 37.5 %all-to-all-start = ((bf16[16,112,512]{2,1,0:T(8,128)(2,1)}), bf16[16,112,512]{2,1,0:T(8,128)(2,1)S(1)}, u32[]{:S(2)}, u32[]{:S(2)}) async-start(bf16[16,112,512]{2,1,0:T(8,128)(2,1)} %pad_maximum_fusion), calls=%async_computation | async-start | bytes 3670016 | tf_op jit(solution)/shard_map/all_to_all | solution.py:299
  64.8 10.2 %copy-start.4 = (bf16[640,640]{1,0:T(8,128)(2,1)}, bf16[640,640]{1,0:T(8,128)(2,1)S(1)}, u32[]{:S(2)}) copy-start(bf16[640,640]{1,0:T(8,128)(2,1)S(1)} %all_gather.12.own_ref) | copy-start | bytes 2457604
  64.8 10.2 %collective-permute-start.5 = (bf16[640,640]{1,0:T(8,128)(2,1)S(1)}, bf16[640,640]{1,0:T(8,128)(2,1)S(1)}, u32[]{:S(2)}, u32[]{:S(2)}) collective-permute-start(bf16[640,640]{1,0:T(8,128)(2,1)S(1)} %all_gather.12.own_ref), channel_id=1, source_target_pairs={{0,1},{1,0},{2,3},{3,2},{4,5},{5,4},{6,7},{7,6},{8,9},{9,8},{10,11... | collective-permute-start | bytes 2457608 | tf_op jit(solution)/shard_map/ppermute | solution.py:31
  71.6 3.3 %copy-start = (bf16[16,112,512]{2,1,0:T(8,128)(2,1)}, bf16[16,112,512]{2,1,0:T(8,128)(2,1)S(1)}, u32[]{:S(2)}) copy-start(bf16[16,112,512]{2,1,0:T(8,128)(2,1)S(1)} %all-to-all-done.xq_ref) | copy-start | bytes 5505028
  72.9 39.5 %collective-permute-start.7 = (bf16[16,80,512]{2,1,0:T(8,128)(2,1)}, bf16[16,80,512]{2,1,0:T(8,128)(2,1)}, u32[]{:S(2)}, u32[]{:S(2)}) collective-permute-start(bf16[16,80,512]{2,1,0:T(8,128)(2,1)} %slice.20), channel_id=1, source_target_pairs={{0,14},{2,0},{4,2},{6,4},{8,6},{10,8},{12,10},{14,12},{1,15},{3,1}... | collective-permute-start | bytes 3932168 | tf_op jit(solution)/shard_map/ppermute | solution.py:303
  73.0 39.4 %collective-permute-start.8 = (bf16[16,80,512]{2,1,0:T(8,128)(2,1)}, bf16[16,80,512]{2,1,0:T(8,128)(2,1)}, u32[]{:S(2)}, u32[]{:S(2)}) collective-permute-start(bf16[16,80,512]{2,1,0:T(8,128)(2,1)} %slice.20), channel_id=1, source_target_pairs={{0,2},{2,4},{4,6},{6,8},{8,10},{10,12},{12,14},{14,0},{1,3},{3,5},... | collective-permute-start | bytes 3932168 | tf_op jit(solution)/shard_map/ppermute | solution.py:304
  75.0 0.9 copy-start.6
  106.3 14.4 %copy-start.7 = (bf16[16,80,256]{2,1,0:T(8,128)(2,1)}, bf16[16,80,256]{2,1,0:T(8,128)(2,1)S(1)}, u32[]{:S(2)}) copy-start(bf16[16,80,256]{2,1,0:T(8,128)(2,1)S(1)} %all_to_all.25) | copy-start | bytes 1966084
  106.3 6.1 %collective-permute-start.6 = (bf16[1280,256]{1,0:T(8,128)(2,1)S(1)}, bf16[1280,256]{1,0:T(8,128)(2,1)S(1)}, u32[]{:S(2)}, u32[]{:S(2)}) collective-permute-start(bf16[1280,256]{1,0:T(8,128)(2,1)S(1)} %bitcast.35), channel_id=1, source_target_pairs={{0,1},{1,0},{2,3},{3,2},{4,5},{5,4},{6,7},{7,6},{8,9},{9,8},{10,11... | collective-permute-start | bytes 1966088 | tf_op jit(solution)/shard_map/ppermute | solution.py:31
  110.6 1.8 collective-permute-start.9
  112.4 8.3 %copy-start.14 = (bf16[8,32,512]{2,1,0:T(8,128)(2,1)}, bf16[8,32,512]{2,1,0:T(8,128)(2,1)S(1)}, u32[]{:S(2)}) copy-start(bf16[8,32,512]{2,1,0:T(8,128)(2,1)S(1)} %collective-permute-done.9.zx_ref) | copy-start | bytes 786436
  112.4 8.3 %copy-start.13 = (bf16[1280,256]{1,0:T(8,128)(2,1)}, bf16[1280,256]{1,0:T(8,128)(2,1)S(1)}, u32[]{:S(2)}) copy-start(bf16[1280,256]{1,0:T(8,128)(2,1)S(1)} %collective-permute-done.6.hx_ref) | copy-start | bytes 1966084
  141.2 2.8 %collective-permute-start.10 = (bf16[1280,256]{1,0:T(8,128)(2,1)}, bf16[1280,256]{1,0:T(8,128)(2,1)S(1)}, u32[]{:S(2)}, u32[]{:S(2)}) collective-permute-start(bf16[1280,256]{1,0:T(8,128)(2,1)} %get-tuple-element.9), channel_id=1, source_target_pairs={{0,1},{1,0},{2,3},{3,2},{4,5},{5,4},{6,7},{7,6},{8,9},{9,8},{10,11... | collective-permute-start | bytes 1966088 | tf_op jit(solution)/shard_map/ppermute | solution.py:31
  143.9 7.5 %copy-start.1 = (bf16[16,112,512]{2,1,0:T(8,128)(2,1)S(1)}, bf16[16,112,512]{2,1,0:T(8,128)(2,1)}, u32[]{:S(2)}) copy-start(bf16[16,112,512]{2,1,0:T(8,128)(2,1)} %copy-done) | copy-start | bytes 5505028
  146.4 16.5 %all-to-all-start.2 = ((bf16[16,80,256]{2,1,0:T(8,128)(2,1)}), bf16[16,80,256]{2,1,0:T(8,128)(2,1)}, u32[]{:S(2)}, u32[]{:S(2)}) async-start(bf16[16,80,256]{2,1,0:T(8,128)(2,1)} %bitcast.15), calls=%async_computation.2 | async-start | bytes 1310720 | tf_op jit(solution)/shard_map/all_to_all | solution.py:317
  167.3 4.6 %collective-permute-start.11 = (bf16[320,1200]{1,0:T(8,128)(2,1)}, bf16[320,1200]{1,0:T(8,128)(2,1)S(1)}, u32[]{:S(2)}, u32[]{:S(2)}) collective-permute-start(bf16[320,1200]{1,0:T(8,128)(2,1)} %get-tuple-element.11), channel_id=1, source_target_pairs={{0,1},{1,0},{2,3},{3,2},{4,5},{5,4},{6,7},{7,6},{8,9},{9,8},{10,11... | collective-permute-start | bytes 2304008 | tf_op jit(solution)/shard_map/ppermute | solution.py:31
  174.4 6.9 %copy-start.11 = (f32[1200]{0:T(1024)S(1)}, f32[1200]{0:T(1024)}, u32[]{:S(2)}) copy-start(f32[1200]{0:T(1024)} %param.10) | copy-start | bytes 14404
  174.4 7.5 %copy-start.12 = (f32[8]{0:T(128)S(1)}, f32[8]{0:T(128)}, u32[]{:S(2)}) copy-start(f32[8]{0:T(128)} %param.11) | copy-start | bytes 100
  174.4 31.1 %all-to-all-start.3 = ((bf16[8,40,1200]{2,1,0:T(8,128)(2,1)}), bf16[8,40,1200]{2,1,0:T(8,128)(2,1)S(1)}, u32[]{:S(2)}, u32[]{:S(2)}) async-start(bf16[8,40,1200]{2,1,0:T(8,128)(2,1)} %bitcast.16), calls=%async_computation.3 | async-start | bytes 1638400 | tf_op jit(solution)/shard_map/all_to_all | solution.py:323
  205.5 0.9 copy-start.3
  229.8 8.4 %copy-start.2 = (bf16[320,1280]{1,0:T(8,128)(2,1)}, bf16[320,1280]{1,0:T(8,128)(2,1)S(1)}, u32[]{:S(2)}) copy-start(bf16[320,1280]{1,0:T(8,128)(2,1)S(1)} %all_gather.15.own_ref) | copy-start | bytes 2457604
  229.8 8.3 %collective-permute-start.12 = (bf16[320,1280]{1,0:T(8,128)(2,1)S(1)}, bf16[320,1280]{1,0:T(8,128)(2,1)S(1)}, u32[]{:S(2)}, u32[]{:S(2)}) collective-permute-start(bf16[320,1280]{1,0:T(8,128)(2,1)S(1)} %all_gather.15.own_ref), channel_id=1, source_target_pairs={{0,1},{1,0},{2,3},{3,2},{4,5},{5,4},{6,7},{7,6},{8,9},{9,8},{10,11... | collective-permute-start | bytes 2457608 | tf_op jit(solution)/shard_map/ppermute | solution.py:31
  238.1 0.9 copy-start.5
  241.0 10.0 %all-to-all-start.4 = ((f32[16,8,128]{2,1,0:T(8,128)}), f32[16,8,128]{2,1,0:T(8,128)S(1)}, u32[]{:S(2)}, u32[]{:S(2)}) async-start(f32[16,8,128]{2,1,0:T(8,128)} %broadcast_in_dim.16), calls=%async_computation.4 | async-start | bytes 131072 | tf_op jit(solution)/shard_map/all_to_all | solution.py:336
  (1 other events, 0.8 us)
Sparse Core Ops, SparseCore 0:
  32.5 88.1 all-gather.2

commit v4 on v2

--- a/solution.py
+++ b/solution.py
@@ -29,6 +29,10 @@
 
 def core_swap(value):
     return lax.ppermute(value, "c", [(0, 1), (1, 0)])
+
+
+def ring(shift):
+    return [(s, (s + shift) % NZ) for s in range(NZ)]
 
 
 def regroup(tiles, want):
@@ -70,74 +74,142 @@
     )(place, t_own, t_oth, xz)
 
 
-def main_kernel(
-    place_ref, ho_ref, hx_ref, xq_ref, x_ref, zo_ref, zx_ref, bo_ref, bx_ref, h_ref, acc_ref
+FIRST = (0, 1, NZ - 1, 3, 4, 5)
+LAST = (2, NZ - 2)
+HALF_M = PAIRS * QC
+
+
+def back_block(h, x, z_own, z_oth):
+    coupled = jnp.dot(h, x, preferred_element_type=F32)
+    z_own = z_own.reshape(1, QC, BLK).astype(F32)
+    z_oth = z_oth.reshape(1, QC, BLK).astype(F32)
+    c_own = coupled[:HALF_M].reshape(PAIRS, QC, BLK) * z_own
+    c_oth = coupled[HALF_M:].reshape(PAIRS, QC, BLK) * z_oth
+    w = jnp.concatenate(
+        [c_own.reshape(HALF_M, BLK), c_oth.reshape(HALF_M, BLK)], axis=0
+    ).astype(BF)
+    return lax.dot_general(x, w, (((1,), (1,)), ((), ())), preferred_element_type=F32)
+
+
+def first_kernel(
+    place_ref, ho_ref, hx_ref, xq_ref, xu_ref, xd_ref, x_ref, zo_ref, zx_ref, acc_ref, h_ref, now_ref
 ):
     step = pl.program_id(0)
-    half_m = PAIRS * QC
-
-    def block(x):
-        coupled = jnp.dot(h_ref[...], x, preferred_element_type=F32)
-        z_own = zo_ref[0, 0, PAD:, :].reshape(1, QC, BLK).astype(F32)
-        z_oth = zx_ref[...].reshape(1, QC, BLK).astype(F32)
-        c_own = coupled[:half_m].reshape(PAIRS, QC, BLK) * z_own
-        c_oth = coupled[half_m:].reshape(PAIRS, QC, BLK) * z_oth
-        w = jnp.concatenate(
-            [c_own.reshape(half_m, BLK), c_oth.reshape(half_m, BLK)], axis=0
-        ).astype(BF)
-        return lax.dot_general(x, w, (((1,), (1,)), ((), ())), preferred_element_type=F32)
 
     @pl.when(step == 0)
     def _():
-        h_ref[pl.ds(0, half_m), :] = ho_ref[...].astype(F32).T.astype(BF)
-        h_ref[pl.ds(half_m, half_m), :] = hx_ref[...].astype(F32).T.astype(BF)
-        acc_ref[...] = block(xq_ref[:, :PAD, :].reshape(NV * PAD, BLK))
-
-    @pl.when(step > 0)
-    def _():
-        acc_ref[...] += block(x_ref[...].reshape(NV * PAD, BLK))
-
-    @pl.when(step == NZ - 1)
-    def _():
-        bo_ref[...] = acc_ref[:, :half_m]
-        bx_ref[...] = acc_ref[:, half_m:].astype(BF)
-
-
-def make_main(place, h_own, h_oth, xz, x_all, z_oth):
+        h_ref[pl.ds(0, HALF_M), :] = ho_ref[...].astype(F32).T.astype(BF)
+        h_ref[pl.ds(HALF_M, HALF_M), :] = hx_ref[...].astype(F32).T.astype(BF)
+        acc_ref[...] = jnp.zeros_like(acc_ref)
+        now_ref[...] = xq_ref[:, :PAD, :].reshape(NV * PAD, BLK)
+
+    @pl.when(step == 1)
+    def _():
+        now_ref[...] = xu_ref[...].reshape(NV * PAD, BLK)
+
+    @pl.when(step == 2)
+    def _():
+        now_ref[...] = xd_ref[...].reshape(NV * PAD, BLK)
+
+    @pl.when(step > 2)
+    def _():
+        now_ref[...] = x_ref[...].reshape(NV * PAD, BLK)
+
+    acc_ref[...] += back_block(h_ref[...], now_ref[...], zo_ref[0, 0, PAD:, :], zx_ref[...])
+
+
+def first_level(step, place):
+    far = jnp.where(step == 2, NZ - 1, step)
+    return (place[1] + far) % NZ
+
+
+def make_first(place, h_own, h_oth, xz, x_up, x_down, x_all, z_oth):
     rows = NV * PAD
-    half_m = PAIRS * QC
-    return pl.pallas_call(
-        main_kernel,
+    whole = pl.BlockSpec((NV, PAD, BLK), lambda k, p: (0, 0, 0))
+    return pl.pallas_call(
+        first_kernel,
         out_shape=(
-            jax.ShapeDtypeStruct((rows, half_m), F32),
-            jax.ShapeDtypeStruct((rows, half_m), BF),
+            jax.ShapeDtypeStruct((rows, 2 * HALF_M), F32),
+            jax.ShapeDtypeStruct((2 * HALF_M, rows), BF),
         ),
         grid_spec=pltpu.PrefetchScalarGridSpec(
             num_scalar_prefetch=1,
-            grid=(NZ,),
+            grid=(len(FIRST),),
             in_specs=[
-                pl.BlockSpec((rows, half_m), lambda k, p: (0, 0)),
-                pl.BlockSpec((rows, half_m), lambda k, p: (0, 0)),
+                pl.BlockSpec((rows, HALF_M), lambda k, p: (0, 0)),
+                pl.BlockSpec((rows, HALF_M), lambda k, p: (0, 0)),
                 pl.BlockSpec((NV, PAD + QC, BLK), lambda k, p: (0, 0, 0)),
-                pl.BlockSpec((NV, 1, PAD, BLK), lambda k, p: (0, jnp.maximum(k - 1, 0), 0, 0)),
-                pl.BlockSpec((1, 1, PAD + QC, BLK), lambda k, p: ((p[1] + k) % NZ, p[0], 0, 0)),
-                pl.BlockSpec((1, QC, BLK), lambda k, p: ((p[1] + k) % NZ, 0, 0)),
+                whole,
+                whole,
+                pl.BlockSpec((NV, 1, PAD, BLK), lambda k, p: (0, jnp.maximum(k - 3, 0), 0, 0)),
+                pl.BlockSpec((1, 1, PAD + QC, BLK), lambda k, p: (first_level(k, p), p[0], 0, 0)),
+                pl.BlockSpec((1, QC, BLK), lambda k, p: (first_level(k, p), 0, 0)),
             ],
             out_specs=(
-                pl.BlockSpec((rows, half_m), lambda k, p: (0, 0)),
-                pl.BlockSpec((rows, half_m), lambda k, p: (0, 0)),
+                pl.BlockSpec((rows, 2 * HALF_M), lambda k, p: (0, 0)),
+                pl.BlockSpec((2 * HALF_M, rows), lambda k, p: (0, 0)),
             ),
-            scratch_shapes=[
-                pltpu.VMEM((2 * half_m, rows), BF),
-                pltpu.VMEM((rows, 2 * half_m), F32),
-            ],
+            scratch_shapes=[pltpu.VMEM((rows, BLK), BF)],
         ),
         compiler_params=pltpu.CompilerParams(dimension_semantics=("arbitrary",)),
         cost_estimate=pl.CostEstimate(
-            flops=4 * 512 * 1280 * 4096, bytes_accessed=14_000_000, transcendentals=0
-        ),
-        name="ladder_core",
-    )(place, h_own, h_oth, xz, x_all, xz.reshape(NZ, NC, PAD + QC, BLK), z_oth)
+            flops=4 * 512 * 1280 * 512 * len(FIRST), bytes_accessed=12_000_000, transcendentals=0
+        ),
+        name="core_first",
+    )(place, h_own, h_oth, xz, x_up, x_down, x_all, xz.reshape(NZ, NC, PAD + QC, BLK), z_oth)
+
+
+def last_kernel(
+    place_ref, acc_ref, h_ref, xu_ref, xd_ref, zou_ref, zxu_ref, zod_ref, zxd_ref, bo_ref, bx_ref
+):
+    h = h_ref[...]
+    up = xu_ref[...].reshape(NV * PAD, BLK)
+    down = xd_ref[...].reshape(NV * PAD, BLK)
+    total = acc_ref[...] + back_block(h, up, zou_ref[0, 0, PAD:, :], zxu_ref[...])
+    total += back_block(h, down, zod_ref[0, 0, PAD:, :], zxd_ref[...])
+    bo_ref[...] = total[:, :HALF_M]
+    bx_ref[...] = total[:, HALF_M:].astype(BF)
+
+
+def make_last(place, acc, h, x_up, x_down, xz, z_oth):
+    rows = NV * PAD
+    whole = pl.BlockSpec((NV, PAD, BLK), lambda k, p: (0, 0, 0))
+
+    def z_specs(far):
+        return [
+            pl.BlockSpec((1, 1, PAD + QC, BLK), lambda k, p: ((p[1] + far) % NZ, p[0], 0, 0)),
+            pl.BlockSpec((1, QC, BLK), lambda k, p: ((p[1] + far) % NZ, 0, 0)),
+        ]
+
+    z_all = xz.reshape(NZ, NC, PAD + QC, BLK)
+    return pl.pallas_call(
+        last_kernel,
+        out_shape=(
+            jax.ShapeDtypeStruct((rows, HALF_M), F32),
+            jax.ShapeDtypeStruct((rows, HALF_M), BF),
+        ),
+        grid_spec=pltpu.PrefetchScalarGridSpec(
+            num_scalar_prefetch=1,
+            grid=(1,),
+            in_specs=[
+                pl.BlockSpec((rows, 2 * HALF_M), lambda k, p: (0, 0)),
+                pl.BlockSpec((2 * HALF_M, rows), lambda k, p: (0, 0)),
+                whole,
+                whole,
+            ]
+            + z_specs(LAST[0])
+            + z_specs(LAST[1]),
+            out_specs=(
+                pl.BlockSpec((rows, HALF_M), lambda k, p: (0, 0)),
+                pl.BlockSpec((rows, HALF_M), lambda k, p: (0, 0)),
+            ),
+        ),
+        compiler_params=pltpu.CompilerParams(dimension_semantics=("arbitrary",)),
+        cost_estimate=pl.CostEstimate(
+            flops=4 * 512 * 1280 * 512 * len(LAST), bytes_accessed=8_000_000, transcendentals=0
+        ),
+        name="core_last",
+    )(place, acc, h, x_up, x_down, z_all, z_oth, z_all, z_oth)
 
 
 def ladder_kernel(place_ref, b_ref, x_ref, own_ref, oth_ref, g_ref):
@@ -252,31 +324,40 @@
     place = jnp.stack([core, level, core * NZ + level])
 
     x_pad = jnp.pad(factors, ((0, PAD - ROW), (0, 0)))
-    x_far = [
-        lax.ppermute(x_pad, "z", [(s, (s - j) % NZ) for s in range(NZ)]) for j in range(1, NZ)
-    ]
-    x_far = jnp.stack(x_far)
-    x_all = lax.all_gather(x_far, XY, axis=0)
-
     z_cols = kernel.T.reshape(NV, QC, BLK)
     xz = jnp.concatenate([jnp.broadcast_to(x_pad[None], (NV, PAD, BLK)), z_cols], axis=1)
+    x_pad, xz = lax.optimization_barrier((x_pad, xz))
+    with jax.named_scope("own"):
+        xz = lax.all_to_all(xz, XY, split_axis=0, concat_axis=0, tiled=True)
+    with jax.named_scope("far"):
+        x_far = jnp.stack([lax.ppermute(x_pad, "z", ring(-j)) for j in FIRST[3:]])
+    x_all = lax.all_gather(x_far, XY, axis=0)
+
     t_cols = jnp.pad(amplitudes, ((0, 0), (0, PAD - ROW), (0, PAD - ROW)))
     t_cols = jnp.transpose(t_cols, (2, 0, 1)).reshape(PAD, PAIRS * PAD)
-    t_cols, xz, _ = lax.optimization_barrier((t_cols, xz, x_far))
-    xz = lax.all_to_all(xz, XY, split_axis=0, concat_axis=0, tiled=True)
+    t_cols, _ = lax.optimization_barrier((t_cols, x_far))
     t_own = lax.all_gather(t_cols, "z", axis=0, tiled=True)
     t_oth = core_swap(t_own)
+    x_own = xz[:, :PAD]
+    with jax.named_scope("near"):
+        x_up = lax.ppermute(x_own, "z", ring(-1))
+        x_down = lax.ppermute(x_own, "z", ring(1))
+    with jax.named_scope("next"):
+        x_up2 = lax.ppermute(x_up, "z", ring(-1))
+        x_down2 = lax.ppermute(x_down, "z", ring(1))
     x_rows = xz[:, :ROW].reshape(NVIR, BLK)
 
     h_msg = make_half(place, t_own, t_oth, xz.reshape(NZ, NC, PAD + QC, BLK))
-    h_own = lax.all_to_all(h_msg, XY, split_axis=0, concat_axis=0, tiled=True)
+    with jax.named_scope("spread"):
+        h_own = lax.all_to_all(h_msg, XY, split_axis=0, concat_axis=0, tiled=True)
     h_own = h_own.reshape(NV * PAD, PAIRS * QC)
     h_oth = core_swap(h_own)
     z_all = xz.reshape(NZ, NC, PAD + QC, BLK)
     z_oth = lax.dynamic_index_in_dim(z_all, 1 - core, 1, keepdims=False)[:, PAD:]
     z_oth = core_swap(z_oth)
 
-    b_own, b_send = make_main(place, h_own, h_oth, xz, x_all, z_oth)
+    acc, h = make_first(place, h_own, h_oth, xz, x_up, x_down, x_all, z_oth)
+    b_own, b_send = make_last(place, acc, h, x_up2, x_down2, xz, z_oth)
     b_sum = (b_own + core_swap(b_send).astype(F32)).astype(BF)
     b_all = lax.all_to_all(
         b_sum.reshape(NV, PAD, PAIRS * QC), XY, split_axis=0, concat_axis=0, tiled=True

time: 272 us -> 264 us (0.971)
  waiting for transfers between devices: 77.4 us -> 62 us
  Pallas kernels: 34.3 us -> 40.6 us
  starting transfers between devices: 55.5 us -> 50.7 us
    all_gather x1, waiting for transfers between devices: 21.6 us -> 0.01 us  [shards(): x_all = lax.all_gather(x_far, XY, axis=0)]
    ppermute x7, waiting for transfers between devices: 11.8 us -> 20 us  [the longest x3 9.11 us: shards(): x_far = jnp.stack([lax.ppermute(x_pad, 'z', ring(-j)) for j in FIRST[3:]])]
    pallas_call x1 -> x2, Pallas kernels: 18.3 us -> 24.6 us  [the longest x1 16.8 us: make_first(): pl.pallas_call(first_kernel, out_shape=(jax.ShapeDtypeStruct((rows, 2 * H...]
  transfers between devices with their start and end apart: 18 -> 18, of which waited for: 14 -> 11; matrix products, arithmetic and copies ran while one was open for 3% -> 2% of each run, Pallas kernels for 3% -> 10%
where the time goes in v4:
time: 264 us; the launch traced here: 263 us
  blocking collectives  70.8 us (27%)
  waiting for transfers between devices  62 us (23%)
  starting transfers between devices  50.7 us (19%)
  Pallas kernels  40.6 us (15%)
  between operations  16 us (6%)
  local copies, waits for them, and re-layouts  13.7 us (5%)
  other arithmetic  9.15 us (3%)
    all_to_all x1, blocking collectives, shards(): h_own = lax.all_to_all(h_msg, XY, split_axis=0, concat_axis=0, tiled=True)  26.5 us
    all_gather x1, blocking collectives, shards(): t_own = lax.all_gather(t_cols, 'z', axis=0, tiled=True)  23.6 us
    all_to_all x1, waiting for transfers between devices, shards(): lax.all_to_all(l_sum.reshape(NZ, CHUNK * PAIRS, NVIR), 'z', split_axis=0,...  22.6 us
    all_gather x1, blocking collectives, shards(): l_mine = lax.all_gather(chunk, 'z', axis=0, tiled=True)  20.7 us
    ppermute x6, starting transfers between devices, core_swap(): return lax.ppermute(value, 'c', [(0, 1), (1, 0)])  17 us
    pallas_call x1, Pallas kernels, make_first(): pl.pallas_call(first_kernel, out_shape=(jax.ShapeDtypeStruct((rows, 2 * H...  16.8 us
    ppermute x3, starting transfers between devices, shards(): x_far = jnp.stack([lax.ppermute(x_pad, 'z', ring(-j)) for j in FIRST[3:]])  11 us
    all_to_all x1, waiting for transfers between devices, shards(): lax.all_to_all(b_sum.reshape(NV, PAD, PAIRS * QC), XY, split_axis=0, conc...  9.95 us
  transfers between devices with their start and end apart: 18, of which 11 were waited for; matrix products, arithmetic and copies ran while one was open for 2% of the time, Pallas kernels for 10%

profile of v4, /device:TPU:1, one launch (start us, length us, event | category | flops | bytes accessed | tf_op | source)
XLA Modules:
  0.0 263.0 jit_solution(18420119875841071864)
XLA Ops:
  10.9 7.3 %collective-permute-start = (bf16[80,512]{1,0:T(8,128)(2,1)S(1)}, bf16[80,512]{1,0:T(8,128)(2,1)S(1)}, u32[]{:S(2)}, u32[]{:S(2)}) collective-permute-start(bf16[80,512]{1,0:T(8,128)(2,1)S(1)} %pad.9), channel_id=1, source_target_pairs={{0,10},{2,12},{4,14},{6,0},{8,2},{10,4},{12,6},{14,8},{1,11},{3,13... | collective-permute-start | bytes 245768 | tf_op jit(solution)/shard_map/far/ppermute | solution.py:333
  18.6 3.3 %collective-permute-start.2 = (bf16[80,512]{1,0:T(8,128)(2,1)S(1)}, bf16[80,512]{1,0:T(8,128)(2,1)S(1)}, u32[]{:S(2)}, u32[]{:S(2)}) collective-permute-start(bf16[80,512]{1,0:T(8,128)(2,1)S(1)} %pad.9), channel_id=1, source_target_pairs={{0,6},{2,8},{4,10},{6,12},{8,14},{10,0},{12,2},{14,4},{1,7},{3,9},... | collective-permute-start | bytes 245768 | tf_op jit(solution)/shard_map/far/ppermute | solution.py:333
  21.8 4.9 %collective-permute-done = bf16[80,512]{1,0:T(8,128)(2,1)S(1)} collective-permute-done((bf16[80,512]{1,0:T(8,128)(2,1)S(1)}, bf16[80,512]{1,0:T(8,128)(2,1)S(1)}, u32[]{:S(2)}, u32[]{:S(2)}) %collective-permute-start) | collective-permute-done | bytes 81952 | tf_op jit(solution)/shard_map/far/ppermute | solution.py:333
  26.7 4.2 %collective-permute-done.2 = bf16[80,512]{1,0:T(8,128)(2,1)S(1)} collective-permute-done((bf16[80,512]{1,0:T(8,128)(2,1)S(1)}, bf16[80,512]{1,0:T(8,128)(2,1)S(1)}, u32[]{:S(2)}, u32[]{:S(2)}) %collective-permute-start.2) | collective-permute-done | bytes 81952 | tf_op jit(solution)/shard_map/far/ppermute | solution.py:333
  31.7 6.9 %all-to-all-start = ((bf16[16,112,512]{2,1,0:T(8,128)(2,1)}), bf16[16,112,512]{2,1,0:T(8,128)(2,1)S(1)}, u32[]{:S(2)}, u32[]{:S(2)}) async-start(bf16[16,112,512]{2,1,0:T(8,128)(2,1)} %pad_maximum_fusion), calls=%async_computation | async-start | bytes 3670016 | tf_op jit(solution)/shard_map/own/all_to_all | solution.py:331
  39.0 23.6 %all_gather.12.own_ref = bf16[640,640]{1,0:T(8,128)(2,1)S(1)} all-gather(bf16[80,640]{1,0:T(8,128)(2,1)S(1)} %reshape.58), channel_id=1, replica_groups=mesh['x'=4,'y'=4,'z'=8,'c'=2] {'z'}, dimensions={0}, use_global_device_ids=true | all-gather | bytes 921600 | tf_op jit(solution)/shard_map/all_gather | solution.py:339
  62.7 4.8 %collective-permute-start.3 = (bf16[640,640]{1,0:T(8,128)(2,1)S(1)}, bf16[640,640]{1,0:T(8,128)(2,1)S(1)}, u32[]{:S(2)}, u32[]{:S(2)}) collective-permute-start(bf16[640,640]{1,0:T(8,128)(2,1)S(1)} %all_gather.12.own_ref), channel_id=1, source_target_pairs={{0,1},{1,0},{2,3},{3,2},{4,5},{5,4},{6,7},{7,6},{8,9},{9,8},{10,11... | collective-permute-start | bytes 2457608 | tf_op jit(solution)/shard_map/ppermute | solution.py:31
  71.7 4.5 %half.1 = bf16[16,80,256]{2,1,0:T(8,128)(2,1)} custom-call(s32[3]{0:T(128)} %pad_add_fusion.core_ref.place_ref, bf16[640,640]{1,0:T(8,128)(2,1)} %copy-done.4, bf16[640,640]{1,0:T(8,128)(2,1)} %copy-done.9, bf16[8,2,112,512]{3,2,1,0:T(8,128)(2,1)} %bitcast.20), custom_call_target="tpu_custom_call" | custom-call | tf_op jit(solution)/shard_map/half/pallas_call | solution.py:67
  76.2 26.5 %all_to_all.25 = bf16[16,80,256]{2,1,0:T(8,128)(2,1)S(1)} all-to-all(bf16[16,80,256]{2,1,0:T(8,128)(2,1)} %half.1), channel_id=1, replica_groups=mesh['x'=4,'y'=4,'z'=8,'c'=2] {'x','y'}, dimensions={0} | all-to-all | bytes 1310720 | tf_op jit(solution)/shard_map/spread/all_to_all | solution.py:352
  102.7 1.5 collective-permute-start.4
  104.2 2.9 %collective-permute-start.8 = (bf16[16,80,512]{2,1,0:T(8,128)(2,1)}, bf16[16,80,512]{2,1,0:T(8,128)(2,1)S(1)}, u32[]{:S(2)}, u32[]{:S(2)}) collective-permute-start(bf16[16,80,512]{2,1,0:T(8,128)(2,1)} %collective-permute-done.5.xu_ref), channel_id=1, source_target_pairs={{0,14},{2,0},{4,2},{6,4},{8,6},{10,8},{12,10},{14,12},{1,15},{3,1}... | collective-permute-start | bytes 3932168 | tf_op jit(solution)/shard_map/next/ppermute | solution.py:346
  110.9 16.8 %core_first.1 = (f32[1280,512]{1,0:T(8,128)}, bf16[512,1280]{1,0:T(8,128)(2,1)}) custom-call(s32[3]{0:T(128)} %pad_add_fusion.core_ref.place_ref, bf16[1280,256]{1,0:T(8,128)(2,1)} %bitcast.31, bf16[1280,256]{1,0:T(8,128)(2,1)} %collective-permute-done.4.hx_ref, bf16[16,112,512]{2,1,0:T(8,128)(2,1)} %copy-done, ...), custom_call_target="tpu_custom_call" | custom-call | flops 8053063680 | bytes 12000000 | tf_op jit(solution)/shard_map/core_first/pallas_call | solution.py:129
  127.6 7.8 %collective-permute-done.8.xu_ref = bf16[16,80,512]{2,1,0:T(8,128)(2,1)S(1)} collective-permute-done((bf16[16,80,512]{2,1,0:T(8,128)(2,1)}, bf16[16,80,512]{2,1,0:T(8,128)(2,1)S(1)}, u32[]{:S(2)}, u32[]{:S(2)}) %collective-permute-start.8) | collective-permute-done | bytes 1310752 | tf_op jit(solution)/shard_map/next/ppermute | solution.py:346
  135.5 3.0 %collective-permute-done.9.xd_ref = bf16[16,80,512]{2,1,0:T(8,128)(2,1)S(1)} collective-permute-done((bf16[16,80,512]{2,1,0:T(8,128)(2,1)}, bf16[16,80,512]{2,1,0:T(8,128)(2,1)S(1)}, u32[]{:S(2)}, u32[]{:S(2)}) %collective-permute-start.9) | collective-permute-done | bytes 1310752 | tf_op jit(solution)/shard_map/next/ppermute | solution.py:347
  139.6 7.8 %core_last.1 = (f32[1280,256]{1,0:T(8,128)}, bf16[1280,256]{1,0:T(8,128)(2,1)}) custom-call(s32[3]{0:T(128)} %pad_add_fusion.core_ref.place_ref, f32[1280,512]{1,0:T(8,128)} %get-tuple-element.14.acc_ref, bf16[512,1280]{1,0:T(8,128)(2,1)} %get-tuple-element.15.h_ref, bf16[16,80,512]{2,1,0:T(8,128)(2,1)} %copy-done.6, bf16[16,80,512]{2,1,0:T(8,128)(2,1)} %copy-done.7, ...), custom_call_target="tpu_custom_call" | custom-call | flops 2684354560 | bytes 8000000 | tf_op jit(solution)/shard_map/core_last/pallas_call | solution.py:185
  148.6 1.9 collective-permute-done.10
  150.6 2.5 add_convert_fusion.1
  153.0 4.3 %all-to-all-start.2 = ((bf16[16,80,256]{2,1,0:T(8,128)(2,1)}), bf16[16,80,256]{2,1,0:T(8,128)(2,1)}, u32[]{:S(2)}, u32[]{:S(2)}) async-start(bf16[16,80,256]{2,1,0:T(8,128)(2,1)} %bitcast.13), calls=%async_computation.2 | async-start | bytes 1310720 | tf_op jit(solution)/shard_map/all_to_all | solution.py:362
  158.7 10.0 %all-to-all-done.2.b_ref = bf16[16,80,256]{2,1,0:T(8,128)(2,1)} async-done(((bf16[16,80,256]{2,1,0:T(8,128)(2,1)}), bf16[16,80,256]{2,1,0:T(8,128)(2,1)}, u32[]{:S(2)}, u32[]{:S(2)}) %all-to-all-start.2) | async-done | bytes 655392 | tf_op jit(solution)/shard_map/all_to_all | solution.py:362
  168.7 4.4 %ladder_rank.1 = (f32[320,1200]{1,0:T(8,128)}, bf16[320,1200]{1,0:T(8,128)(2,1)}) custom-call(s32[3]{0:T(128)} %pad_add_fusion.core_ref.place_ref, bf16[16,80,256]{2,1,0:T(8,128)(2,1)} %all-to-all-done.2.b_ref, bf16[1200,512]{1,0:T(8,128)(2,1)} %reshape.63.x_ref), custom_call_target="tpu_custom_call" | custom-call | tf_op jit(solution)/shard_map/ladder_rank/pallas_call | solution.py:238
  173.0 2.6 collective-permute-start.11
  175.6 2.2 collective-permute-done.11
  177.8 2.5 add_convert_fusion
  180.3 3.7 %all-to-all-start.3 = ((bf16[8,40,1200]{2,1,0:T(8,128)(2,1)}), bf16[8,40,1200]{2,1,0:T(8,128)(2,1)S(1)}, u32[]{:S(2)}, u32[]{:S(2)}) async-start(bf16[8,40,1200]{2,1,0:T(8,128)(2,1)} %bitcast.14), calls=%async_computation.3 | async-start | bytes 1638400 | tf_op jit(solution)/shard_map/all_to_all | solution.py:368
  185.6 22.6 %all-to-all-done.3.parts_ref = bf16[8,40,1200]{2,1,0:T(8,128)(2,1)S(1)} async-done(((bf16[8,40,1200]{2,1,0:T(8,128)(2,1)}), bf16[8,40,1200]{2,1,0:T(8,128)(2,1)S(1)}, u32[]{:S(2)}, u32[]{:S(2)}) %all-to-all-start.3) | async-done | bytes 768032 | tf_op jit(solution)/shard_map/all_to_all | solution.py:368
  209.1 2.8 %chunk.1 = bf16[40,1280]{1,0:T(8,128)(2,1)} custom-call(s32[3]{0:T(128)} %pad_add_fusion.core_ref.place_ref, bf16[8,40,1200]{2,1,0:T(8,128)(2,1)} %copy-done.3, f32[75,8,1200]{2,1,0:T(8,128)} %bitcast.25, f32[1,1200]{1,0:T(1,128)} %broadcast_in_dim.7.col_ref, f32[600,1]{1,0:T(8,128)} %sub.31.low_ref), custom_call_target="tpu_custom_call" | custom-call | tf_op jit(solution)/shard_map/chunk/pallas_call | solution.py:276
  211.9 20.7 %all_gather.15.own_ref = bf16[320,1280]{1,0:T(8,128)(2,1)S(1)} all-gather(bf16[40,1280]{1,0:T(8,128)(2,1)} %chunk.1), channel_id=1, replica_groups=mesh['x'=4,'y'=4,'z'=8,'c'=2] {'z'}, dimensions={0}, use_global_device_ids=true | all-gather | bytes 921600 | tf_op jit(solution)/shard_map/all_gather | solution.py:375
  232.6 6.2 %collective-permute-start.12 = (bf16[320,1280]{1,0:T(8,128)(2,1)S(1)}, bf16[320,1280]{1,0:T(8,128)(2,1)S(1)}, u32[]{:S(2)}, u32[]{:S(2)}) collective-permute-start(bf16[320,1280]{1,0:T(8,128)(2,1)S(1)} %all_gather.15.own_ref), channel_id=1, source_target_pairs={{0,1},{1,0},{2,3},{3,2},{4,5},{5,4},{6,7},{7,6},{8,9},{9,8},{10,11... | collective-permute-start | bytes 2457608 | tf_op jit(solution)/shard_map/ppermute | solution.py:31
  238.9 2.0 collective-permute-done.12.oth_ref
  243.7 3.5 %all-to-all-start.4 = ((f32[16,8,128]{2,1,0:T(8,128)}), f32[16,8,128]{2,1,0:T(8,128)S(1)}, u32[]{:S(2)}, u32[]{:S(2)}) async-start(f32[16,8,128]{2,1,0:T(8,128)} %broadcast_in_dim.16), calls=%async_computation.4 | async-start | bytes 131072 | tf_op jit(solution)/shard_map/all_to_all | solution.py:381
  247.2 4.3 %residual.1 = f32[75,8,1200]{2,1,0:T(8,128)} custom-call(s32[3]{0:T(128)} %pad_add_fusion.core_ref.place_ref, bf16[320,1280]{1,0:T(8,128)(2,1)} %copy-done.2, bf16[320,1280]{1,0:T(8,128)(2,1)} %copy-done.5, f32[75,8,1200]{2,1,0:T(8,128)} %bitcast.26), custom_call_target="tpu_custom_call" | custom-call | tf_op jit(solution)/shard_map/residual/pallas_call | solution.py:312
  251.5 2.2 all-to-all-done.4
  (66 shorter events, 22.9 us)
Async XLA Ops:
  7.2 103.0 %all-gather.3.cloned.1.call-start = ((), (), s32[]{:S(2)}) async-start(), calls=%async_computation.5 | async-start | bytes 4177920 | tf_op jit(solution)/shard_map/all_gather | solution.py:334
  10.9 15.9 %collective-permute-start = (bf16[80,512]{1,0:T(8,128)(2,1)S(1)}, bf16[80,512]{1,0:T(8,128)(2,1)S(1)}, u32[]{:S(2)}, u32[]{:S(2)}) collective-permute-start(bf16[80,512]{1,0:T(8,128)(2,1)S(1)} %pad.9), channel_id=1, source_target_pairs={{0,10},{2,12},{4,14},{6,0},{8,2},{10,4},{12,6},{14,8},{1,11},{3,13... | collective-permute-start | bytes 245768 | tf_op jit(solution)/shard_map/far/ppermute | solution.py:333
  18.1 8.6 %collective-permute-start.1 = (bf16[80,512]{1,0:T(8,128)(2,1)S(1)}, bf16[80,512]{1,0:T(8,128)(2,1)S(1)}, u32[]{:S(2)}, u32[]{:S(2)}) collective-permute-start(bf16[80,512]{1,0:T(8,128)(2,1)S(1)} %pad.9), channel_id=1, source_target_pairs={{0,8},{2,10},{4,12},{6,14},{8,0},{10,2},{12,4},{14,6},{1,9},{3,11}... | collective-permute-start | bytes 245768 | tf_op jit(solution)/shard_map/far/ppermute | solution.py:333
  18.6 12.4 %collective-permute-start.2 = (bf16[80,512]{1,0:T(8,128)(2,1)S(1)}, bf16[80,512]{1,0:T(8,128)(2,1)S(1)}, u32[]{:S(2)}, u32[]{:S(2)}) collective-permute-start(bf16[80,512]{1,0:T(8,128)(2,1)S(1)} %pad.9), channel_id=1, source_target_pairs={{0,6},{2,8},{4,10},{6,12},{8,14},{10,0},{12,2},{14,4},{1,7},{3,9},... | collective-permute-start | bytes 245768 | tf_op jit(solution)/shard_map/far/ppermute | solution.py:333
  31.7 6.9 %copy-start.11 = (bf16[8,75,75]{2,0,1:T(8,128)(2,1)S(1)}, bf16[8,75,75]{2,0,1:T(8,128)(2,1)}, u32[]{:S(2)}) copy-start(bf16[8,75,75]{2,0,1:T(8,128)(2,1)} %param.6) | copy-start | bytes 270004
  31.7 35.7 %all-to-all-start = ((bf16[16,112,512]{2,1,0:T(8,128)(2,1)}), bf16[16,112,512]{2,1,0:T(8,128)(2,1)S(1)}, u32[]{:S(2)}, u32[]{:S(2)}) async-start(bf16[16,112,512]{2,1,0:T(8,128)(2,1)} %pad_maximum_fusion), calls=%async_computation | async-start | bytes 3670016 | tf_op jit(solution)/shard_map/own/all_to_all | solution.py:331
  62.6 8.1 %copy-start.4 = (bf16[640,640]{1,0:T(8,128)(2,1)}, bf16[640,640]{1,0:T(8,128)(2,1)S(1)}, u32[]{:S(2)}) copy-start(bf16[640,640]{1,0:T(8,128)(2,1)S(1)} %all_gather.12.own_ref) | copy-start | bytes 2457604
  62.7 8.1 %collective-permute-start.3 = (bf16[640,640]{1,0:T(8,128)(2,1)S(1)}, bf16[640,640]{1,0:T(8,128)(2,1)S(1)}, u32[]{:S(2)}, u32[]{:S(2)}) collective-permute-start(bf16[640,640]{1,0:T(8,128)(2,1)S(1)} %all_gather.12.own_ref), channel_id=1, source_target_pairs={{0,1},{1,0},{2,3},{3,2},{4,5},{5,4},{6,7},{7,6},{8,9},{9,8},{10,11... | collective-permute-start | bytes 2457608 | tf_op jit(solution)/shard_map/ppermute | solution.py:31
  67.5 3.3 %copy-start = (bf16[16,112,512]{2,1,0:T(8,128)(2,1)}, bf16[16,112,512]{2,1,0:T(8,128)(2,1)S(1)}, u32[]{:S(2)}) copy-start(bf16[16,112,512]{2,1,0:T(8,128)(2,1)S(1)} %all-to-all-done.xq_ref) | copy-start | bytes 5505028
  68.7 35.6 %collective-permute-start.5 = (bf16[16,80,512]{2,1,0:T(8,128)(2,1)}, bf16[16,80,512]{2,1,0:T(8,128)(2,1)}, u32[]{:S(2)}, u32[]{:S(2)}) collective-permute-start(bf16[16,80,512]{2,1,0:T(8,128)(2,1)} %slice.20), channel_id=1, source_target_pairs={{0,14},{2,0},{4,2},{6,4},{8,6},{10,8},{12,10},{14,12},{1,15},{3,1}... | collective-permute-start | bytes 3932168 | tf_op jit(solution)/shard_map/near/ppermute | solution.py:343
  70.1 37.1 %collective-permute-start.6 = (bf16[16,80,512]{2,1,0:T(8,128)(2,1)}, bf16[16,80,512]{2,1,0:T(8,128)(2,1)}, u32[]{:S(2)}, u32[]{:S(2)}) collective-permute-start(bf16[16,80,512]{2,1,0:T(8,128)(2,1)} %slice.20), channel_id=1, source_target_pairs={{0,2},{2,4},{4,6},{6,8},{8,10},{10,12},{12,14},{14,0},{1,3},{3,5},... | collective-permute-start | bytes 3932168 | tf_op jit(solution)/shard_map/near/ppermute | solution.py:344
  70.8 0.9 copy-start.9
  102.7 7.5 %copy-start.10 = (bf16[16,80,256]{2,1,0:T(8,128)(2,1)}, bf16[16,80,256]{2,1,0:T(8,128)(2,1)S(1)}, u32[]{:S(2)}) copy-start(bf16[16,80,256]{2,1,0:T(8,128)(2,1)S(1)} %all_to_all.25) | copy-start | bytes 1966084
  102.7 7.5 %collective-permute-start.4 = (bf16[1280,256]{1,0:T(8,128)(2,1)S(1)}, bf16[1280,256]{1,0:T(8,128)(2,1)}, u32[]{:S(2)}, u32[]{:S(2)}) collective-permute-start(bf16[1280,256]{1,0:T(8,128)(2,1)S(1)} %bitcast.30), channel_id=1, source_target_pairs={{0,1},{1,0},{2,3},{3,2},{4,5},{5,4},{6,7},{7,6},{8,9},{9,8},{10,11... | collective-permute-start | bytes 1966088 | tf_op jit(solution)/shard_map/ppermute | solution.py:31
  104.2 31.2 %collective-permute-start.8 = (bf16[16,80,512]{2,1,0:T(8,128)(2,1)}, bf16[16,80,512]{2,1,0:T(8,128)(2,1)S(1)}, u32[]{:S(2)}, u32[]{:S(2)}) collective-permute-start(bf16[16,80,512]{2,1,0:T(8,128)(2,1)} %collective-permute-done.5.xu_ref), channel_id=1, source_target_pairs={{0,14},{2,0},{4,2},{6,4},{8,6},{10,8},{12,10},{14,12},{1,15},{3,1}... | collective-permute-start | bytes 3932168 | tf_op jit(solution)/shard_map/next/ppermute | solution.py:346
  107.1 31.4 %collective-permute-start.9 = (bf16[16,80,512]{2,1,0:T(8,128)(2,1)}, bf16[16,80,512]{2,1,0:T(8,128)(2,1)S(1)}, u32[]{:S(2)}, u32[]{:S(2)}) collective-permute-start(bf16[16,80,512]{2,1,0:T(8,128)(2,1)} %collective-permute-done.6.xd_ref), channel_id=1, source_target_pairs={{0,2},{2,4},{4,6},{6,8},{8,10},{10,12},{12,14},{14,0},{1,3},{3,5},... | collective-permute-start | bytes 3932168 | tf_op jit(solution)/shard_map/next/ppermute | solution.py:347
  108.4 1.8 collective-permute-start.7
  110.2 0.7 copy-start.8
  135.5 3.0 %copy-start.6 = (bf16[16,80,512]{2,1,0:T(8,128)(2,1)}, bf16[16,80,512]{2,1,0:T(8,128)(2,1)S(1)}, u32[]{:S(2)}) copy-start(bf16[16,80,512]{2,1,0:T(8,128)(2,1)S(1)} %collective-permute-done.8.xu_ref) | copy-start | bytes 3932164
  138.5 1.1 copy-start.7
  147.4 3.2 %collective-permute-start.10 = (bf16[1280,256]{1,0:T(8,128)(2,1)}, bf16[1280,256]{1,0:T(8,128)(2,1)S(1)}, u32[]{:S(2)}, u32[]{:S(2)}) collective-permute-start(bf16[1280,256]{1,0:T(8,128)(2,1)} %get-tuple-element.17), channel_id=1, source_target_pairs={{0,1},{1,0},{2,3},{3,2},{4,5},{5,4},{6,7},{7,6},{8,9},{9,8},{10,11... | collective-permute-start | bytes 1966088 | tf_op jit(solution)/shard_map/ppermute | solution.py:31
  150.6 6.7 %copy-start.1 = (bf16[16,112,512]{2,1,0:T(8,128)(2,1)S(1)}, bf16[16,112,512]{2,1,0:T(8,128)(2,1)}, u32[]{:S(2)}) copy-start(bf16[16,112,512]{2,1,0:T(8,128)(2,1)} %copy-done) | copy-start | bytes 5505028
  153.0 15.6 %all-to-all-start.2 = ((bf16[16,80,256]{2,1,0:T(8,128)(2,1)}), bf16[16,80,256]{2,1,0:T(8,128)(2,1)}, u32[]{:S(2)}, u32[]{:S(2)}) async-start(bf16[16,80,256]{2,1,0:T(8,128)(2,1)} %bitcast.13), calls=%async_computation.2 | async-start | bytes 1310720 | tf_op jit(solution)/shard_map/all_to_all | solution.py:362
  173.0 4.8 %collective-permute-start.11 = (bf16[320,1200]{1,0:T(8,128)(2,1)}, bf16[320,1200]{1,0:T(8,128)(2,1)S(1)}, u32[]{:S(2)}, u32[]{:S(2)}) collective-permute-start(bf16[320,1200]{1,0:T(8,128)(2,1)} %get-tuple-element.19), channel_id=1, source_target_pairs={{0,1},{1,0},{2,3},{3,2},{4,5},{5,4},{6,7},{7,6},{8,9},{9,8},{10,11... | collective-permute-start | bytes 2304008 | tf_op jit(solution)/shard_map/ppermute | solution.py:31
  180.3 3.7 %copy-start.12 = (f32[1200]{0:T(1024)S(1)}, f32[1200]{0:T(1024)}, u32[]{:S(2)}) copy-start(f32[1200]{0:T(1024)} %param.10) | copy-start | bytes 14404
  180.3 4.4 %copy-start.13 = (f32[8]{0:T(128)S(1)}, f32[8]{0:T(128)}, u32[]{:S(2)}) copy-start(f32[8]{0:T(128)} %param.11) | copy-start | bytes 100
  180.3 27.9 %all-to-all-start.3 = ((bf16[8,40,1200]{2,1,0:T(8,128)(2,1)}), bf16[8,40,1200]{2,1,0:T(8,128)(2,1)S(1)}, u32[]{:S(2)}, u32[]{:S(2)}) async-start(bf16[8,40,1200]{2,1,0:T(8,128)(2,1)} %bitcast.14), calls=%async_computation.3 | async-start | bytes 1638400 | tf_op jit(solution)/shard_map/all_to_all | solution.py:368
  208.2 0.9 copy-start.3
  232.6 8.3 %copy-start.2 = (bf16[320,1280]{1,0:T(8,128)(2,1)}, bf16[320,1280]{1,0:T(8,128)(2,1)S(1)}, u32[]{:S(2)}) copy-start(bf16[320,1280]{1,0:T(8,128)(2,1)S(1)} %all_gather.15.own_ref) | copy-start | bytes 2457604
  232.6 8.2 %collective-permute-start.12 = (bf16[320,1280]{1,0:T(8,128)(2,1)S(1)}, bf16[320,1280]{1,0:T(8,128)(2,1)S(1)}, u32[]{:S(2)}, u32[]{:S(2)}) collective-permute-start(bf16[320,1280]{1,0:T(8,128)(2,1)S(1)} %all_gather.15.own_ref), channel_id=1, source_target_pairs={{0,1},{1,0},{2,3},{3,2},{4,5},{5,4},{6,7},{7,6},{8,9},{9,8},{10,11... | collective-permute-start | bytes 2457608 | tf_op jit(solution)/shard_map/ppermute | solution.py:31
  240.8 0.9 copy-start.5
  243.7 10.0 %all-to-all-start.4 = ((f32[16,8,128]{2,1,0:T(8,128)}), f32[16,8,128]{2,1,0:T(8,128)S(1)}, u32[]{:S(2)}, u32[]{:S(2)}) async-start(f32[16,8,128]{2,1,0:T(8,128)} %broadcast_in_dim.16), calls=%async_computation.4 | async-start | bytes 131072 | tf_op jit(solution)/shard_map/all_to_all | solution.py:381
Sparse Core Ops, SparseCore 0:
  31.8 72.3 all-gather.2

commit v5 on v4

--- a/solution.py
+++ b/solution.py
@@ -327,29 +327,32 @@
     z_cols = kernel.T.reshape(NV, QC, BLK)
     xz = jnp.concatenate([jnp.broadcast_to(x_pad[None], (NV, PAD, BLK)), z_cols], axis=1)
     x_pad, xz = lax.optimization_barrier((x_pad, xz))
-    with jax.named_scope("own"):
-        xz = lax.all_to_all(xz, XY, split_axis=0, concat_axis=0, tiled=True)
-    with jax.named_scope("far"):
-        x_far = jnp.stack([lax.ppermute(x_pad, "z", ring(-j)) for j in FIRST[3:]])
-    x_all = lax.all_gather(x_far, XY, axis=0)
+    xz = lax.all_to_all(xz, XY, split_axis=0, concat_axis=0, tiled=True)
+    x_far = jnp.stack([lax.ppermute(x_pad, "z", ring(-j)) for j in FIRST[3:]])
+    x_all = lax.all_to_all(
+        jnp.broadcast_to(x_far[None], (NV, *x_far.shape)),
+        XY,
+        split_axis=0,
+        concat_axis=0,
+        tiled=True,
+    )
 
     t_cols = jnp.pad(amplitudes, ((0, 0), (0, PAD - ROW), (0, PAD - ROW)))
     t_cols = jnp.transpose(t_cols, (2, 0, 1)).reshape(PAD, PAIRS * PAD)
-    t_cols, _ = lax.optimization_barrier((t_cols, x_far))
+    t_cols, _, _ = lax.optimization_barrier((t_cols, x_far, xz))
     t_own = lax.all_gather(t_cols, "z", axis=0, tiled=True)
     t_oth = core_swap(t_own)
     x_own = xz[:, :PAD]
-    with jax.named_scope("near"):
-        x_up = lax.ppermute(x_own, "z", ring(-1))
-        x_down = lax.ppermute(x_own, "z", ring(1))
-    with jax.named_scope("next"):
-        x_up2 = lax.ppermute(x_up, "z", ring(-1))
-        x_down2 = lax.ppermute(x_down, "z", ring(1))
+    x_up = lax.ppermute(x_own, "z", ring(-1))
+    x_down = lax.ppermute(x_own, "z", ring(1))
+    x_up2 = lax.ppermute(x_up, "z", ring(-1))
+    x_down2 = lax.ppermute(x_down, "z", ring(1))
     x_rows = xz[:, :ROW].reshape(NVIR, BLK)
 
+    t_own, t_oth, _, _ = lax.optimization_barrier((t_own, t_oth, x_up, x_down))
     h_msg = make_half(place, t_own, t_oth, xz.reshape(NZ, NC, PAD + QC, BLK))
-    with jax.named_scope("spread"):
-        h_own = lax.all_to_all(h_msg, XY, split_axis=0, concat_axis=0, tiled=True)
+    h_msg, x_all = lax.optimization_barrier((h_msg, x_all))
+    h_own = lax.all_to_all(h_msg, XY, split_axis=0, concat_axis=0, tiled=True)
     h_own = h_own.reshape(NV * PAD, PAIRS * QC)
     h_oth = core_swap(h_own)
     z_all = xz.reshape(NZ, NC, PAD + QC, BLK)

time: 264 us -> 282 us (1.068)
  blocking collectives: 70.8 us -> 85.4 us
  between operations: 16 us -> 2.63 us
  starting transfers between devices: 50.7 us -> 61.7 us
  waiting for transfers between devices: 62 us -> 68 us
    all_gather x1, blocking collectives: 23.6 us -> 45.8 us  [shards(): t_own = lax.all_gather(t_cols, 'z', axis=0, tiled=True)]
    all_to_all x1, blocking collectives: 26.5 us -> 18.9 us  [shards(): h_own = lax.all_to_all(h_msg, XY, split_axis=0, concat_axis=0, tiled=True)]
    all_to_all x0 -> x1, starting transfers between devices: none -> 4.83 us  [shards(): lax.all_to_all(jnp.broadcast_to(x_far[None], (NV, *x_far.shape)), XY, spl...]
    all_to_all x1, waiting for transfers between devices: 0.01 us -> 4.62 us  [shards(): xz = lax.all_to_all(xz, XY, split_axis=0, concat_axis=0, tiled=True)]
    ppermute x1, starting transfers between devices: 1.36 us -> 5.58 us  [shards(): x_up = lax.ppermute(x_own, 'z', ring(-1))]
    ppermute x6, starting transfers between devices: 17 us -> 20.6 us  [core_swap(): return lax.ppermute(value, 'c', [(0, 1), (1, 0)])]
    ppermute x1, starting transfers between devices: 2.86 us -> 0.01 us  [shards(): x_up2 = lax.ppermute(x_up, 'z', ring(-1))]
  transfers between devices with their start and end apart: 18 -> 18, of which waited for: 11 -> 13; matrix products, arithmetic and copies ran while one was open for 2% -> 2% of each run, Pallas kernels for 10% -> 9%
where the time goes in v5:
time: 282 us; the launch traced here: 281 us
  blocking collectives  85.4 us (30%)
  waiting for transfers between devices  68 us (24%)
  starting transfers between devices  61.7 us (22%)
  Pallas kernels  40.7 us (14%)
  local copies, waits for them, and re-layouts  14.3 us (5%)
  other arithmetic  8.51 us (3%)
    all_gather x1, blocking collectives, shards(): t_own = lax.all_gather(t_cols, 'z', axis=0, tiled=True)  45.8 us
    all_to_all x1, waiting for transfers between devices, shards(): lax.all_to_all(l_sum.reshape(NZ, CHUNK * PAIRS, NVIR), 'z', split_axis=0,...  22.6 us
    all_gather x1, blocking collectives, shards(): l_mine = lax.all_gather(chunk, 'z', axis=0, tiled=True)  20.7 us
    ppermute x6, starting transfers between devices, core_swap(): return lax.ppermute(value, 'c', [(0, 1), (1, 0)])  20.6 us
    all_to_all x1, blocking collectives, shards(): h_own = lax.all_to_all(h_msg, XY, split_axis=0, concat_axis=0, tiled=True)  18.9 us
    pallas_call x1, Pallas kernels, make_first(): pl.pallas_call(first_kernel, out_shape=(jax.ShapeDtypeStruct((rows, 2 * H...  16.8 us
    ppermute x3, starting transfers between devices, shards(): x_far = jnp.stack([lax.ppermute(x_pad, 'z', ring(-j)) for j in FIRST[3:]])  10.3 us
    all_to_all x1, waiting for transfers between devices, shards(): lax.all_to_all(b_sum.reshape(NV, PAD, PAIRS * QC), XY, split_axis=0, conc...  9.97 us
  transfers between devices with their start and end apart: 18, of which 13 were waited for; matrix products, arithmetic and copies ran while one was open for 2% of the time, Pallas kernels for 9%

profile of v5, /device:TPU:1, one launch (start us, length us, event | category | flops | bytes accessed | tf_op | source)
XLA Modules:
  0.0 281.2 jit_solution(2190752483710791424)
XLA Ops:
  4.3 7.6 %all-to-all-start = ((bf16[16,112,512]{2,1,0:T(8,128)(2,1)}), bf16[16,112,512]{2,1,0:T(8,128)(2,1)S(1)}, u32[]{:S(2)}, u32[]{:S(2)}) async-start(bf16[16,112,512]{2,1,0:T(8,128)(2,1)} %pad_maximum_fusion), calls=%async_computation | async-start | bytes 3670016 | tf_op jit(solution)/shard_map/all_to_all | solution.py:330
  11.9 6.5 %collective-permute-start = (bf16[80,512]{1,0:T(8,128)(2,1)S(1)}, bf16[80,512]{1,0:T(8,128)(2,1)S(1)}, u32[]{:S(2)}, u32[]{:S(2)}) collective-permute-start(bf16[80,512]{1,0:T(8,128)(2,1)S(1)} %pad.9), channel_id=1, source_target_pairs={{0,10},{2,12},{4,14},{6,0},{8,2},{10,4},{12,6},{14,8},{1,11},{3,13... | collective-permute-start | bytes 245768 | tf_op jit(solution)/shard_map/ppermute | solution.py:331
  19.0 3.2 %collective-permute-start.2 = (bf16[80,512]{1,0:T(8,128)(2,1)S(1)}, bf16[80,512]{1,0:T(8,128)(2,1)S(1)}, u32[]{:S(2)}, u32[]{:S(2)}) collective-permute-start(bf16[80,512]{1,0:T(8,128)(2,1)S(1)} %pad.9), channel_id=1, source_target_pairs={{0,6},{2,8},{4,10},{6,12},{8,14},{10,0},{12,2},{14,4},{1,7},{3,9},... | collective-permute-start | bytes 245768 | tf_op jit(solution)/shard_map/ppermute | solution.py:331
  22.1 4.9 %collective-permute-done = bf16[80,512]{1,0:T(8,128)(2,1)S(1)} collective-permute-done((bf16[80,512]{1,0:T(8,128)(2,1)S(1)}, bf16[80,512]{1,0:T(8,128)(2,1)S(1)}, u32[]{:S(2)}, u32[]{:S(2)}) %collective-permute-start) | collective-permute-done | bytes 81952 | tf_op jit(solution)/shard_map/ppermute | solution.py:331
  27.0 4.4 %collective-permute-done.2 = bf16[80,512]{1,0:T(8,128)(2,1)S(1)} collective-permute-done((bf16[80,512]{1,0:T(8,128)(2,1)S(1)}, bf16[80,512]{1,0:T(8,128)(2,1)S(1)}, u32[]{:S(2)}, u32[]{:S(2)}) %collective-permute-start.2) | collective-permute-done | bytes 81952 | tf_op jit(solution)/shard_map/ppermute | solution.py:331
  31.5 4.6 %all-to-all-done.xq_ref = bf16[16,112,512]{2,1,0:T(8,128)(2,1)S(1)} async-done(((bf16[16,112,512]{2,1,0:T(8,128)(2,1)}), bf16[16,112,512]{2,1,0:T(8,128)(2,1)S(1)}, u32[]{:S(2)}, u32[]{:S(2)}) %all-to-all-start) | async-done | bytes 1835040 | tf_op jit(solution)/shard_map/all_to_all | solution.py:330
  36.1 2.4 broadcast_in_dim.9
  38.5 4.8 %all-to-all-start.1 = ((bf16[16,3,80,512]{3,2,1,0:T(8,128)(2,1)}), bf16[16,3,80,512]{3,2,1,0:T(8,128)(2,1)}, u32[]{:S(2)}, u32[]{:S(2)}) async-start(bf16[16,3,80,512]{3,2,1,0:T(8,128)(2,1)} %broadcast_in_dim.9), calls=%async_computation.1 | async-start | bytes 7864320 | tf_op jit(solution)/shard_map/all_to_all | solution.py:332
  44.5 5.6 %collective-permute-start.4 = (bf16[16,80,512]{2,1,0:T(8,128)(2,1)}, bf16[16,80,512]{2,1,0:T(8,128)(2,1)S(1)}, u32[]{:S(2)}, u32[]{:S(2)}) collective-permute-start(bf16[16,80,512]{2,1,0:T(8,128)(2,1)} %slice.20), channel_id=1, source_target_pairs={{0,14},{2,0},{4,2},{6,4},{8,6},{10,8},{12,10},{14,12},{1,15},{3,1}... | collective-permute-start | bytes 3932168 | tf_op jit(solution)/shard_map/ppermute | solution.py:346
  50.5 45.8 %all_gather.6.own_ref = bf16[640,640]{1,0:T(8,128)(2,1)S(1)} all-gather(bf16[80,640]{1,0:T(8,128)(2,1)S(1)} %reshape.59), channel_id=1, replica_groups=mesh['x'=4,'y'=4,'z'=8,'c'=2] {'z'}, dimensions={0}, use_global_device_ids=true | all-gather | bytes 921600 | tf_op jit(solution)/shard_map/all_gather | solution.py:343
  96.3 8.3 %collective-permute-start.3 = (bf16[640,640]{1,0:T(8,128)(2,1)S(1)}, bf16[640,640]{1,0:T(8,128)(2,1)S(1)}, u32[]{:S(2)}, u32[]{:S(2)}) collective-permute-start(bf16[640,640]{1,0:T(8,128)(2,1)S(1)} %all_gather.6.own_ref), channel_id=1, source_target_pairs={{0,1},{1,0},{2,3},{3,2},{4,5},{5,4},{6,7},{7,6},{8,9},{9,8},{10,11... | collective-permute-start | bytes 2457608 | tf_op jit(solution)/shard_map/ppermute | solution.py:31
  107.9 4.7 %half.1 = bf16[16,80,256]{2,1,0:T(8,128)(2,1)} custom-call(s32[3]{0:T(128)} %pad_add_fusion.core_ref.place_ref, bf16[640,640]{1,0:T(8,128)(2,1)} %copy-done.5, bf16[640,640]{1,0:T(8,128)(2,1)} %copy-done.9, bf16[8,2,112,512]{3,2,1,0:T(8,128)(2,1)} %bitcast.19), custom_call_target="tpu_custom_call" | custom-call | tf_op jit(solution)/shard_map/half/pallas_call | solution.py:67
  112.6 18.9 %all_to_all.30 = bf16[16,80,256]{2,1,0:T(8,128)(2,1)} all-to-all(bf16[16,80,256]{2,1,0:T(8,128)(2,1)} %half.1), channel_id=1, replica_groups=mesh['x'=4,'y'=4,'z'=8,'c'=2] {'x','y'}, dimensions={0} | all-to-all | bytes 1310720 | tf_op jit(solution)/shard_map/all_to_all | solution.py:355
  137.5 16.8 %core_first.1 = (f32[1280,512]{1,0:T(8,128)}, bf16[512,1280]{1,0:T(8,128)(2,1)}) custom-call(s32[3]{0:T(128)} %pad_add_fusion.core_ref.place_ref, bf16[1280,256]{1,0:T(8,128)(2,1)} %bitcast.10.ho_ref, bf16[1280,256]{1,0:T(8,128)(2,1)} %collective-permute-done.6.hx_ref, bf16[16,112,512]{2,1,0:T(8,128)(2,1)} %copy-done, bf16[16,80,512]{2,1,0:T(8,128)(2,1)} %copy-done.13, ...), custom_call_target="tpu_custom_call" | custom-call | flops 8053063680 | bytes 12000000 | tf_op jit(solution)/shard_map/core_first/pallas_call | solution.py:129
  154.2 9.6 %collective-permute-done.8.xu_ref = bf16[16,80,512]{2,1,0:T(8,128)(2,1)S(1)} collective-permute-done((bf16[16,80,512]{2,1,0:T(8,128)(2,1)}, bf16[16,80,512]{2,1,0:T(8,128)(2,1)S(1)}, u32[]{:S(2)}, u32[]{:S(2)}) %collective-permute-start.8) | collective-permute-done | bytes 1310752 | tf_op jit(solution)/shard_map/ppermute | solution.py:348
  165.0 7.8 %core_last.1 = (f32[1280,256]{1,0:T(8,128)}, bf16[1280,256]{1,0:T(8,128)(2,1)}) custom-call(s32[3]{0:T(128)} %pad_add_fusion.core_ref.place_ref, f32[1280,512]{1,0:T(8,128)} %get-tuple-element.22.acc_ref, bf16[512,1280]{1,0:T(8,128)(2,1)} %get-tuple-element.23.h_ref, bf16[16,80,512]{2,1,0:T(8,128)(2,1)} %copy-done.7, ...), custom_call_target="tpu_custom_call" | custom-call | flops 2684354560 | bytes 8000000 | tf_op jit(solution)/shard_map/core_last/pallas_call | solution.py:185
  175.7 2.5 add_convert_fusion.1
  178.1 4.3 %all-to-all-start.3 = ((bf16[16,80,256]{2,1,0:T(8,128)(2,1)}), bf16[16,80,256]{2,1,0:T(8,128)(2,1)}, u32[]{:S(2)}, u32[]{:S(2)}) async-start(bf16[16,80,256]{2,1,0:T(8,128)(2,1)} %bitcast.12), calls=%async_computation.3 | async-start | bytes 1310720 | tf_op jit(solution)/shard_map/all_to_all | solution.py:365
  183.8 10.0 %all-to-all-done.3.b_ref = bf16[16,80,256]{2,1,0:T(8,128)(2,1)} async-done(((bf16[16,80,256]{2,1,0:T(8,128)(2,1)}), bf16[16,80,256]{2,1,0:T(8,128)(2,1)}, u32[]{:S(2)}, u32[]{:S(2)}) %all-to-all-start.3) | async-done | bytes 655392 | tf_op jit(solution)/shard_map/all_to_all | solution.py:365
  193.8 4.4 %ladder_rank.1 = (f32[320,1200]{1,0:T(8,128)}, bf16[320,1200]{1,0:T(8,128)(2,1)}) custom-call(s32[3]{0:T(128)} %pad_add_fusion.core_ref.place_ref, bf16[16,80,256]{2,1,0:T(8,128)(2,1)} %all-to-all-done.3.b_ref, bf16[1200,512]{1,0:T(8,128)(2,1)} %reshape.64.x_ref), custom_call_target="tpu_custom_call" | custom-call | tf_op jit(solution)/shard_map/ladder_rank/pallas_call | solution.py:238
  198.1 2.6 collective-permute-start.11
  200.7 2.2 collective-permute-done.11
  202.9 2.5 add_convert_fusion
  205.4 3.7 %all-to-all-start.4 = ((bf16[8,40,1200]{2,1,0:T(8,128)(2,1)}), bf16[8,40,1200]{2,1,0:T(8,128)(2,1)S(1)}, u32[]{:S(2)}, u32[]{:S(2)}) async-start(bf16[8,40,1200]{2,1,0:T(8,128)(2,1)} %bitcast.13), calls=%async_computation.4 | async-start | bytes 1638400 | tf_op jit(solution)/shard_map/all_to_all | solution.py:371
  210.7 22.6 %all-to-all-done.4.parts_ref = bf16[8,40,1200]{2,1,0:T(8,128)(2,1)S(1)} async-done(((bf16[8,40,1200]{2,1,0:T(8,128)(2,1)}), bf16[8,40,1200]{2,1,0:T(8,128)(2,1)S(1)}, u32[]{:S(2)}, u32[]{:S(2)}) %all-to-all-start.4) | async-done | bytes 768032 | tf_op jit(solution)/shard_map/all_to_all | solution.py:371
  234.2 2.8 chunk.1
  237.0 20.7 %all_gather.7.own_ref = bf16[320,1280]{1,0:T(8,128)(2,1)S(1)} all-gather(bf16[40,1280]{1,0:T(8,128)(2,1)} %chunk.1), channel_id=1, replica_groups=mesh['x'=4,'y'=4,'z'=8,'c'=2] {'z'}, dimensions={0}, use_global_device_ids=true | all-gather | bytes 921600 | tf_op jit(solution)/shard_map/all_gather | solution.py:378
  257.7 6.2 %collective-permute-start.12 = (bf16[320,1280]{1,0:T(8,128)(2,1)S(1)}, bf16[320,1280]{1,0:T(8,128)(2,1)S(1)}, u32[]{:S(2)}, u32[]{:S(2)}) collective-permute-start(bf16[320,1280]{1,0:T(8,128)(2,1)S(1)} %all_gather.7.own_ref), channel_id=1, source_target_pairs={{0,1},{1,0},{2,3},{3,2},{4,5},{5,4},{6,7},{7,6},{8,9},{9,8},{10,11... | collective-permute-start | bytes 2457608 | tf_op jit(solution)/shard_map/ppermute | solution.py:31
  264.0 2.0 collective-permute-done.12.oth_ref
  268.8 3.5 %all-to-all-start.5 = ((f32[16,8,128]{2,1,0:T(8,128)}), f32[16,8,128]{2,1,0:T(8,128)S(1)}, u32[]{:S(2)}, u32[]{:S(2)}) async-start(f32[16,8,128]{2,1,0:T(8,128)} %broadcast_in_dim.11), calls=%async_computation.5 | async-start | bytes 131072 | tf_op jit(solution)/shard_map/all_to_all | solution.py:384
  272.3 4.3 %residual.1 = f32[75,8,1200]{2,1,0:T(8,128)} custom-call(s32[3]{0:T(128)} %pad_add_fusion.core_ref.place_ref, bf16[320,1280]{1,0:T(8,128)(2,1)} %copy-done.3, bf16[320,1280]{1,0:T(8,128)(2,1)} %copy-done.6, f32[75,8,1200]{2,1,0:T(8,128)} %bitcast.25), custom_call_target="tpu_custom_call" | custom-call | tf_op jit(solution)/shard_map/residual/pallas_call | solution.py:312
  276.6 2.2 all-to-all-done.5
  (66 shorter events, 26.4 us)
Async XLA Ops:
  4.3 31.8 %all-to-all-start = ((bf16[16,112,512]{2,1,0:T(8,128)(2,1)}), bf16[16,112,512]{2,1,0:T(8,128)(2,1)S(1)}, u32[]{:S(2)}, u32[]{:S(2)}) async-start(bf16[16,112,512]{2,1,0:T(8,128)(2,1)} %pad_maximum_fusion), calls=%async_computation | async-start | bytes 3670016 | tf_op jit(solution)/shard_map/all_to_all | solution.py:330
  11.9 15.1 %collective-permute-start = (bf16[80,512]{1,0:T(8,128)(2,1)S(1)}, bf16[80,512]{1,0:T(8,128)(2,1)S(1)}, u32[]{:S(2)}, u32[]{:S(2)}) collective-permute-start(bf16[80,512]{1,0:T(8,128)(2,1)S(1)} %pad.9), channel_id=1, source_target_pairs={{0,10},{2,12},{4,14},{6,0},{8,2},{10,4},{12,6},{14,8},{1,11},{3,13... | collective-permute-start | bytes 245768 | tf_op jit(solution)/shard_map/ppermute | solution.py:331
  18.4 8.6 %collective-permute-start.1 = (bf16[80,512]{1,0:T(8,128)(2,1)S(1)}, bf16[80,512]{1,0:T(8,128)(2,1)S(1)}, u32[]{:S(2)}, u32[]{:S(2)}) collective-permute-start(bf16[80,512]{1,0:T(8,128)(2,1)S(1)} %pad.9), channel_id=1, source_target_pairs={{0,8},{2,10},{4,12},{6,14},{8,0},{10,2},{12,4},{14,6},{1,9},{3,11}... | collective-permute-start | bytes 245768 | tf_op jit(solution)/shard_map/ppermute | solution.py:331
  19.0 12.5 %collective-permute-start.2 = (bf16[80,512]{1,0:T(8,128)(2,1)S(1)}, bf16[80,512]{1,0:T(8,128)(2,1)S(1)}, u32[]{:S(2)}, u32[]{:S(2)}) collective-permute-start(bf16[80,512]{1,0:T(8,128)(2,1)S(1)} %pad.9), channel_id=1, source_target_pairs={{0,6},{2,8},{4,10},{6,12},{8,14},{10,0},{12,2},{14,4},{1,7},{3,9},... | collective-permute-start | bytes 245768 | tf_op jit(solution)/shard_map/ppermute | solution.py:331
  36.1 7.3 %copy-start = (bf16[16,112,512]{2,1,0:T(8,128)(2,1)}, bf16[16,112,512]{2,1,0:T(8,128)(2,1)S(1)}, u32[]{:S(2)}) copy-start(bf16[16,112,512]{2,1,0:T(8,128)(2,1)S(1)} %all-to-all-done.xq_ref) | copy-start | bytes 5505028
  38.5 74.0 %all-to-all-start.1 = ((bf16[16,3,80,512]{3,2,1,0:T(8,128)(2,1)}), bf16[16,3,80,512]{3,2,1,0:T(8,128)(2,1)}, u32[]{:S(2)}, u32[]{:S(2)}) async-start(bf16[16,3,80,512]{3,2,1,0:T(8,128)(2,1)} %broadcast_in_dim.9), calls=%async_computation.1 | async-start | bytes 7864320 | tf_op jit(solution)/shard_map/all_to_all | solution.py:332
  43.4 6.7 %copy-start.10 = (bf16[8,75,75]{2,0,1:T(8,128)(2,1)S(1)}, bf16[8,75,75]{2,0,1:T(8,128)(2,1)}, u32[]{:S(2)}) copy-start(bf16[8,75,75]{2,0,1:T(8,128)(2,1)} %param.6) | copy-start | bytes 270004
  44.5 62.0 %collective-permute-start.4 = (bf16[16,80,512]{2,1,0:T(8,128)(2,1)}, bf16[16,80,512]{2,1,0:T(8,128)(2,1)S(1)}, u32[]{:S(2)}, u32[]{:S(2)}) collective-permute-start(bf16[16,80,512]{2,1,0:T(8,128)(2,1)} %slice.20), channel_id=1, source_target_pairs={{0,14},{2,0},{4,2},{6,4},{8,6},{10,8},{12,10},{14,12},{1,15},{3,1}... | collective-permute-start | bytes 3932168 | tf_op jit(solution)/shard_map/ppermute | solution.py:346
  50.1 56.4 %collective-permute-start.5 = (bf16[16,80,512]{2,1,0:T(8,128)(2,1)}, bf16[16,80,512]{2,1,0:T(8,128)(2,1)}, u32[]{:S(2)}, u32[]{:S(2)}) collective-permute-start(bf16[16,80,512]{2,1,0:T(8,128)(2,1)} %slice.20), channel_id=1, source_target_pairs={{0,2},{2,4},{4,6},{6,8},{8,10},{10,12},{12,14},{14,0},{1,3},{3,5},... | collective-permute-start | bytes 3932168 | tf_op jit(solution)/shard_map/ppermute | solution.py:347
  96.3 11.4 %copy-start.5 = (bf16[640,640]{1,0:T(8,128)(2,1)}, bf16[640,640]{1,0:T(8,128)(2,1)S(1)}, u32[]{:S(2)}) copy-start(bf16[640,640]{1,0:T(8,128)(2,1)S(1)} %all_gather.6.own_ref) | copy-start | bytes 2457604
  96.3 10.3 %collective-permute-start.3 = (bf16[640,640]{1,0:T(8,128)(2,1)S(1)}, bf16[640,640]{1,0:T(8,128)(2,1)S(1)}, u32[]{:S(2)}, u32[]{:S(2)}) collective-permute-start(bf16[640,640]{1,0:T(8,128)(2,1)S(1)} %all_gather.6.own_ref), channel_id=1, source_target_pairs={{0,1},{1,0},{2,3},{3,2},{4,5},{5,4},{6,7},{7,6},{8,9},{9,8},{10,11... | collective-permute-start | bytes 2457608 | tf_op jit(solution)/shard_map/ppermute | solution.py:31
  106.6 1.3 copy-start.9
  106.6 1.1 copy-start.13
  107.9 26.8 %copy-start.1 = (bf16[16,112,512]{2,1,0:T(8,128)(2,1)S(1)}, bf16[16,112,512]{2,1,0:T(8,128)(2,1)}, u32[]{:S(2)}) copy-start(bf16[16,112,512]{2,1,0:T(8,128)(2,1)} %copy-done) | copy-start | bytes 5505028
  131.5 5.3 %collective-permute-start.6 = (bf16[1280,256]{1,0:T(8,128)(2,1)}, bf16[1280,256]{1,0:T(8,128)(2,1)}, u32[]{:S(2)}, u32[]{:S(2)}) collective-permute-start(bf16[1280,256]{1,0:T(8,128)(2,1)} %bitcast.10.ho_ref), channel_id=1, source_target_pairs={{0,1},{1,0},{2,3},{3,2},{4,5},{5,4},{6,7},{7,6},{8,9},{9,8},{10,11... | collective-permute-start | bytes 1966088 | tf_op jit(solution)/shard_map/ppermute | solution.py:31
  133.2 30.6 %collective-permute-start.8 = (bf16[16,80,512]{2,1,0:T(8,128)(2,1)}, bf16[16,80,512]{2,1,0:T(8,128)(2,1)S(1)}, u32[]{:S(2)}, u32[]{:S(2)}) collective-permute-start(bf16[16,80,512]{2,1,0:T(8,128)(2,1)} %copy-done.13), channel_id=1, source_target_pairs={{0,14},{2,0},{4,2},{6,4},{8,6},{10,8},{12,10},{14,12},{1,15},{3,1}... | collective-permute-start | bytes 3932168 | tf_op jit(solution)/shard_map/ppermute | solution.py:348
  133.2 31.8 %collective-permute-start.9 = (bf16[16,80,512]{2,1,0:T(8,128)(2,1)}, bf16[16,80,512]{2,1,0:T(8,128)(2,1)}, u32[]{:S(2)}, u32[]{:S(2)}) collective-permute-start(bf16[16,80,512]{2,1,0:T(8,128)(2,1)} %collective-permute-done.5.xd_ref), channel_id=1, source_target_pairs={{0,2},{2,4},{4,6},{6,8},{8,10},{10,12},{12,14},{14,0},{1,3},{3,5},... | collective-permute-start | bytes 3932168 | tf_op jit(solution)/shard_map/ppermute | solution.py:349
  134.8 2.0 collective-permute-start.7
  136.8 0.7 copy-start.8
  163.8 1.1 copy-start.7
  172.8 2.9 %collective-permute-start.10 = (bf16[1280,256]{1,0:T(8,128)(2,1)}, bf16[1280,256]{1,0:T(8,128)(2,1)S(1)}, u32[]{:S(2)}, u32[]{:S(2)}) collective-permute-start(bf16[1280,256]{1,0:T(8,128)(2,1)} %get-tuple-element.25), channel_id=1, source_target_pairs={{0,1},{1,0},{2,3},{3,2},{4,5},{5,4},{6,7},{7,6},{8,9},{9,8},{10,11... | collective-permute-start | bytes 1966088 | tf_op jit(solution)/shard_map/ppermute | solution.py:31
  175.7 6.7 %copy-start.2 = (bf16[16,112,512]{2,1,0:T(8,128)(2,1)S(1)}, bf16[16,112,512]{2,1,0:T(8,128)(2,1)}, u32[]{:S(2)}) copy-start(bf16[16,112,512]{2,1,0:T(8,128)(2,1)} %copy-done) | copy-start | bytes 5505028
  178.1 15.6 %all-to-all-start.3 = ((bf16[16,80,256]{2,1,0:T(8,128)(2,1)}), bf16[16,80,256]{2,1,0:T(8,128)(2,1)}, u32[]{:S(2)}, u32[]{:S(2)}) async-start(bf16[16,80,256]{2,1,0:T(8,128)(2,1)} %bitcast.12), calls=%async_computation.3 | async-start | bytes 1310720 | tf_op jit(solution)/shard_map/all_to_all | solution.py:365
  198.1 4.8 %collective-permute-start.11 = (bf16[320,1200]{1,0:T(8,128)(2,1)}, bf16[320,1200]{1,0:T(8,128)(2,1)S(1)}, u32[]{:S(2)}, u32[]{:S(2)}) collective-permute-start(bf16[320,1200]{1,0:T(8,128)(2,1)} %get-tuple-element.27), channel_id=1, source_target_pairs={{0,1},{1,0},{2,3},{3,2},{4,5},{5,4},{6,7},{7,6},{8,9},{9,8},{10,11... | collective-permute-start | bytes 2304008 | tf_op jit(solution)/shard_map/ppermute | solution.py:31
  205.4 3.7 %copy-start.11 = (f32[1200]{0:T(1024)S(1)}, f32[1200]{0:T(1024)}, u32[]{:S(2)}) copy-start(f32[1200]{0:T(1024)} %param.10) | copy-start | bytes 14404
  205.4 4.4 %copy-start.12 = (f32[8]{0:T(128)S(1)}, f32[8]{0:T(128)}, u32[]{:S(2)}) copy-start(f32[8]{0:T(128)} %param.11) | copy-start | bytes 100
  205.4 27.9 %all-to-all-start.4 = ((bf16[8,40,1200]{2,1,0:T(8,128)(2,1)}), bf16[8,40,1200]{2,1,0:T(8,128)(2,1)S(1)}, u32[]{:S(2)}, u32[]{:S(2)}) async-start(bf16[8,40,1200]{2,1,0:T(8,128)(2,1)} %bitcast.13), calls=%async_computation.4 | async-start | bytes 1638400 | tf_op jit(solution)/shard_map/all_to_all | solution.py:371
  233.3 0.9 copy-start.4
  257.7 8.3 %copy-start.3 = (bf16[320,1280]{1,0:T(8,128)(2,1)}, bf16[320,1280]{1,0:T(8,128)(2,1)S(1)}, u32[]{:S(2)}) copy-start(bf16[320,1280]{1,0:T(8,128)(2,1)S(1)} %all_gather.7.own_ref) | copy-start | bytes 2457604
  257.7 8.2 %collective-permute-start.12 = (bf16[320,1280]{1,0:T(8,128)(2,1)S(1)}, bf16[320,1280]{1,0:T(8,128)(2,1)S(1)}, u32[]{:S(2)}, u32[]{:S(2)}) collective-permute-start(bf16[320,1280]{1,0:T(8,128)(2,1)S(1)} %all_gather.7.own_ref), channel_id=1, source_target_pairs={{0,1},{1,0},{2,3},{3,2},{4,5},{5,4},{6,7},{7,6},{8,9},{9,8},{10,11... | collective-permute-start | bytes 2457608 | tf_op jit(solution)/shard_map/ppermute | solution.py:31
  266.0 0.9 copy-start.6
  268.8 9.9 %all-to-all-start.5 = ((f32[16,8,128]{2,1,0:T(8,128)}), f32[16,8,128]{2,1,0:T(8,128)S(1)}, u32[]{:S(2)}, u32[]{:S(2)}) async-start(f32[16,8,128]{2,1,0:T(8,128)} %broadcast_in_dim.11), calls=%async_computation.5 | async-start | bytes 131072 | tf_op jit(solution)/shard_map/all_to_all | solution.py:384

commit v6 on v2

v6 whole, which is shorter than its diff:
```python
import jax
import jax.numpy as jnp
from jax import lax
from jax.experimental import pallas as pl
from jax.experimental.pallas import tpu as pltpu
from jax.sharding import Mesh
from jax.sharding import PartitionSpec as P

AXES = ("x", "y", "z", "c")
XY = ("x", "y")
RANK = ("z", "c")
BF = jnp.bfloat16
F32 = jnp.float32
epsilon = 1e-06

NX, NY, NZ, NC = 4, 4, 8, 2
NV = NX * NY
PAIRS = 8
ROW = 75
PAD = 80
BLK = 512
QC = 32
NVIR = 1200
LANE = 128
HALF = PAD // 2
WIDE = 1280


def core_swap(value):
    return lax.ppermute(value, "c", [(0, 1), (1, 0)])


def ring(shift):
    return [(s, (s + shift) % NZ) for s in range(NZ)]


def regroup(tiles, want):
    out = None
    lane = lax.broadcasted_iota(jnp.int32, (PAD, LANE), 1) // QC
    for group, tile in enumerate(tiles):
        shift = ((group - want) * QC) % LANE
        moved = pltpu.roll(tile, shift, 1) if shift else tile
        out = moved if out is None else jnp.where(lane == group, moved, out)
    return out


ORDER = (0, 1, NZ - 1, 2, 3, 4, 5, 6)
NEAR = 3
HALF_M = PAIRS * QC


def level_of(step, place):
    far = jnp.where(step == 2, NZ - 1, jnp.where(step > 2, step - 1, step))
    return (place[1] + far) % NZ


def x_specs():
    whole = pl.BlockSpec((NV, PAD, BLK), lambda k, p: (0, 0, 0))
    return [
        pl.BlockSpec((NV, PAD + QC, BLK), lambda k, p: (0, 0, 0)),
        whole,
        whole,
        pl.BlockSpec((NV, 1, PAD, BLK), lambda k, p: (0, jnp.maximum(k - NEAR, 0), 0, 0)),
    ]


def with_block(step, xq_ref, xu_ref, xd_ref, x_ref, body):
    @pl.when(step == 0)
    def _():
        body(xq_ref[:, :PAD, :].reshape(NV * PAD, BLK))

    @pl.when(step == 1)
    def _():
        body(xu_ref[...].reshape(NV * PAD, BLK))

    @pl.when(step == 2)
    def _():
        body(xd_ref[...].reshape(NV * PAD, BLK))

    @pl.when(step > 2)
    def _():
        body(x_ref[...].reshape(NV * PAD, BLK))


def half_kernel(place_ref, to_ref, tx_ref, xq_ref, xu_ref, xd_ref, x_ref, out_ref, t_ref, tt_ref, acc_ref):
    step = pl.program_id(0)
    core, level = place_ref[0], place_ref[1]

    @pl.when(step == 0)
    def _():
        for j in range(NZ):
            rank = 2 * ((level + NZ - j) % NZ)
            own = pl.multiple_of((rank + core) * PAD, PAD)
            oth = pl.multiple_of((rank + 1 - core) * PAD, PAD)
            t_ref[pl.ds(own, PAD), :] = to_ref[j].astype(F32)
            t_ref[pl.ds(oth, PAD), :] = tx_ref[j].astype(F32)
        tt_ref[...] = t_ref[...].T.astype(BF)

    def body(x):
        acc_ref[level_of(step, place_ref)] = jnp.dot(
            tt_ref[...], x, preferred_element_type=F32
        )

    with_block(step, xq_ref, xu_ref, xd_ref, x_ref, body)

    @pl.when(step == NZ - 1)
    def _():
        for xx in range(NX):
            for half in range(2):
                tiles = [acc_ref[half * 4 + g, :, pl.ds(xx * LANE, LANE)] for g in range(4)]
                for yy in range(NY):
                    out_ref[xx * NY + yy, :, pl.ds(half * LANE, LANE)] = regroup(
                        tiles, yy
                    ).astype(BF)


def make_half(place, t_own, t_oth, xs):
    piece = pl.BlockSpec((NZ, PAD, PAD), lambda k, p: (0, 0, 0))
    return pl.pallas_call(
        half_kernel,
        out_shape=jax.ShapeDtypeStruct((NV, PAD, HALF_M), BF),
        grid_spec=pltpu.PrefetchScalarGridSpec(
            num_scalar_prefetch=1,
            grid=(NZ,),
            in_specs=[piece, piece] + x_specs(),
            out_specs=pl.BlockSpec((NV, PAD, HALF_M), lambda k, p: (0, 0, 0)),
            scratch_shapes=[
                pltpu.VMEM((NV * PAD, PAD), F32),
                pltpu.VMEM((PAD, NV * PAD), BF),
                pltpu.VMEM((NZ, PAD, BLK), F32),
            ],
        ),
        compiler_params=pltpu.CompilerParams(dimension_semantics=("arbitrary",)),
        name="half",
    )(place, t_own, t_oth, *xs)


def main_kernel(
    place_ref, ho_ref, hx_ref, xq_ref, xu_ref, xd_ref, x_ref, *rest
):
    pieces, (bo_ref, bx_ref, h_ref, z_ref, acc_ref) = rest[:-5], rest[-5:]
    step = pl.program_id(0)
    level = place_ref[1]

    @pl.when(step == 0)
    def _():
        h_ref[pl.ds(0, HALF_M), :] = ho_ref[...].astype(F32).T.astype(BF)
        h_ref[pl.ds(HALF_M, HALF_M), :] = hx_ref[...].astype(F32).T.astype(BF)
        acc_ref[...] = jnp.zeros_like(acc_ref)

    for (far, first, count), ref in zip(Z_PARTS, pieces):
        start = ((level + far) % NZ) * QC
        for j in range(count):
            at = pl.multiple_of((first + j) * HALF_M + start, QC)
            z_ref[pl.ds(at, QC), :] = ref[j, 0].astype(F32)

    def body(x):
        coupled = jnp.dot(h_ref[...], x, preferred_element_type=F32)
        w = (coupled * z_ref[...]).astype(BF)
        acc_ref[...] += lax.dot_general(
            x, w, (((1,), (1,)), ((), ())), preferred_element_type=F32
        )

    with_block(step, xq_ref, xu_ref, xd_ref, x_ref, body)

    @pl.when(step == NZ - 1)
    def _():
        bo_ref[...] = acc_ref[:, :HALF_M]
        bx_ref[...] = acc_ref[:, HALF_M:].astype(BF)


Z_PARTS = (
    (0, 0, 2),
    (1, 0, 2),
    (2, 0, 2),
    (3, 0, 2),
    (7, 0, 2),
    (6, 0, 2),
    (5, 0, 2),
    (4, 0, 1),
    (4, 1, 1),
)


def make_main(place, h_own, h_oth, xs, z_pieces):
    rows = NV * PAD

    def z_spec(count):
        return pl.BlockSpec((count, 1, QC, BLK), lambda k, p: (0, level_of(k, p), 0, 0))

    flat = pl.BlockSpec((rows, HALF_M), lambda k, p: (0, 0))
    return pl.pallas_call(
        main_kernel,
        out_shape=(
            jax.ShapeDtypeStruct((rows, HALF_M), F32),
            jax.ShapeDtypeStruct((rows, HALF_M), BF),
        ),
        grid_spec=pltpu.PrefetchScalarGridSpec(
            num_scalar_prefetch=1,
            grid=(NZ,),
            in_specs=[flat, flat] + x_specs() + [z_spec(part[2]) for part in Z_PARTS],
            out_specs=(flat, flat),
            scratch_shapes=[
                pltpu.VMEM((2 * HALF_M, rows), BF),
                pltpu.VMEM((2 * HALF_M, BLK), F32),
                pltpu.VMEM((rows, 2 * HALF_M), F32),
            ],
        ),
        compiler_params=pltpu.CompilerParams(dimension_semantics=("arbitrary",)),
        cost_estimate=pl.CostEstimate(
            flops=4 * 512 * 1280 * 4096, bytes_accessed=18_000_000, transcendentals=0
        ),
        name="core",
    )(place, h_own, h_oth, *xs, *z_pieces)


def ladder_kernel(
    place_ref, b_ref, xq_ref, xu_ref, xd_ref, x_ref, own_ref, oth_ref, g_ref, acc_ref
):
    step = pl.program_id(0)

    @pl.when(step == 0)
    def _():
        for xx in range(NX):
            for half in range(2):
                tiles = [
                    b_ref[xx * NY + yy, :, pl.ds(half * LANE, LANE)].astype(F32)
                    for yy in range(NY)
                ]
                for g in range(4):
                    g_ref[half * 4 + g, :, pl.ds(xx * LANE, LANE)] = regroup(tiles, g).astype(BF)
        acc_ref[...] = jnp.zeros_like(acc_ref)

    def body(x):
        acc_ref[...] += lax.dot_general(
            g_ref[level_of(step, place_ref)],
            x,
            (((1,), (1,)), ((), ())),
            preferred_element_type=F32,
        )

    with_block(step, xq_ref, xu_ref, xd_ref, x_ref, body)

    @pl.when(step == NZ - 1)
    def _():
        core = place_ref[0]
        own_ref[...] = acc_ref[pl.ds(pl.multiple_of(core * HALF, HALF), HALF), :]
        oth_ref[...] = acc_ref[pl.ds(pl.multiple_of((1 - core) * HALF, HALF), HALF), :]


def make_ladder(place, b_all, xs):
    flat = pl.BlockSpec((HALF, WIDE), lambda k, p: (0, 0))
    return pl.pallas_call(
        ladder_kernel,
        out_shape=(
            jax.ShapeDtypeStruct((HALF, WIDE), F32),
            jax.ShapeDtypeStruct((HALF, WIDE), F32),
        ),
        grid_spec=pltpu.PrefetchScalarGridSpec(
            num_scalar_prefetch=1,
            grid=(NZ,),
            in_specs=[pl.BlockSpec((NV, PAD, HALF_M), lambda k, p: (0, 0, 0))] + x_specs(),
            out_specs=(flat, flat),
            scratch_shapes=[
                pltpu.VMEM((NZ, PAD, BLK), BF),
                pltpu.VMEM((PAD, WIDE), F32),
            ],
        ),
        compiler_params=pltpu.CompilerParams(dimension_semantics=("arbitrary",)),
        name="ladder",
    )(place, b_all, *xs)


def chunk_kernel(place_ref, own_ref, oth_ref, other_ref, col_ref, low_ref, out_ref):
    wide = own_ref[...] + oth_ref[...]
    lane = lax.broadcasted_iota(jnp.int32, (HALF, WIDE), 1)
    row = lax.broadcasted_iota(jnp.int32, (HALF, WIDE), 0)
    total = wide
    for v in range(1, NV):
        moved = pltpu.roll(wide, WIDE - v * (PAD - ROW), 1)
        total = jnp.where(lane >= v * ROW, moved, total)
    res = total[:, :NVIR] + other_ref[...]
    upd = res / (low_ref[...] + col_ref[...])
    real = row[:, :NVIR] + place_ref[0] * HALF < ROW
    upd = jnp.where(real, upd, 0.0)
    squares = jnp.sum(upd * upd, axis=1, keepdims=True)
    squares = jnp.sum(squares, axis=0, keepdims=True)
    high = squares.astype(BF).astype(F32)
    rest = squares - high
    mid = rest.astype(BF).astype(F32)
    low = rest - mid
    kept = jnp.where(lane == NVIR, high, jnp.where(lane == NVIR + 1, mid, low))
    kept = jnp.where((row == 0) & (lane < NVIR + 3), kept, 0.0)
    out_ref[...] = jnp.where(lane < NVIR, total, kept).astype(BF)


def make_chunk(place, own, oth, other_part, col_energy, low_energy):
    return pl.pallas_call(
        chunk_kernel,
        out_shape=jax.ShapeDtypeStruct((HALF, WIDE), BF),
        in_specs=[pl.BlockSpec(memory_space=pltpu.SMEM)]
        + [pl.BlockSpec(memory_space=pltpu.VMEM)] * 5,
        name="chunk",
    )(place, own, oth, other_part, col_energy, low_energy)


def final_kernel(place_ref, own_ref, oth_ref, other_ref, out_ref, mix_ref):
    def fill(source, start, count):
        for t in range(WIDE // LANE):
            lanes = min(LANE, NVIR - t * LANE)
            for i in range(PAIRS):
                mix_ref[t, pl.ds(i, HALF, stride=PAIRS), :] = source[
                    i, :, pl.ds(t * LANE, LANE)
                ].astype(F32)
            part = mix_ref[t, : count * PAIRS, :lanes].reshape(count, PAIRS, lanes)
            at = (pl.ds(start, count), slice(None), pl.ds(t * LANE, lanes))
            out_ref[at] = other_ref[at] + part

    @pl.when(place_ref[0] == 0)
    def _():
        fill(own_ref, 0, HALF)
        fill(oth_ref, HALF, ROW - HALF)

    @pl.when(place_ref[0] == 1)
    def _():
        fill(oth_ref, 0, HALF)
        fill(own_ref, HALF, ROW - HALF)


def make_final(place, l_own, l_oth, other_rows):
    return pl.pallas_call(
        final_kernel,
        out_shape=jax.ShapeDtypeStruct((ROW, PAIRS, NVIR), F32),
        in_specs=[pl.BlockSpec(memory_space=pltpu.SMEM)]
        + [pl.BlockSpec(memory_space=pltpu.VMEM)] * 3,
        scratch_shapes=[pltpu.VMEM((WIDE // LANE, HALF * PAIRS, LANE), F32)],
        name="residual",
    )(place, l_own, l_oth, other_rows)


def shards(amplitudes, factors, kernel, other_terms, virt_energy, pair_energy):
    core = lax.axis_index("c").astype(jnp.int32)
    level = lax.axis_index("z").astype(jnp.int32)
    place = jnp.stack([core, level])

    x_pad = jnp.pad(factors, ((0, PAD - ROW), (0, 0)))
    z_cols = kernel.T.reshape(NV, QC, BLK)
    xz = jnp.concatenate([jnp.broadcast_to(x_pad[None], (NV, PAD, BLK)), z_cols], axis=1)
    x_pad, xz = lax.optimization_barrier((x_pad, xz))
    xz = lax.all_to_all(xz, XY, split_axis=0, concat_axis=0, tiled=True)
    x_far = jnp.stack([lax.ppermute(x_pad, "z", ring(-j)) for j in ORDER[NEAR:]])
    x_all = lax.all_to_all(
        jnp.broadcast_to(x_far[None], (NV, *x_far.shape)),
        XY,
        split_axis=0,
        concat_axis=0,
        tiled=True,
    )
    x_own = xz[:, :PAD]
    x_up = lax.ppermute(x_own, "z", ring(-1))
    x_down = lax.ppermute(x_own, "z", ring(1))
    xs = (xz, x_up, x_down, x_all)

    z_all = xz.reshape(NZ, NC, PAD + QC, BLK)
    z_own = lax.dynamic_index_in_dim(z_all, core, 1, keepdims=False)[:, PAD:]
    z_oth = lax.dynamic_index_in_dim(z_all, 1 - core, 1, keepdims=False)[:, PAD:]
    z_here = jnp.stack([z_own, core_swap(z_oth)])
    ups, downs = [z_here], [z_here]
    for _ in range(3):
        ups.append(lax.ppermute(ups[-1], "z", ring(-1)))
        downs.append(lax.ppermute(downs[-1], "z", ring(1)))
    last_up = lax.ppermute(ups[-1][:1], "z", ring(-1))
    last_down = lax.ppermute(downs[-1][1:], "z", ring(1))
    z_pieces = (*ups, *downs[1:], last_up, last_down)

    t_cols = jnp.pad(amplitudes, ((0, 0), (0, PAD - ROW), (0, PAD - ROW)))
    t_cols = jnp.transpose(t_cols, (0, 2, 1))
    t_cols = lax.dynamic_slice_in_dim(jnp.concatenate([t_cols, t_cols]), level, NZ, 0)
    t_own = jnp.stack(
        [t_cols[0]] + [lax.ppermute(t_cols[j], "z", ring(j)) for j in range(1, NZ)]
    )
    t_oth = core_swap(t_own)

    h_msg = make_half(place, t_own, t_oth, xs)
    h_own = lax.all_to_all(h_msg, XY, split_axis=0, concat_axis=0, tiled=True)
    h_own = h_own.reshape(NV * PAD, HALF_M)
    h_oth = core_swap(h_own)

    b_own, b_send = make_main(place, h_own, h_oth, xs, z_pieces)
    b_sum = (b_own + core_swap(b_send).astype(F32)).astype(BF)
    b_all = lax.all_to_all(
        b_sum.reshape(NV, PAD, HALF_M), XY, split_axis=0, concat_axis=0, tiled=True
    )

    l_own, l_send = make_ladder(place, b_all, xs)
    l_recv = core_swap(l_send)
    other_part = lax.dynamic_index_in_dim(other_terms, level, 0, keepdims=False)
    other_part = jnp.pad(other_part, ((0, PAD - ROW), (0, 0)))
    other_part = lax.dynamic_slice_in_dim(other_part, core * HALF, HALF, 0)
    row_energy = lax.dynamic_slice_in_dim(virt_energy, lax.axis_index(XY) * ROW, ROW, 0)
    low_energy = jnp.pad(row_energy, (0, PAD - ROW), constant_values=1.0)
    low_energy = lax.dynamic_slice_in_dim(low_energy, core * HALF, HALF, 0)
    low_energy = (low_energy - lax.dynamic_index_in_dim(pair_energy, level, 0))[:, None]
    chunk = make_chunk(place, l_own, l_recv, other_part, virt_energy[None, :], low_energy)
    l_mine = lax.all_gather(chunk, "z", axis=0)
    l_rest = core_swap(l_mine)

    marks = jnp.concatenate([l_mine, l_rest])
    squares = jnp.sum(marks[:, 0, NVIR : NVIR + 3].astype(F32))
    total = jnp.broadcast_to(squares, (NV, 8, LANE))
    totals = lax.all_to_all(total, XY, split_axis=0, concat_axis=0, tiled=True)
    other_rows = jnp.transpose(other_terms, (1, 0, 2))
    residual = jnp.transpose(make_final(place, l_mine, l_rest, other_rows), (1, 0, 2))
    count = PAIRS * NVIR * NVIR
    update_rms = jnp.sqrt(jnp.sum(totals[:, 0, 0]) / count + epsilon)
    return residual, update_rms


def solution(mesh):
    torus = Mesh(mesh.devices.reshape(NX, NY, NZ, NC), AXES)
    return jax.shard_map(
        shards,
        mesh=torus,
        in_specs=(
            P(None, XY, RANK),
            P(XY, RANK),
            P(XY, RANK),
            P(None, XY, None),
            P(),
            P(),
        ),
        out_specs=(P(None, XY, None), P()),
        check_vma=False,
    )
```

time: 272 us -> 298 us (1.096)
  starting transfers between devices: 55.5 us -> 126 us
  blocking collectives: 68.4 us -> 20.6 us
  Pallas kernels: 34.3 us -> 50 us
  between operations: 16 us -> 2.82 us
  local copies, waits for them, and re-layouts: 11 us -> 15.8 us
    ppermute x7 -> x22, starting transfers between devices: 16.1 us -> 69.7 us  [the longest x3 21 us: shards(): downs.append(lax.ppermute(downs[-1], 'z', ring(1)))]
    ppermute x7 -> x22, waiting for transfers between devices: 11.8 us -> 45.3 us  [the longest x7 25.6 us: shards(): lax.ppermute(t_cols[j], 'z', ring(j))]
    all_to_all x1 -> x0, blocking collectives: 25.6 us -> none  [shards(): h_own = lax.all_to_all(h_msg, XY, split_axis=0, concat_axis=0, tiled=True)]
    all_gather x2 -> x1, blocking collectives: 42.9 us -> 20.6 us  [shards(): l_mine = lax.all_gather(chunk, 'z', axis=0)]
    all_gather x1 -> x0, waiting for transfers between devices: 21.6 us -> none  [shards(): x_all = lax.all_gather(x_far, XY, axis=0)]
    pallas_call x4, Pallas kernels: 30 us -> 45 us  [the longest x1 21.7 us: make_main(): pl.pallas_call(main_kernel, out_shape=(jax.ShapeDtypeStruct((rows, HALF_M...]
    all_to_all x2 -> x3, waiting for transfers between devices: 32.7 us -> 20.6 us  [the longest x1 14 us: shards(): lax.all_to_all(jnp.broadcast_to(x_far[None], (NV, *x_far.shape)), XY, spl...]
    all_to_all x2 -> x3, starting transfers between devices: 9.96 us -> 21.1 us  [the longest x1 9.02 us: shards(): h_own = lax.all_to_all(h_msg, XY, split_axis=0, concat_axis=0, tiled=True)]
  transfers between devices with their start and end apart: 18 -> 33, of which waited for: 14 -> 14; matrix products, arithmetic and copies ran while one was open for 3% -> 2% of each run, Pallas kernels for 3% -> 5%
where the time goes in v6:
time: 298 us; the launch traced here: 297 us
  starting transfers between devices  126 us (42%)
  waiting for transfers between devices  74.7 us (25%)
  Pallas kernels  50 us (17%)
  blocking collectives  20.6 us (7%)
  local copies, waits for them, and re-layouts  15.8 us (5%)
  other arithmetic  6.77 us (2%)
    ppermute x7, waiting for transfers between devices, shards(): lax.ppermute(t_cols[j], 'z', ring(j))  25.6 us
    ppermute x6, starting transfers between devices, core_swap(): return lax.ppermute(value, 'c', [(0, 1), (1, 0)])  24.6 us
    pallas_call x1, Pallas kernels, make_main(): pl.pallas_call(main_kernel, out_shape=(jax.ShapeDtypeStruct((rows, HALF_M...  21.7 us
    ppermute x3, starting transfers between devices, shards(): downs.append(lax.ppermute(downs[-1], 'z', ring(1)))  21 us
    all_gather x1, blocking collectives, shards(): l_mine = lax.all_gather(chunk, 'z', axis=0)  20.6 us
    ppermute x7, starting transfers between devices, shards(): lax.ppermute(t_cols[j], 'z', ring(j))  18.5 us
    all_to_all x1, waiting for transfers between devices, shards(): lax.all_to_all(jnp.broadcast_to(x_far[None], (NV, *x_far.shape)), XY, spl...  14 us
    ppermute x5, starting transfers between devices, shards(): lax.ppermute(x_pad, 'z', ring(-j))  13.8 us
  transfers between devices with their start and end apart: 33, of which 14 were waited for; matrix products, arithmetic and copies ran while one was open for 2% of the time, Pallas kernels for 5%

profile of v6, /device:TPU:1, one launch (start us, length us, event | category | flops | bytes accessed | tf_op | source)
XLA Modules:
  0.0 297.2 jit_solution(10978052534086764182)
XLA Ops:
  4.3 7.6 %all-to-all-start = ((bf16[16,112,512]{2,1,0:T(8,128)(2,1)}), bf16[16,112,512]{2,1,0:T(8,128)(2,1)S(1)}, u32[]{:S(2)}, u32[]{:S(2)}) async-start(bf16[16,112,512]{2,1,0:T(8,128)(2,1)} %pad_maximum_fusion), calls=%async_computation | async-start | bytes 3670016 | tf_op jit(solution)/shard_map/all_to_all | solution.py:350
  11.9 6.1 %collective-permute-start.10 = (bf16[80,512]{1,0:T(8,128)(2,1)S(1)}, bf16[80,512]{1,0:T(8,128)(2,1)S(1)}, u32[]{:S(2)}, u32[]{:S(2)}) collective-permute-start(bf16[80,512]{1,0:T(8,128)(2,1)S(1)} %pad.17), channel_id=1, source_target_pairs={{0,12},{2,14},{4,0},{6,2},{8,4},{10,6},{12,8},{14,10},{1,13},{3,15... | collective-permute-start | bytes 245768 | tf_op jit(solution)/shard_map/ppermute | solution.py:351
  18.7 4.2 %collective-permute-start.12 = (bf16[80,512]{1,0:T(8,128)(2,1)S(1)}, bf16[80,512]{1,0:T(8,128)(2,1)S(1)}, u32[]{:S(2)}, u32[]{:S(2)}) collective-permute-start(bf16[80,512]{1,0:T(8,128)(2,1)S(1)} %pad.17), channel_id=1, source_target_pairs={{0,8},{2,10},{4,12},{6,14},{8,0},{10,2},{12,4},{14,6},{1,9},{3,11}... | collective-permute-start | bytes 245768 | tf_op jit(solution)/shard_map/ppermute | solution.py:351
  22.9 2.8 collective-permute-start.14
  27.1 6.1 %collective-permute-done.13 = bf16[80,512]{1,0:T(8,128)(2,1)S(1)} collective-permute-done((bf16[80,512]{1,0:T(8,128)(2,1)S(1)}, bf16[80,512]{1,0:T(8,128)(2,1)S(1)}, u32[]{:S(2)}, u32[]{:S(2)}) %collective-permute-start.13) | collective-permute-done | bytes 81952 | tf_op jit(solution)/shard_map/ppermute | solution.py:351
  36.1 3.6 %broadcast_in_dim.22 = bf16[16,5,80,512]{3,2,1,0:T(8,128)(2,1)} broadcast(bf16[5,80,512]{2,1,0:T(8,128)(2,1)S(1)} %bitcast_dynamic-update-slice_fusion), dimensions={1,2,3} | broadcast | bytes 6963200 | tf_op jit(solution)/shard_map/broadcast_in_dim | solution.py:353
  39.7 5.0 %all-to-all-start.1 = ((bf16[16,5,80,512]{3,2,1,0:T(8,128)(2,1)}), bf16[16,5,80,512]{3,2,1,0:T(8,128)(2,1)}, u32[]{:S(2)}, u32[]{:S(2)}) async-start(bf16[16,5,80,512]{3,2,1,0:T(8,128)(2,1)} %broadcast_in_dim.22), calls=%async_computation.1 | async-start | bytes 13107200 | tf_op jit(solution)/shard_map/all_to_all | solution.py:352
  45.1 3.4 %collective-permute-start = (bf16[80,80]{1,0:T(8,128)(2,1)S(1)}, bf16[80,80]{1,0:T(8,128)(2,1)S(1)}, u32[]{:S(2)}, u32[]{:S(2)}) collective-permute-start(bf16[80,80]{1,0:T(8,128)(2,1)S(1)} %get-tuple-element.22), channel_id=1, source_target_pairs={{0,2},{2,4},{4,6},{6,8},{8,10},{10,12},{12,14},{14,0},{1,3},{3,5},... | collective-permute-start | bytes 38408 | tf_op jit(solution)/shard_map/ppermute | solution.py:380
  50.8 2.8 collective-permute-start.2
  54.0 4.5 %collective-permute-start.4 = (bf16[80,80]{1,0:T(8,128)(2,1)S(1)}, bf16[80,80]{1,0:T(8,128)(2,1)S(1)}, u32[]{:S(2)}, u32[]{:S(2)}) collective-permute-start(bf16[80,80]{1,0:T(8,128)(2,1)S(1)} %get-tuple-element.18), channel_id=1, source_target_pairs={{0,10},{2,12},{4,14},{6,0},{8,2},{10,4},{12,6},{14,8},{1,11},{3,13... | collective-permute-start | bytes 38408 | tf_op jit(solution)/shard_map/ppermute | solution.py:380
  62.7 6.2 %collective-permute-start.16 = (bf16[8,32,512]{2,1,0:T(8,128)(2,1)S(1)}, bf16[8,32,512]{2,1,0:T(8,128)(2,1)S(1)}, u32[]{:S(2)}, u32[]{:S(2)}) collective-permute-start(bf16[8,32,512]{2,1,0:T(8,128)(2,1)S(1)} %slice.70), channel_id=1, source_target_pairs={{0,1},{1,0},{2,3},{3,2},{4,5},{5,4},{6,7},{7,6},{8,9},{9,8},{10,11... | collective-permute-start | bytes 786440 | tf_op jit(solution)/shard_map/ppermute | solution.py:30
  72.2 2.7 collective-permute-start.6
  74.9 25.6 %collective-permute-done.6 = bf16[80,80]{1,0:T(8,128)(2,1)S(1)} collective-permute-done((bf16[80,80]{1,0:T(8,128)(2,1)S(1)}, bf16[80,80]{1,0:T(8,128)(2,1)S(1)}, u32[]{:S(2)}, u32[]{:S(2)}) %collective-permute-start.6) | collective-permute-done | bytes 12832 | tf_op jit(solution)/shard_map/ppermute | solution.py:380
  100.5 4.9 %collective-permute-start.7 = (bf16[8,80,80]{2,1,0:T(8,128)(2,1)S(1)}, bf16[8,80,80]{2,1,0:T(8,128)(2,1)S(1)}, u32[]{:S(2)}, u32[]{:S(2)}) collective-permute-start(bf16[8,80,80]{2,1,0:T(8,128)(2,1)S(1)} %constant_dynamic-update-slice_fusion.to_ref), channel_id=1, source_target_pairs={{0,1},{1,0},{2,3},{3,2},{4,5},{5,4},{6,7},{7,6},{8,9},{9,8},{10,11... | collective-permute-start | bytes 307208 | tf_op jit(solution)/shard_map/ppermute | solution.py:30
  108.1 14.0 %all-to-all-done.1.x_ref = bf16[16,5,80,512]{3,2,1,0:T(8,128)(2,1)} async-done(((bf16[16,5,80,512]{3,2,1,0:T(8,128)(2,1)}), bf16[16,5,80,512]{3,2,1,0:T(8,128)(2,1)}, u32[]{:S(2)}, u32[]{:S(2)}) %all-to-all-start.1) | async-done | bytes 6553632 | tf_op jit(solution)/shard_map/all_to_all | solution.py:352
  122.1 10.1 %half.1 = bf16[16,80,256]{2,1,0:T(8,128)(2,1)} custom-call(s32[2]{0:T(128)} %pad_add_fusion.place_ref, bf16[8,80,80]{2,1,0:T(8,128)(2,1)} %copy-done.7, bf16[8,80,80]{2,1,0:T(8,128)(2,1)} %copy-done.9, bf16[16,112,512]{2,1,0:T(8,128)(2,1)} %copy-done, bf16[16,80,512]{2,1,0:T(8,128)(2,1)} %copy-done.2, bf16[16,80,512]{2,1,0:T(8,128)(2,1)} %collective-permute-done.9.xd_ref, ...), custom_call_target="tpu_custom_call" | custom-call | tf_op jit(solution)/shard_map/half/pallas_call | solution.py:119
  132.2 9.0 %all-to-all-start.2 = ((bf16[16,80,256]{2,1,0:T(8,128)(2,1)}), bf16[16,80,256]{2,1,0:T(8,128)(2,1)S(1)}, u32[]{:S(2)}, u32[]{:S(2)}) async-start(bf16[16,80,256]{2,1,0:T(8,128)(2,1)} %half.1), calls=%async_computation.2 | async-start | bytes 1310720 | tf_op jit(solution)/shard_map/all_to_all | solution.py:385
  141.2 5.7 %collective-permute-start.19 = (bf16[2,8,32,512]{3,2,1,0:T(8,128)(2,1)}, bf16[2,8,32,512]{3,2,1,0:T(8,128)(2,1)S(1)}, u32[]{:S(2)}, u32[]{:S(2)}) collective-permute-start(bf16[2,8,32,512]{3,2,1,0:T(8,128)(2,1)} %collective-permute-done.18.rest_2_), channel_id=1, source_target_pairs={{0,14},{2,0},{4,2},{6,4},{8,6},{10,8},{12,10},{14,12},{1,15},{3,1}... | collective-permute-start | bytes 1572872 | tf_op jit(solution)/shard_map/ppermute | solution.py:370
  146.9 21.0 %collective-permute-start.22 = (bf16[2,8,32,512]{3,2,1,0:T(8,128)(2,1)}, bf16[2,8,32,512]{3,2,1,0:T(8,128)(2,1)S(1)}, u32[]{:S(2)}, u32[]{:S(2)}) collective-permute-start(bf16[2,8,32,512]{3,2,1,0:T(8,128)(2,1)} %collective-permute-done.21.rest_5_), channel_id=1, source_target_pairs={{0,2},{2,4},{4,6},{6,8},{8,10},{10,12},{12,14},{14,0},{1,3},{3,5},... | collective-permute-start | bytes 1572872 | tf_op jit(solution)/shard_map/ppermute | solution.py:371
  167.9 3.6 %collective-permute-start.15 = (bf16[1280,256]{1,0:T(8,128)(2,1)S(1)}, bf16[1280,256]{1,0:T(8,128)(2,1)S(1)}, u32[]{:S(2)}, u32[]{:S(2)}) collective-permute-start(bf16[1280,256]{1,0:T(8,128)(2,1)S(1)} %bitcast.71), channel_id=1, source_target_pairs={{0,1},{1,0},{2,3},{3,2},{4,5},{5,4},{6,7},{7,6},{8,9},{9,8},{10,11... | collective-permute-start | bytes 1966088 | tf_op jit(solution)/shard_map/ppermute | solution.py:30
  171.5 5.5 %collective-permute-done.19.rest_3_ = bf16[2,8,32,512]{3,2,1,0:T(8,128)(2,1)S(1)} collective-permute-done((bf16[2,8,32,512]{3,2,1,0:T(8,128)(2,1)}, bf16[2,8,32,512]{3,2,1,0:T(8,128)(2,1)S(1)}, u32[]{:S(2)}, u32[]{:S(2)}) %collective-permute-start.19) | collective-permute-done | bytes 524320 | tf_op jit(solution)/shard_map/ppermute | solution.py:370
  177.2 5.1 %collective-permute-start.24 = (bf16[1,8,32,512]{3,2,1,0:T(8,128)(2,1)S(1)}, bf16[1,8,32,512]{3,2,1,0:T(8,128)(2,1)S(1)}, u32[]{:S(2)}, u32[]{:S(2)}) collective-permute-start(bf16[1,8,32,512]{3,2,1,0:T(8,128)(2,1)S(1)} %slice.72), channel_id=1, source_target_pairs={{0,2},{2,4},{4,6},{6,8},{8,10},{10,12},{12,14},{14,0},{1,3},{3,5},... | collective-permute-start | bytes 786440 | tf_op jit(solution)/shard_map/ppermute | solution.py:373
  182.3 5.5 %collective-permute-done.23.rest_7_ = bf16[1,8,32,512]{3,2,1,0:T(8,128)(2,1)S(1)} collective-permute-done((bf16[1,8,32,512]{3,2,1,0:T(8,128)(2,1)S(1)}, bf16[1,8,32,512]{3,2,1,0:T(8,128)(2,1)S(1)}, u32[]{:S(2)}, u32[]{:S(2)}) %collective-permute-start.23) | collective-permute-done | bytes 262176 | tf_op jit(solution)/shard_map/ppermute | solution.py:372
  189.4 21.7 %core.1 = (f32[1280,256]{1,0:T(8,128)}, bf16[1280,256]{1,0:T(8,128)(2,1)}) custom-call(s32[2]{0:T(128)} %pad_add_fusion.place_ref, bf16[1280,256]{1,0:T(8,128)(2,1)} %bitcast.72, bf16[1280,256]{1,0:T(8,128)(2,1)} %copy-done.14, bf16[16,112,512]{2,1,0:T(8,128)(2,1)} %copy-done, bf16[16,80,512]{2,1,0:T(8,128)(2,1)} %copy-done.2, ...), custom_call_target="tpu_custom_call" | custom-call | flops 10737418240 | bytes 18000000 | tf_op jit(solution)/shard_map/core/pallas_call | solution.py:192
  214.6 2.4 add_convert_fusion
  217.0 7.1 %all-to-all-start.3 = ((bf16[16,80,256]{2,1,0:T(8,128)(2,1)}), bf16[16,80,256]{2,1,0:T(8,128)(2,1)S(1)}, u32[]{:S(2)}, u32[]{:S(2)}) async-start(bf16[16,80,256]{2,1,0:T(8,128)(2,1)} %bitcast.30), calls=%async_computation.3 | async-start | bytes 1310720 | tf_op jit(solution)/shard_map/all_to_all | solution.py:391
  229.0 6.6 %all-to-all-done.3.b_ref = bf16[16,80,256]{2,1,0:T(8,128)(2,1)S(1)} async-done(((bf16[16,80,256]{2,1,0:T(8,128)(2,1)}), bf16[16,80,256]{2,1,0:T(8,128)(2,1)S(1)}, u32[]{:S(2)}, u32[]{:S(2)}) %all-to-all-start.3) | async-done | bytes 655392 | tf_op jit(solution)/shard_map/all_to_all | solution.py:391
  236.4 11.1 %ladder.1 = (f32[40,1280]{1,0:T(8,128)}, f32[40,1280]{1,0:T(8,128)}) custom-call(s32[2]{0:T(128)} %pad_add_fusion.place_ref, bf16[16,80,256]{2,1,0:T(8,128)(2,1)} %copy-done.4, bf16[16,112,512]{2,1,0:T(8,128)(2,1)} %copy-done, bf16[16,80,512]{2,1,0:T(8,128)(2,1)} %copy-done.2, bf16[16,80,512]{2,1,0:T(8,128)(2,1)} %collective-permute-done.9.xd_ref, ...), custom_call_target="tpu_custom_call" | custom-call | tf_op jit(solution)/shard_map/ladder/pallas_call | solution.py:253
  254.0 20.6 %all-gather = bf16[320,1280]{1,0:T(8,128)(2,1)S(1)} all-gather(bf16[40,1280]{1,0:T(8,128)(2,1)} %chunk.1), channel_id=2, replica_groups=mesh['x'=4,'y'=4,'z'=8,'c'=2] {'z'}, dimensions={0}, use_global_device_ids=true | all-gather | bytes 921600 | tf_op jit(solution)/shard_map/all_gather | solution.py:405
  274.6 6.1 %collective-permute-start.27 = (bf16[8,40,1280]{2,1,0:T(8,128)(2,1)S(1)}, bf16[8,40,1280]{2,1,0:T(8,128)(2,1)S(1)}, u32[]{:S(2)}, u32[]{:S(2)}) collective-permute-start(bf16[8,40,1280]{2,1,0:T(8,128)(2,1)S(1)} %bitcast.64), channel_id=1, source_target_pairs={{0,1},{1,0},{2,3},{3,2},{4,5},{5,4},{6,7},{7,6},{8,9},{9,8},{10,11... | collective-permute-start | bytes 2457608 | tf_op jit(solution)/shard_map/ppermute | solution.py:30
  284.8 3.5 %all-to-all-start.4 = ((f32[16,8,128]{2,1,0:T(8,128)}), f32[16,8,128]{2,1,0:T(8,128)S(1)}, u32[]{:S(2)}, u32[]{:S(2)}) async-start(f32[16,8,128]{2,1,0:T(8,128)} %broadcast_in_dim.25), calls=%async_computation.4 | async-start | bytes 131072 | tf_op jit(solution)/shard_map/all_to_all | solution.py:411
  288.3 5.0 %residual.1 = f32[75,8,1200]{2,1,0:T(8,128)} custom-call(s32[2]{0:T(128)} %pad_add_fusion.place_ref, bf16[8,40,1280]{2,1,0:T(8,128)(2,1)} %bitcast.66, bf16[8,40,1280]{2,1,0:T(8,128)(2,1)} %copy-done.3, f32[75,8,1200]{2,1,0:T(8,128)} %bitcast.67), custom_call_target="tpu_custom_call" | custom-call | tf_op jit(solution)/shard_map/residual/pallas_call | solution.py:331
  (121 shorter events, 45.3 us)
Async XLA Ops:
  4.3 31.8 %all-to-all-start = ((bf16[16,112,512]{2,1,0:T(8,128)(2,1)}), bf16[16,112,512]{2,1,0:T(8,128)(2,1)S(1)}, u32[]{:S(2)}, u32[]{:S(2)}) async-start(bf16[16,112,512]{2,1,0:T(8,128)(2,1)} %pad_maximum_fusion), calls=%async_computation | async-start | bytes 3670016 | tf_op jit(solution)/shard_map/all_to_all | solution.py:350
  11.9 13.8 %collective-permute-start.10 = (bf16[80,512]{1,0:T(8,128)(2,1)S(1)}, bf16[80,512]{1,0:T(8,128)(2,1)S(1)}, u32[]{:S(2)}, u32[]{:S(2)}) collective-permute-start(bf16[80,512]{1,0:T(8,128)(2,1)S(1)} %pad.17), channel_id=1, source_target_pairs={{0,12},{2,14},{4,0},{6,2},{8,4},{10,6},{12,8},{14,10},{1,13},{3,15... | collective-permute-start | bytes 245768 | tf_op jit(solution)/shard_map/ppermute | solution.py:351
  18.0 9.1 %collective-permute-start.11 = (bf16[80,512]{1,0:T(8,128)(2,1)S(1)}, bf16[80,512]{1,0:T(8,128)(2,1)S(1)}, u32[]{:S(2)}, u32[]{:S(2)}) collective-permute-start(bf16[80,512]{1,0:T(8,128)(2,1)S(1)} %pad.17), channel_id=1, source_target_pairs={{0,10},{2,12},{4,14},{6,0},{8,2},{10,4},{12,6},{14,8},{1,11},{3,13... | collective-permute-start | bytes 245768 | tf_op jit(solution)/shard_map/ppermute | solution.py:351
  18.7 8.4 %collective-permute-start.12 = (bf16[80,512]{1,0:T(8,128)(2,1)S(1)}, bf16[80,512]{1,0:T(8,128)(2,1)S(1)}, u32[]{:S(2)}, u32[]{:S(2)}) collective-permute-start(bf16[80,512]{1,0:T(8,128)(2,1)S(1)} %pad.17), channel_id=1, source_target_pairs={{0,8},{2,10},{4,12},{6,14},{8,0},{10,2},{12,4},{14,6},{1,9},{3,11}... | collective-permute-start | bytes 245768 | tf_op jit(solution)/shard_map/ppermute | solution.py:351
  22.9 10.3 %collective-permute-start.13 = (bf16[80,512]{1,0:T(8,128)(2,1)S(1)}, bf16[80,512]{1,0:T(8,128)(2,1)S(1)}, u32[]{:S(2)}, u32[]{:S(2)}) collective-permute-start(bf16[80,512]{1,0:T(8,128)(2,1)S(1)} %pad.17), channel_id=1, source_target_pairs={{0,6},{2,8},{4,10},{6,12},{8,14},{10,0},{12,2},{14,4},{1,7},{3,9},... | collective-permute-start | bytes 245768 | tf_op jit(solution)/shard_map/ppermute | solution.py:351
  22.9 11.5 %collective-permute-start.14 = (bf16[80,512]{1,0:T(8,128)(2,1)S(1)}, bf16[80,512]{1,0:T(8,128)(2,1)S(1)}, u32[]{:S(2)}, u32[]{:S(2)}) collective-permute-start(bf16[80,512]{1,0:T(8,128)(2,1)S(1)} %pad.17), channel_id=1, source_target_pairs={{0,4},{2,6},{4,8},{6,10},{8,12},{10,14},{12,0},{14,2},{1,5},{3,7},... | collective-permute-start | bytes 245768 | tf_op jit(solution)/shard_map/ppermute | solution.py:351
  39.7 82.4 %all-to-all-start.1 = ((bf16[16,5,80,512]{3,2,1,0:T(8,128)(2,1)}), bf16[16,5,80,512]{3,2,1,0:T(8,128)(2,1)}, u32[]{:S(2)}, u32[]{:S(2)}) async-start(bf16[16,5,80,512]{3,2,1,0:T(8,128)(2,1)} %broadcast_in_dim.22), calls=%async_computation.1 | async-start | bytes 13107200 | tf_op jit(solution)/shard_map/all_to_all | solution.py:352
  45.1 13.4 %collective-permute-start = (bf16[80,80]{1,0:T(8,128)(2,1)S(1)}, bf16[80,80]{1,0:T(8,128)(2,1)S(1)}, u32[]{:S(2)}, u32[]{:S(2)}) collective-permute-start(bf16[80,80]{1,0:T(8,128)(2,1)S(1)} %get-tuple-element.22), channel_id=1, source_target_pairs={{0,2},{2,4},{4,6},{6,8},{8,10},{10,12},{12,14},{14,0},{1,3},{3,5},... | collective-permute-start | bytes 38408 | tf_op jit(solution)/shard_map/ppermute | solution.py:380
  48.5 12.4 %collective-permute-start.1 = (bf16[80,80]{1,0:T(8,128)(2,1)S(1)}, bf16[80,80]{1,0:T(8,128)(2,1)S(1)}, u32[]{:S(2)}, u32[]{:S(2)}) collective-permute-start(bf16[80,80]{1,0:T(8,128)(2,1)S(1)} %get-tuple-element.21), channel_id=1, source_target_pairs={{0,4},{2,6},{4,8},{6,10},{8,12},{10,14},{12,0},{14,2},{1,5},{3,7},... | collective-permute-start | bytes 38408 | tf_op jit(solution)/shard_map/ppermute | solution.py:380
  50.8 10.1 %collective-permute-start.2 = (bf16[80,80]{1,0:T(8,128)(2,1)S(1)}, bf16[80,80]{1,0:T(8,128)(2,1)S(1)}, u32[]{:S(2)}, u32[]{:S(2)}) collective-permute-start(bf16[80,80]{1,0:T(8,128)(2,1)S(1)} %get-tuple-element.20), channel_id=1, source_target_pairs={{0,6},{2,8},{4,10},{6,12},{8,14},{10,0},{12,2},{14,4},{1,7},{3,9},... | collective-permute-start | bytes 38408 | tf_op jit(solution)/shard_map/ppermute | solution.py:380
  53.5 9.2 %collective-permute-start.3 = (bf16[80,80]{1,0:T(8,128)(2,1)S(1)}, bf16[80,80]{1,0:T(8,128)(2,1)S(1)}, u32[]{:S(2)}, u32[]{:S(2)}) collective-permute-start(bf16[80,80]{1,0:T(8,128)(2,1)S(1)} %get-tuple-element.19), channel_id=1, source_target_pairs={{0,8},{2,10},{4,12},{6,14},{8,0},{10,2},{12,4},{14,6},{1,9},{3,11}... | collective-permute-start | bytes 38408 | tf_op jit(solution)/shard_map/ppermute | solution.py:380
  54.0 18.1 %collective-permute-start.4 = (bf16[80,80]{1,0:T(8,128)(2,1)S(1)}, bf16[80,80]{1,0:T(8,128)(2,1)S(1)}, u32[]{:S(2)}, u32[]{:S(2)}) collective-permute-start(bf16[80,80]{1,0:T(8,128)(2,1)S(1)} %get-tuple-element.18), channel_id=1, source_target_pairs={{0,10},{2,12},{4,14},{6,0},{8,2},{10,4},{12,6},{14,8},{1,11},{3,13... | collective-permute-start | bytes 38408 | tf_op jit(solution)/shard_map/ppermute | solution.py:380
  58.5 13.7 %collective-permute-start.5 = (bf16[80,80]{1,0:T(8,128)(2,1)S(1)}, bf16[80,80]{1,0:T(8,128)(2,1)S(1)}, u32[]{:S(2)}, u32[]{:S(2)}) collective-permute-start(bf16[80,80]{1,0:T(8,128)(2,1)S(1)} %get-tuple-element.17), channel_id=1, source_target_pairs={{0,12},{2,14},{4,0},{6,2},{8,4},{10,6},{12,8},{14,10},{1,13},{3,15... | collective-permute-start | bytes 38408 | tf_op jit(solution)/shard_map/ppermute | solution.py:380
  61.0 47.0 %collective-permute-start.8 = (bf16[16,80,512]{2,1,0:T(8,128)(2,1)S(1)}, bf16[16,80,512]{2,1,0:T(8,128)(2,1)S(1)}, u32[]{:S(2)}, u32[]{:S(2)}) collective-permute-start(bf16[16,80,512]{2,1,0:T(8,128)(2,1)S(1)} %slice.68), channel_id=1, source_target_pairs={{0,14},{2,0},{4,2},{6,4},{8,6},{10,8},{12,10},{14,12},{1,15},{3,1}... | collective-permute-start | bytes 3932168 | tf_op jit(solution)/shard_map/ppermute | solution.py:360
  61.8 46.2 %collective-permute-start.9 = (bf16[16,80,512]{2,1,0:T(8,128)(2,1)S(1)}, bf16[16,80,512]{2,1,0:T(8,128)(2,1)}, u32[]{:S(2)}, u32[]{:S(2)}) collective-permute-start(bf16[16,80,512]{2,1,0:T(8,128)(2,1)S(1)} %slice.68), channel_id=1, source_target_pairs={{0,2},{2,4},{4,6},{6,8},{8,10},{10,12},{12,14},{14,0},{1,3},{3,5},... | collective-permute-start | bytes 3932168 | tf_op jit(solution)/shard_map/ppermute | solution.py:361
  62.7 7.3 %collective-permute-start.16 = (bf16[8,32,512]{2,1,0:T(8,128)(2,1)S(1)}, bf16[8,32,512]{2,1,0:T(8,128)(2,1)S(1)}, u32[]{:S(2)}, u32[]{:S(2)}) collective-permute-start(bf16[8,32,512]{2,1,0:T(8,128)(2,1)S(1)} %slice.70), channel_id=1, source_target_pairs={{0,1},{1,0},{2,3},{3,2},{4,5},{5,4},{6,7},{7,6},{8,9},{9,8},{10,11... | collective-permute-start | bytes 786440 | tf_op jit(solution)/shard_map/ppermute | solution.py:30
  70.1 35.2 %collective-permute-start.17 = (bf16[2,8,32,512]{3,2,1,0:T(8,128)(2,1)S(1)}, bf16[2,8,32,512]{3,2,1,0:T(8,128)(2,1)S(1)}, u32[]{:S(2)}, u32[]{:S(2)}) collective-permute-start(bf16[2,8,32,512]{3,2,1,0:T(8,128)(2,1)S(1)} %pad_maximum_fusion.1.rest_0_), channel_id=1, source_target_pairs={{0,14},{2,0},{4,2},{6,4},{8,6},{10,8},{12,10},{14,12},{1,15},{3,1}... | collective-permute-start | bytes 1572872 | tf_op jit(solution)/shard_map/ppermute | solution.py:370
  72.1 35.2 %collective-permute-start.20 = (bf16[2,8,32,512]{3,2,1,0:T(8,128)(2,1)S(1)}, bf16[2,8,32,512]{3,2,1,0:T(8,128)(2,1)S(1)}, u32[]{:S(2)}, u32[]{:S(2)}) collective-permute-start(bf16[2,8,32,512]{3,2,1,0:T(8,128)(2,1)S(1)} %pad_maximum_fusion.1.rest_0_), channel_id=1, source_target_pairs={{0,2},{2,4},{4,6},{6,8},{8,10},{10,12},{12,14},{14,0},{1,3},{3,5},... | collective-permute-start | bytes 1572872 | tf_op jit(solution)/shard_map/ppermute | solution.py:371
  72.2 28.3 %collective-permute-start.6 = (bf16[80,80]{1,0:T(8,128)(2,1)S(1)}, bf16[80,80]{1,0:T(8,128)(2,1)S(1)}, u32[]{:S(2)}, u32[]{:S(2)}) collective-permute-start(bf16[80,80]{1,0:T(8,128)(2,1)S(1)} %get-tuple-element.16), channel_id=1, source_target_pairs={{0,14},{2,0},{4,2},{6,4},{8,6},{10,8},{12,10},{14,12},{1,15},{3,1}... | collective-permute-start | bytes 38408 | tf_op jit(solution)/shard_map/ppermute | solution.py:380
  100.5 7.5 %collective-permute-start.7 = (bf16[8,80,80]{2,1,0:T(8,128)(2,1)S(1)}, bf16[8,80,80]{2,1,0:T(8,128)(2,1)S(1)}, u32[]{:S(2)}, u32[]{:S(2)}) collective-permute-start(bf16[8,80,80]{2,1,0:T(8,128)(2,1)S(1)} %constant_dynamic-update-slice_fusion.to_ref), channel_id=1, source_target_pairs={{0,1},{1,0},{2,3},{3,2},{4,5},{5,4},{6,7},{7,6},{8,9},{9,8},{10,11... | collective-permute-start | bytes 307208 | tf_op jit(solution)/shard_map/ppermute | solution.py:30
  105.4 35.9 %collective-permute-start.18 = (bf16[2,8,32,512]{3,2,1,0:T(8,128)(2,1)S(1)}, bf16[2,8,32,512]{3,2,1,0:T(8,128)(2,1)}, u32[]{:S(2)}, u32[]{:S(2)}) collective-permute-start(bf16[2,8,32,512]{3,2,1,0:T(8,128)(2,1)S(1)} %collective-permute-done.17.rest_1_), channel_id=1, source_target_pairs={{0,14},{2,0},{4,2},{6,4},{8,6},{10,8},{12,10},{14,12},{1,15},{3,1}... | collective-permute-start | bytes 1572872 | tf_op jit(solution)/shard_map/ppermute | solution.py:370
  107.3 39.6 %collective-permute-start.21 = (bf16[2,8,32,512]{3,2,1,0:T(8,128)(2,1)S(1)}, bf16[2,8,32,512]{3,2,1,0:T(8,128)(2,1)}, u32[]{:S(2)}, u32[]{:S(2)}) collective-permute-start(bf16[2,8,32,512]{3,2,1,0:T(8,128)(2,1)S(1)} %collective-permute-done.20.rest_4_), channel_id=1, source_target_pairs={{0,2},{2,4},{4,6},{6,8},{8,10},{10,12},{12,14},{14,0},{1,3},{3,5},... | collective-permute-start | bytes 1572872 | tf_op jit(solution)/shard_map/ppermute | solution.py:371
  132.2 35.7 %all-to-all-start.2 = ((bf16[16,80,256]{2,1,0:T(8,128)(2,1)}), bf16[16,80,256]{2,1,0:T(8,128)(2,1)S(1)}, u32[]{:S(2)}, u32[]{:S(2)}) async-start(bf16[16,80,256]{2,1,0:T(8,128)(2,1)} %half.1), calls=%async_computation.2 | async-start | bytes 1310720 | tf_op jit(solution)/shard_map/all_to_all | solution.py:385
  141.2 35.8 %collective-permute-start.19 = (bf16[2,8,32,512]{3,2,1,0:T(8,128)(2,1)}, bf16[2,8,32,512]{3,2,1,0:T(8,128)(2,1)S(1)}, u32[]{:S(2)}, u32[]{:S(2)}) collective-permute-start(bf16[2,8,32,512]{3,2,1,0:T(8,128)(2,1)} %collective-permute-done.18.rest_2_), channel_id=1, source_target_pairs={{0,14},{2,0},{4,2},{6,4},{8,6},{10,8},{12,10},{14,12},{1,15},{3,1}... | collective-permute-start | bytes 1572872 | tf_op jit(solution)/shard_map/ppermute | solution.py:370
  146.9 30.2 %collective-permute-start.22 = (bf16[2,8,32,512]{3,2,1,0:T(8,128)(2,1)}, bf16[2,8,32,512]{3,2,1,0:T(8,128)(2,1)S(1)}, u32[]{:S(2)}, u32[]{:S(2)}) collective-permute-start(bf16[2,8,32,512]{3,2,1,0:T(8,128)(2,1)} %collective-permute-done.21.rest_5_), channel_id=1, source_target_pairs={{0,2},{2,4},{4,6},{6,8},{8,10},{10,12},{12,14},{14,0},{1,3},{3,5},... | collective-permute-start | bytes 1572872 | tf_op jit(solution)/shard_map/ppermute | solution.py:371
  167.9 19.9 %collective-permute-start.15 = (bf16[1280,256]{1,0:T(8,128)(2,1)S(1)}, bf16[1280,256]{1,0:T(8,128)(2,1)S(1)}, u32[]{:S(2)}, u32[]{:S(2)}) collective-permute-start(bf16[1280,256]{1,0:T(8,128)(2,1)S(1)} %bitcast.71), channel_id=1, source_target_pairs={{0,1},{1,0},{2,3},{3,2},{4,5},{5,4},{6,7},{7,6},{8,9},{9,8},{10,11... | collective-permute-start | bytes 1966088 | tf_op jit(solution)/shard_map/ppermute | solution.py:30
  177.0 10.8 %collective-permute-start.23 = (bf16[1,8,32,512]{3,2,1,0:T(8,128)(2,1)S(1)}, bf16[1,8,32,512]{3,2,1,0:T(8,128)(2,1)S(1)}, u32[]{:S(2)}, u32[]{:S(2)}) collective-permute-start(bf16[1,8,32,512]{3,2,1,0:T(8,128)(2,1)S(1)} %slice.71), channel_id=1, source_target_pairs={{0,14},{2,0},{4,2},{6,4},{8,6},{10,8},{12,10},{14,12},{1,15},{3,1}... | collective-permute-start | bytes 786440 | tf_op jit(solution)/shard_map/ppermute | solution.py:372
  177.2 10.6 %collective-permute-start.24 = (bf16[1,8,32,512]{3,2,1,0:T(8,128)(2,1)S(1)}, bf16[1,8,32,512]{3,2,1,0:T(8,128)(2,1)S(1)}, u32[]{:S(2)}, u32[]{:S(2)}) collective-permute-start(bf16[1,8,32,512]{3,2,1,0:T(8,128)(2,1)S(1)} %slice.72), channel_id=1, source_target_pairs={{0,2},{2,4},{4,6},{6,8},{8,10},{10,12},{12,14},{14,0},{1,3},{3,5},... | collective-permute-start | bytes 786440 | tf_op jit(solution)/shard_map/ppermute | solution.py:373
  217.0 18.6 %all-to-all-start.3 = ((bf16[16,80,256]{2,1,0:T(8,128)(2,1)}), bf16[16,80,256]{2,1,0:T(8,128)(2,1)S(1)}, u32[]{:S(2)}, u32[]{:S(2)}) async-start(bf16[16,80,256]{2,1,0:T(8,128)(2,1)} %bitcast.30), calls=%async_computation.3 | async-start | bytes 1310720 | tf_op jit(solution)/shard_map/all_to_all | solution.py:391
  247.5 3.7 %collective-permute-start.26 = (f32[40,1280]{1,0:T(8,128)}, f32[40,1280]{1,0:T(8,128)S(1)}, u32[]{:S(2)}, u32[]{:S(2)}) collective-permute-start(f32[40,1280]{1,0:T(8,128)} %get-tuple-element.13), channel_id=1, source_target_pairs={{0,1},{1,0},{2,3},{3,2},{4,5},{5,4},{6,7},{7,6},{8,9},{9,8},{10,11... | collective-permute-start | bytes 614408 | tf_op jit(solution)/shard_map/ppermute | solution.py:30
  274.6 8.1 %collective-permute-start.27 = (bf16[8,40,1280]{2,1,0:T(8,128)(2,1)S(1)}, bf16[8,40,1280]{2,1,0:T(8,128)(2,1)S(1)}, u32[]{:S(2)}, u32[]{:S(2)}) collective-permute-start(bf16[8,40,1280]{2,1,0:T(8,128)(2,1)S(1)} %bitcast.64), channel_id=1, source_target_pairs={{0,1},{1,0},{2,3},{3,2},{4,5},{5,4},{6,7},{7,6},{8,9},{9,8},{10,11... | collective-permute-start | bytes 2457608 | tf_op jit(solution)/shard_map/ppermute | solution.py:30
  284.8 10.0 %all-to-all-start.4 = ((f32[16,8,128]{2,1,0:T(8,128)}), f32[16,8,128]{2,1,0:T(8,128)S(1)}, u32[]{:S(2)}, u32[]{:S(2)}) async-start(f32[16,8,128]{2,1,0:T(8,128)} %broadcast_in_dim.25), calls=%async_computation.4 | async-start | bytes 131072 | tf_op jit(solution)/shard_map/all_to_all | solution.py:411
  (21 other events, 282.7 us)
